TPU v7x, 128 devices: a whole 4x4x4 slice. The times are simulated.
128 devices in a mesh: gx: 4 (over z_lo, core), gy: 16 (over x, y), gz: 2 (over z_hi).
Axes of the slice: x: 4, y: 4, z: 4 (z_hi: 2, z_lo: 2; z = z_hi * 2 + z_lo), core: 2. Of those that a mesh axis runs over, the one named last changes fastest.
Arguments:
- eigvecs: bfloat16 [64, 128, 96, 512], P('gx', 'gy', 'gz'), may hold values from -7 to 7, as said below
- material: float32 [2, 64, 128, 96], P(None, 'gx', 'gy', 'gz'), may hold values from 0.5 to 2
Outputs:
- stiffness: float32 [512, 512], P(('gx', 'gy', 'gz'))
- mass_matrix: float32 [512, 512], P(('gx', 'gy', 'gz'))
Inputs may be any that keep to these rules, and one draw needn't show every extreme that they name: `eigvecs`: entries are a rough part plus a part that varies slowly over the grid.
All inputs are finite; a program needn't handle non-finite values.
Results may differ from a plain program's by a relative error of at most 0.0003.
Values may be sent and summed in bfloat16 or wider, within the bound.
No kernel may reach another device: no remote copies, remote signals or barrier semaphores. Data moves between devices by JAX's collectives and lax.ppermute only.
A program may use at most 128 MiB of HBM per device.

v0:
```python
import jax
import jax.numpy as jnp
from jax import lax
from jax.sharding import PartitionSpec as P

corner_weight = 0.0625
coupling_total = 3.5
mass_side = 1.0 / 6.0
mass_middle = 4.0 / 6.0


def with_halo(cells, sides, width):
    for axis, dim in sides:
        count = lax.axis_size(axis)
        ends = count - 1
        head = lax.slice_in_dim(cells, 0, width, axis=dim)
        tail = lax.slice_in_dim(cells, cells.shape[dim] - width, cells.shape[dim], axis=dim)
        cells = jnp.concatenate(
            [
                lax.ppermute(tail, axis, [(i, (i + 1) % count) for i in range(ends)]),
                cells,
                lax.ppermute(head, axis, [((i + 1) % count, i) for i in range(ends)]),
            ],
            axis=dim,
        )
    return cells


def split_up(x, dim, devices):
    dims = x.shape
    parts = x.reshape(*dims[:dim], devices, dims[dim] // devices, *dims[dim + 1 :])
    return jnp.moveaxis(parts, dim, 0)


def sum_at_owner(x, axis, dim):
    devices = lax.axis_size(axis)
    parts = lax.all_to_all(split_up(x, dim, devices), axis, 0, 0, tiled=True)
    return jnp.sum(parts, axis=0)


def three_taps(field, side, middle):
    for axis_dim in (0, 1, 2):
        inner = field.shape[axis_dim] - 2
        lower = lax.slice_in_dim(field, 0, inner, axis=axis_dim)
        centre = lax.slice_in_dim(field, 1, inner + 1, axis=axis_dim)
        upper = lax.slice_in_dim(field, 2, inner + 2, axis=axis_dim)
        field = side * (lower + upper) + middle * centre
    return field


def apply_operators(padded, padded_material):
    values = padded.astype(jnp.float32)
    kappa = padded_material[0]
    rho = padded_material[1]
    centre = values[1:-1, 1:-1, 1:-1]
    kappa_centre = kappa[1:-1, 1:-1, 1:-1]
    rho_centre = rho[1:-1, 1:-1, 1:-1]
    kappa_values = kappa[..., None] * values
    rho_values = rho[..., None] * values
    self_weight = 8.0 * corner_weight
    near_values = corner_weight * three_taps(values, 1.0, 2.0) - self_weight * centre
    near_kappa_values = (
        corner_weight * three_taps(kappa_values, 1.0, 2.0)
        - self_weight * kappa_values[1:-1, 1:-1, 1:-1]
    )
    near_kappa = corner_weight * three_taps(kappa, 1.0, 2.0) - self_weight * kappa_centre
    row_weight = 0.5 * (coupling_total * kappa_centre + near_kappa)
    stiff_sum = (
        row_weight[..., None] * centre
        - 0.5 * kappa_centre[..., None] * near_values
        - 0.5 * near_kappa_values
    )
    mass_sum = 0.5 * rho_centre[..., None] * three_taps(
        values, mass_side, mass_middle
    ) + 0.5 * three_taps(rho_values, mass_side, mass_middle)
    return (stiff_sum.astype(jnp.bfloat16), mass_sum.astype(jnp.bfloat16))


def per_device(eigvecs, material):
    size_x, size_y, size_z, columns = eigvecs.shape
    cells = size_x * size_y * size_z
    block_cols = 128
    padded_material = with_halo(material, (("gx", 1), ("gy", 2), ("gz", 3)), 1)
    padded = with_halo(eigvecs, (("gx", 0), ("gy", 1), ("gz", 2)), 1)

    def column_block(block_index):
        col_block = lax.dynamic_slice_in_dim(padded, block_index * block_cols, block_cols, 3)
        stiff_vecs, mass_vecs = apply_operators(col_block, padded_material)
        return (stiff_vecs.reshape(cells, block_cols), mass_vecs.reshape(cells, block_cols))

    stiff_blocks, mass_blocks = lax.map(
        column_block, jnp.arange(columns // block_cols, dtype=jnp.int32)
    )
    flat_vectors = eigvecs.reshape(cells, columns)
    devices_all = lax.axis_size("gx") * lax.axis_size("gy") * lax.axis_size("gz")
    total_cells = cells * devices_all
    row_count = columns // lax.axis_size("gx") * lax.axis_size("gx")
    stiff_part = jnp.einsum(
        "cp,bcq->pbq", flat_vectors, stiff_blocks, preferred_element_type=jnp.float32
    ).reshape(row_count, columns)
    mass_part = jnp.einsum(
        "cp,bcq->pbq", flat_vectors, mass_blocks, preferred_element_type=jnp.float32
    ).reshape(row_count, columns)
    section_one = sum_at_owner(jnp.concatenate([stiff_part, mass_part], axis=1), "gx", 0)
    section_two = sum_at_owner(section_one, "gy", 0)
    summed = sum_at_owner(section_two, "gz", 0)
    stiffness = summed[:, :columns] / total_cells
    mass_matrix = summed[:, columns:] / total_cells
    return (stiffness, mass_matrix)


def solution(mesh):
    return jax.shard_map(
        per_device,
        mesh=mesh,
        in_specs=(P("gx", "gy", "gz", None), P(None, "gx", "gy", "gz")),
        out_specs=(P(("gx", "gy", "gz"), None), P(("gx", "gy", "gz"), None)),
        check_vma=False,
    )
```

profile of v0, /device:TPU:0, one launch (start us, length us, event | category | flops | bytes accessed | tf_op | source)
XLA Modules:
  0.0 277.3 jit_solution(3379979988916823563)
XLA Ops:
  3.8 4.6 %collective-permute-start = (f32[2,1,8,48]{3,2,1,0:T(8,128)S(1)}, f32[2,1,8,48]{3,2,1,0:T(8,128)S(1)}, u32[]{:S(2)}, u32[]{:S(2)}) collective-permute-start(f32[2,1,8,48]{3,2,1,0:T(8,128)S(1)} %get-tuple-element.101), channel_id=1, source_target_pairs={{0,32},{32,64},{64,96},{1,33},{33,65},{65,97},{2,34},{34,66},{66,9... | collective-permute-start | bytes 9224 | tf_op jit(solution)/shard_map/ppermute | solution.py:20
  11.2 3.9 %constant_dynamic-update-slice_fusion.6 = bf16[18,8,48,512]{3,2,1,0:T(8,128)(2,1)S(1)} fusion(bf16[18,8,48,512]{3,2,1,0:T(8,128)(2,1)S(1)} %constant_dynamic-update-slice_fusion.7, bf16[16,8,48,512]{3,2,1,0:T(8,128)(2,1)} %param.4), kind=kLoop, calls=%fused_computation.87 | loop fusion | bytes 12582912
  15.1 2.9 %copy-done.1 = bf16[18,8,48,512]{3,2,1,0:T(8,128)(2,1)} copy-done((bf16[18,8,48,512]{3,2,1,0:T(8,128)(2,1)}, bf16[18,8,48,512]{3,2,1,0:T(8,128)(2,1)S(1)}, u32[]{:S(2)}) %copy-start.1) | copy-done | bytes 7077912
  20.7 5.5 %collective-permute-start.8 = (bf16[18,1,48,512]{3,2,1,0:T(8,128)(2,1)}, bf16[18,1,48,512]{3,2,1,0:T(8,128)(2,1)}, u32[]{:S(2)}, u32[]{:S(2)}) collective-permute-start(bf16[18,1,48,512]{3,2,1,0:T(8,128)(2,1)} %get-tuple-element.92), channel_id=1, source_target_pairs={{0,2},{2,4},{4,6},{6,8},{8,10},{10,12},{12,14},{14,16},{16,18},{18... | collective-permute-start | bytes 2654216 | tf_op jit(solution)/shard_map/ppermute | solution.py:20
  27.8 4.5 %collective-permute-start.2 = (f32[2,18,1,48]{3,2,1,0:T(1,128)S(1)}, f32[2,18,1,48]{3,2,1,0:T(1,128)S(1)}, u32[]{:S(2)}, u32[]{:S(2)}) collective-permute-start(f32[2,18,1,48]{3,2,1,0:T(1,128)S(1)} %get-tuple-element.98), channel_id=1, source_target_pairs={{0,2},{2,4},{4,6},{6,8},{8,10},{10,12},{12,14},{14,16},{16,18},{18... | collective-permute-start | bytes 20744 | tf_op jit(solution)/shard_map/ppermute | solution.py:20
  32.3 8.1 %collective-permute-done.3 = f32[2,18,1,48]{3,2,1,0:T(1,128)S(1)} collective-permute-done((f32[2,18,1,48]{3,2,1,0:T(1,128)S(1)}, f32[2,18,1,48]{3,2,1,0:T(1,128)S(1)}, u32[]{:S(2)}, u32[]{:S(2)}) %collective-permute-start.3) | collective-permute-done | bytes 6944 | tf_op jit(solution)/shard_map/ppermute | solution.py:22
  40.4 1.7 collective-permute-done.2
  44.5 6.8 %collective-permute-start.4 = (f32[2,18,10,1]{3,2,1,0:T(8,128)}, f32[2,18,10,1]{3,2,1,0:T(8,128)}, u32[]{:S(2)}, u32[]{:S(2)}) collective-permute-start(f32[2,18,10,1]{3,2,1,0:T(8,128)} %get-tuple-element.96), channel_id=1, source_target_pairs={{0,1},{2,3},{4,5},{6,7},{8,9},{10,11},{12,13},{14,15},{16,17},{18,... | collective-permute-start | bytes 4328 | tf_op jit(solution)/shard_map/ppermute | solution.py:20
  51.2 2.5 collective-permute-done.5
  57.0 2.6 pad_maximum_fusion.4
  60.9 6.3 %collective-permute-start.10 = (bf16[18,10,1,512]{3,2,1,0:T(2,128)(2,1)S(1)}, bf16[18,10,1,512]{3,2,1,0:T(2,128)(2,1)S(1)}, u32[]{:S(2)}, u32[]{:S(2)}) collective-permute-start(bf16[18,10,1,512]{3,2,1,0:T(2,128)(2,1)S(1)} %get-tuple-element.90), channel_id=1, source_target_pairs={{0,1},{2,3},{4,5},{6,7},{8,9},{10,11},{12,13},{14,15},{16,17},{18,... | collective-permute-start | bytes 552968 | tf_op jit(solution)/shard_map/ppermute | solution.py:20
  67.2 5.5 %collective-permute-done.11 = bf16[18,10,1,512]{3,2,1,0:T(2,128)(2,1)S(1)} collective-permute-done((bf16[18,10,1,512]{3,2,1,0:T(2,128)(2,1)S(1)}, bf16[18,10,1,512]{3,2,1,0:T(2,128)(2,1)S(1)}, u32[]{:S(2)}, u32[]{:S(2)}) %collective-permute-start.11) | collective-permute-done | bytes 184352 | tf_op jit(solution)/shard_map/ppermute | solution.py:22
  72.7 1.8 collective-permute-done.10
  74.5 9.4 %pad_maximum_fusion = bf16[18,10,50,512]{3,2,1,0:T(8,128)(2,1)} fusion(bf16[18,10,1,512]{3,2,1,0:T(2,128)(2,1)S(1)} %collective-permute-done.11, bf16[18,1,48,512]{3,2,1,0:T(8,128)(2,1)} %collective-permute-done.9, bf16[18,8,48,512]{3,2,1,0:T(8,128)(2,1)S(1)} %bitcast.42, bf16[18,1,48,512]{3,2,1,0:T(8,128)(2,1)} %collective-permute-done.8, ...), kind=kLoop, calls=%fused_computation.72 | loop fusion | flops 46080000 | bytes 18432000 | tf_op jit(solution)/shard_map/concatenate | solution.py:18
  83.9 114.4 %while.13 = (s32[]{:T(128)}, bf16[4,6144,128]{2,1,0:T(8,128)(2,1)}, bf16[4,6144,128]{2,1,0:T(8,128)(2,1)}, f32[2,18,10,50]{3,2,1,0:T(8,128)S(1)}, f32[16,10,50]{...) while((s32[]{:T(128)}, bf16[4,6144,128]{2,1,0:T(8,128)(2,1)}, ...), condition=%wide.region_1.2_spmd, body=%wide.region_0.1_spmd.sunk | while | flops 53078404 | bytes 184562576 | solution.py:91
  85.2 5.8 %broadcast_multiply_fusion.3 = (f32[18,10,50,128]{3,2,1,0:T(8,128)S(1)}, f32[18,10,50,128]{3,2,1,0:T(8,128)S(1)}) fusion(f32[18,10,50]{2,1,0:T(8,128)S(1)} %get-tuple-element.157, bf16[18,10,50,512]{3,2,1,0:T(8,128)(2,1)} %get-tuple-element.195, s32[]{:T(128)S(6)} %select_n.5, f32[18,10,50]{2,1,0:T(8,128)S(1)} %get-tuple-element.158), kind=kLoop, calls=%fused_computation.52.clone.1 | loop fusion | flops 3456000 | bytes 11592004 | tf_op jit(solution)/shard_map/while/body/eval_jaxpr/mul | solution.py:59
  92.1 2.1 dynamic-slice_convert_fusion.2
  94.2 2.9 %multiply_add_fusion.3 = (f32[16,10,50,128]{3,2,1,0:T(8,128)S(1)}, f32[16,10,50,128]{3,2,1,0:T(8,128)}) fusion(f32[18,10,50,128]{3,2,1,0:T(8,128)S(1)} %dynamic-slice_convert_fusion.2), kind=kLoop, calls=%fused_computation.8.clone.1 | loop fusion | flops 6144000 | bytes 20480000 | tf_op jit(solution)/shard_map/while/body/eval_jaxpr/add | solution.py:47
  97.6 3.1 %fusion.57 = bf16[16,8,48,128]{3,2,1,0:T(8,128)(2,1)} fusion(f32[16,8,50,128]{3,2,1,0:T(8,128)S(1)} %fusion.55, f32[16,8,50,128]{3,2,1,0:T(8,128)S(1)} %fusion.56, f32[16,8,48]{2,1,0:T(8,128)S(1)} %slice_multiply_fusion.18), kind=kLoop, calls=%fused_computation.28.clone.1 | loop fusion | flops 9437184 | bytes 20471808 | tf_op jit(solution)/shard_map/while/body/eval_jaxpr/convert_element_type | solution.py:76
  101.7 5.2 %fusion.60 = f32[16,8,50,128]{3,2,1,0:T(8,128)S(1)} fusion(f32[16,10,50,128]{3,2,1,0:T(8,128)} %get-tuple-element.162), kind=kLoop, calls=%fused_computation.22.clone.1 | loop fusion | flops 2457600 | bytes 13107200 | tf_op jit(solution)/shard_map/while/body/eval_jaxpr/add | solution.py:47
  107.1 3.6 %fusion.63 = bf16[16,8,48,128]{3,2,1,0:T(8,128)(2,1)S(1)} fusion(f32[18,10,50,128]{3,2,1,0:T(8,128)S(1)} %get-tuple-element.161, f32[16,8,50,128]{3,2,1,0:T(8,128)S(1)} %fusion.59, f32[16,8,50,128]{3,2,1,0:T(8,128)S(1)} %fusion.60, f32[18,10,50,128]{3,2,1,0:T(8,128)S(1)} %dynamic-slice_convert_fusion.2, f32[16,8,48]{2,1,0:T(8,128)S(1)} %get-tuple-element.163, ...), kind=kLoop, calls=%fused_computation.40.clone.1 | loop fusion | flops 14155776 | bytes 26787840 | tf_op jit(solution)/shard_map/while/body/eval_jaxpr/convert_element_type | solution.py:76
  110.6 1.9 constant_dynamic-update-slice_fusion.9
  113.8 5.8 %broadcast_multiply_fusion.3 = (f32[18,10,50,128]{3,2,1,0:T(8,128)S(1)}, f32[18,10,50,128]{3,2,1,0:T(8,128)S(1)}) fusion(f32[18,10,50]{2,1,0:T(8,128)S(1)} %get-tuple-element.157, bf16[18,10,50,512]{3,2,1,0:T(8,128)(2,1)} %get-tuple-element.195, s32[]{:T(128)S(6)} %select_n.5, f32[18,10,50]{2,1,0:T(8,128)S(1)} %get-tuple-element.158), kind=kLoop, calls=%fused_computation.52.clone.1 | loop fusion | flops 3456000 | bytes 11592004 | tf_op jit(solution)/shard_map/while/body/eval_jaxpr/mul | solution.py:59
  120.7 2.1 dynamic-slice_convert_fusion.2
  122.8 2.9 %multiply_add_fusion.3 = (f32[16,10,50,128]{3,2,1,0:T(8,128)S(1)}, f32[16,10,50,128]{3,2,1,0:T(8,128)}) fusion(f32[18,10,50,128]{3,2,1,0:T(8,128)S(1)} %dynamic-slice_convert_fusion.2), kind=kLoop, calls=%fused_computation.8.clone.1 | loop fusion | flops 6144000 | bytes 20480000 | tf_op jit(solution)/shard_map/while/body/eval_jaxpr/add | solution.py:47
  126.3 3.1 %fusion.57 = bf16[16,8,48,128]{3,2,1,0:T(8,128)(2,1)} fusion(f32[16,8,50,128]{3,2,1,0:T(8,128)S(1)} %fusion.55, f32[16,8,50,128]{3,2,1,0:T(8,128)S(1)} %fusion.56, f32[16,8,48]{2,1,0:T(8,128)S(1)} %slice_multiply_fusion.18), kind=kLoop, calls=%fused_computation.28.clone.1 | loop fusion | flops 9437184 | bytes 20471808 | tf_op jit(solution)/shard_map/while/body/eval_jaxpr/convert_element_type | solution.py:76
  130.3 5.2 %fusion.60 = f32[16,8,50,128]{3,2,1,0:T(8,128)S(1)} fusion(f32[16,10,50,128]{3,2,1,0:T(8,128)} %get-tuple-element.162), kind=kLoop, calls=%fused_computation.22.clone.1 | loop fusion | flops 2457600 | bytes 13107200 | tf_op jit(solution)/shard_map/while/body/eval_jaxpr/add | solution.py:47
  135.7 3.6 %fusion.63 = bf16[16,8,48,128]{3,2,1,0:T(8,128)(2,1)S(1)} fusion(f32[18,10,50,128]{3,2,1,0:T(8,128)S(1)} %get-tuple-element.161, f32[16,8,50,128]{3,2,1,0:T(8,128)S(1)} %fusion.59, f32[16,8,50,128]{3,2,1,0:T(8,128)S(1)} %fusion.60, f32[18,10,50,128]{3,2,1,0:T(8,128)S(1)} %dynamic-slice_convert_fusion.2, f32[16,8,48]{2,1,0:T(8,128)S(1)} %get-tuple-element.163, ...), kind=kLoop, calls=%fused_computation.40.clone.1 | loop fusion | flops 14155776 | bytes 26787840 | tf_op jit(solution)/shard_map/while/body/eval_jaxpr/convert_element_type | solution.py:76
  139.3 1.9 constant_dynamic-update-slice_fusion.9
  142.5 5.8 %broadcast_multiply_fusion.3 = (f32[18,10,50,128]{3,2,1,0:T(8,128)S(1)}, f32[18,10,50,128]{3,2,1,0:T(8,128)S(1)}) fusion(f32[18,10,50]{2,1,0:T(8,128)S(1)} %get-tuple-element.157, bf16[18,10,50,512]{3,2,1,0:T(8,128)(2,1)} %get-tuple-element.195, s32[]{:T(128)S(6)} %select_n.5, f32[18,10,50]{2,1,0:T(8,128)S(1)} %get-tuple-element.158), kind=kLoop, calls=%fused_computation.52.clone.1 | loop fusion | flops 3456000 | bytes 11592004 | tf_op jit(solution)/shard_map/while/body/eval_jaxpr/mul | solution.py:59
  149.4 2.1 dynamic-slice_convert_fusion.2
  151.5 2.9 %multiply_add_fusion.3 = (f32[16,10,50,128]{3,2,1,0:T(8,128)S(1)}, f32[16,10,50,128]{3,2,1,0:T(8,128)}) fusion(f32[18,10,50,128]{3,2,1,0:T(8,128)S(1)} %dynamic-slice_convert_fusion.2), kind=kLoop, calls=%fused_computation.8.clone.1 | loop fusion | flops 6144000 | bytes 20480000 | tf_op jit(solution)/shard_map/while/body/eval_jaxpr/add | solution.py:47
  154.9 3.1 %fusion.57 = bf16[16,8,48,128]{3,2,1,0:T(8,128)(2,1)} fusion(f32[16,8,50,128]{3,2,1,0:T(8,128)S(1)} %fusion.55, f32[16,8,50,128]{3,2,1,0:T(8,128)S(1)} %fusion.56, f32[16,8,48]{2,1,0:T(8,128)S(1)} %slice_multiply_fusion.18), kind=kLoop, calls=%fused_computation.28.clone.1 | loop fusion | flops 9437184 | bytes 20471808 | tf_op jit(solution)/shard_map/while/body/eval_jaxpr/convert_element_type | solution.py:76
  158.9 5.2 %fusion.60 = f32[16,8,50,128]{3,2,1,0:T(8,128)S(1)} fusion(f32[16,10,50,128]{3,2,1,0:T(8,128)} %get-tuple-element.162), kind=kLoop, calls=%fused_computation.22.clone.1 | loop fusion | flops 2457600 | bytes 13107200 | tf_op jit(solution)/shard_map/while/body/eval_jaxpr/add | solution.py:47
  164.3 3.6 %fusion.63 = bf16[16,8,48,128]{3,2,1,0:T(8,128)(2,1)S(1)} fusion(f32[18,10,50,128]{3,2,1,0:T(8,128)S(1)} %get-tuple-element.161, f32[16,8,50,128]{3,2,1,0:T(8,128)S(1)} %fusion.59, f32[16,8,50,128]{3,2,1,0:T(8,128)S(1)} %fusion.60, f32[18,10,50,128]{3,2,1,0:T(8,128)S(1)} %dynamic-slice_convert_fusion.2, f32[16,8,48]{2,1,0:T(8,128)S(1)} %get-tuple-element.163, ...), kind=kLoop, calls=%fused_computation.40.clone.1 | loop fusion | flops 14155776 | bytes 26787840 | tf_op jit(solution)/shard_map/while/body/eval_jaxpr/convert_element_type | solution.py:76
  167.9 1.9 constant_dynamic-update-slice_fusion.9
  171.1 5.8 %broadcast_multiply_fusion.3 = (f32[18,10,50,128]{3,2,1,0:T(8,128)S(1)}, f32[18,10,50,128]{3,2,1,0:T(8,128)S(1)}) fusion(f32[18,10,50]{2,1,0:T(8,128)S(1)} %get-tuple-element.157, bf16[18,10,50,512]{3,2,1,0:T(8,128)(2,1)} %get-tuple-element.195, s32[]{:T(128)S(6)} %select_n.5, f32[18,10,50]{2,1,0:T(8,128)S(1)} %get-tuple-element.158), kind=kLoop, calls=%fused_computation.52.clone.1 | loop fusion | flops 3456000 | bytes 11592004 | tf_op jit(solution)/shard_map/while/body/eval_jaxpr/mul | solution.py:59
  178.0 2.1 dynamic-slice_convert_fusion.2
  180.0 2.9 %multiply_add_fusion.3 = (f32[16,10,50,128]{3,2,1,0:T(8,128)S(1)}, f32[16,10,50,128]{3,2,1,0:T(8,128)}) fusion(f32[18,10,50,128]{3,2,1,0:T(8,128)S(1)} %dynamic-slice_convert_fusion.2), kind=kLoop, calls=%fused_computation.8.clone.1 | loop fusion | flops 6144000 | bytes 20480000 | tf_op jit(solution)/shard_map/while/body/eval_jaxpr/add | solution.py:47
  183.5 3.1 %fusion.57 = bf16[16,8,48,128]{3,2,1,0:T(8,128)(2,1)} fusion(f32[16,8,50,128]{3,2,1,0:T(8,128)S(1)} %fusion.55, f32[16,8,50,128]{3,2,1,0:T(8,128)S(1)} %fusion.56, f32[16,8,48]{2,1,0:T(8,128)S(1)} %slice_multiply_fusion.18), kind=kLoop, calls=%fused_computation.28.clone.1 | loop fusion | flops 9437184 | bytes 20471808 | tf_op jit(solution)/shard_map/while/body/eval_jaxpr/convert_element_type | solution.py:76
  187.5 5.2 %fusion.60 = f32[16,8,50,128]{3,2,1,0:T(8,128)S(1)} fusion(f32[16,10,50,128]{3,2,1,0:T(8,128)} %get-tuple-element.162), kind=kLoop, calls=%fused_computation.22.clone.1 | loop fusion | flops 2457600 | bytes 13107200 | tf_op jit(solution)/shard_map/while/body/eval_jaxpr/add | solution.py:47
  192.9 3.6 %fusion.63 = bf16[16,8,48,128]{3,2,1,0:T(8,128)(2,1)S(1)} fusion(f32[18,10,50,128]{3,2,1,0:T(8,128)S(1)} %get-tuple-element.161, f32[16,8,50,128]{3,2,1,0:T(8,128)S(1)} %fusion.59, f32[16,8,50,128]{3,2,1,0:T(8,128)S(1)} %fusion.60, f32[18,10,50,128]{3,2,1,0:T(8,128)S(1)} %dynamic-slice_convert_fusion.2, f32[16,8,48]{2,1,0:T(8,128)S(1)} %get-tuple-element.163, ...), kind=kLoop, calls=%fused_computation.40.clone.1 | loop fusion | flops 14155776 | bytes 26787840 | tf_op jit(solution)/shard_map/while/body/eval_jaxpr/convert_element_type | solution.py:76
  196.5 1.9 constant_dynamic-update-slice_fusion.9
  198.4 7.5 %convolution_bitcast_fusion = f32[512,4,128]{0,2,1:T(8,128)S(1)} fusion(bf16[4,6144,128]{2,1,0:T(8,128)(2,1)} %get-tuple-element.65, bf16[6144,512,1]{1,0,2:T(8,128)(2,1)} %bitcast.39), kind=kOutput, calls=%fused_computation.74 | convolution fusion | flops 3221225472 | bytes 13631488 | tf_op jit(solution)/shard_map/cp,bcq->pbq/dot_general | solution.py:101
  206.3 7.7 %convolution_bitcast_fusion.1 = f32[512,4,128]{0,2,1:T(8,128)S(1)} fusion(bf16[4,6144,128]{2,1,0:T(8,128)(2,1)} %get-tuple-element.64, bf16[6144,512,1]{1,0,2:T(8,128)(2,1)} %bitcast.40), kind=kOutput, calls=%fused_computation.75 | convolution fusion | flops 3221225472 | bytes 13631488 | tf_op jit(solution)/shard_map/cp,bcq->pbq/dot_general | solution.py:98
  214.7 29.5 %all_to_all.15 = f32[4,128,1024]{1,2,0:T(8,128)S(1)} all-to-all(f32[4,128,1024]{1,2,0:T(8,128)S(1)} %pad_maximum_fusion.1), channel_id=1, replica_groups=mesh['gx'=4,'gy'=16,'gz'=2] {'gx'}, dimensions={0} | all-to-all | bytes 4194304 | tf_op jit(solution)/shard_map/all_to_all | solution.py:37
  244.6 20.9 %all_to_all.16 = f32[16,8,1024]{2,1,0:T(8,128)S(1)} all-to-all(f32[16,8,1024]{2,1,0:T(8,128)S(1)} %bitcast.43), channel_id=1, replica_groups=mesh['gx'=4,'gy'=16,'gz'=2] {'gy'}, dimensions={0} | all-to-all | bytes 1048576 | tf_op jit(solution)/shard_map/all_to_all | solution.py:37
  265.5 11.1 %all_to_all.17 = f32[2,4,1024]{2,1,0:T(4,128)S(1)} all-to-all(f32[2,4,1024]{2,1,0:T(4,128)S(1)} %reshape.46), channel_id=1, replica_groups=mesh['gx'=4,'gy'=16,'gz'=2] {'gz'}, dimensions={0} | all-to-all | bytes 65536 | tf_op jit(solution)/shard_map/all_to_all | solution.py:37
  (103 shorter events, 32.5 us)
Async XLA Ops:
  1.8 9.3 %collective-permute-start.6 = (bf16[1,8,48,512]{3,2,1,0:T(8,128)(2,1)S(1)}, bf16[1,8,48,512]{3,2,1,0:T(8,128)(2,1)S(1)}, u32[]{:S(2)}, u32[]{:S(2)}) collective-permute-start(bf16[1,8,48,512]{3,2,1,0:T(8,128)(2,1)S(1)} %get-tuple-element.95), channel_id=1, source_target_pairs={{0,32},{32,64},{64,96},{1,33},{33,65},{65,97},{2,34},{34,66},{66,9... | collective-permute-start | bytes 1179656 | tf_op jit(solution)/shard_map/ppermute | solution.py:20
  3.8 7.2 %collective-permute-start = (f32[2,1,8,48]{3,2,1,0:T(8,128)S(1)}, f32[2,1,8,48]{3,2,1,0:T(8,128)S(1)}, u32[]{:S(2)}, u32[]{:S(2)}) collective-permute-start(f32[2,1,8,48]{3,2,1,0:T(8,128)S(1)} %get-tuple-element.101), channel_id=1, source_target_pairs={{0,32},{32,64},{64,96},{1,33},{33,65},{65,97},{2,34},{34,66},{66,9... | collective-permute-start | bytes 9224 | tf_op jit(solution)/shard_map/ppermute | solution.py:20
  8.5 17.7 %collective-permute-start.1 = (f32[2,1,8,48]{3,2,1,0:T(8,128)S(1)}, f32[2,1,8,48]{3,2,1,0:T(8,128)S(1)}, u32[]{:S(2)}, u32[]{:S(2)}) collective-permute-start(f32[2,1,8,48]{3,2,1,0:T(8,128)S(1)} %get-tuple-element.100), channel_id=1, source_target_pairs={{32,0},{64,32},{96,64},{33,1},{65,33},{97,65},{34,2},{66,34},{98,6... | collective-permute-start | bytes 9224 | tf_op jit(solution)/shard_map/ppermute | solution.py:22
  9.8 5.2 %collective-permute-start.7 = (bf16[1,8,48,512]{3,2,1,0:T(8,128)(2,1)S(1)}, bf16[1,8,48,512]{3,2,1,0:T(8,128)(2,1)S(1)}, u32[]{:S(2)}, u32[]{:S(2)}) collective-permute-start(bf16[1,8,48,512]{3,2,1,0:T(8,128)(2,1)S(1)} %get-tuple-element.94), channel_id=1, source_target_pairs={{32,0},{64,32},{96,64},{33,1},{65,33},{97,65},{34,2},{66,34},{98,6... | collective-permute-start | bytes 1179656 | tf_op jit(solution)/shard_map/ppermute | solution.py:22
  11.2 15.0 %copy-start.3 = (f32[2,16,8,48]{3,2,1,0:T(8,128)S(1)}, f32[2,16,8,48]{3,2,1,0:T(8,128)}, u32[]{:S(2)}) copy-start(f32[2,16,8,48]{3,2,1,0:T(8,128)} %param.5) | copy-start | bytes 147460
  15.1 2.9 %copy-start.1 = (bf16[18,8,48,512]{3,2,1,0:T(8,128)(2,1)}, bf16[18,8,48,512]{3,2,1,0:T(8,128)(2,1)S(1)}, u32[]{:S(2)}) copy-start(bf16[18,8,48,512]{3,2,1,0:T(8,128)(2,1)S(1)} %constant_dynamic-update-slice_fusion.5) | copy-start | bytes 21233668
  19.4 37.6 %collective-permute-start.9 = (bf16[18,1,48,512]{3,2,1,0:T(8,128)(2,1)}, bf16[18,1,48,512]{3,2,1,0:T(8,128)(2,1)}, u32[]{:S(2)}, u32[]{:S(2)}) collective-permute-start(bf16[18,1,48,512]{3,2,1,0:T(8,128)(2,1)} %get-tuple-element.93), channel_id=1, source_target_pairs={{2,0},{4,2},{6,4},{8,6},{10,8},{12,10},{14,12},{16,14},{18,16},{20... | collective-permute-start | bytes 2654216 | tf_op jit(solution)/shard_map/ppermute | solution.py:22
  20.7 36.3 %collective-permute-start.8 = (bf16[18,1,48,512]{3,2,1,0:T(8,128)(2,1)}, bf16[18,1,48,512]{3,2,1,0:T(8,128)(2,1)}, u32[]{:S(2)}, u32[]{:S(2)}) collective-permute-start(bf16[18,1,48,512]{3,2,1,0:T(8,128)(2,1)} %get-tuple-element.92), channel_id=1, source_target_pairs={{0,2},{2,4},{4,6},{6,8},{8,10},{10,12},{12,14},{14,16},{16,18},{18... | collective-permute-start | bytes 2654216 | tf_op jit(solution)/shard_map/ppermute | solution.py:20
  26.1 48.3 %slice-start = ((s8[7077888]{0:T(1024)(128)(4,1)}), s8[2883584]{0:T(1024)(128)(4,1)S(1)}, s32[]{:S(2)}) async-start(s8[7077888]{0:T(1024)(128)(4,1)} %bitcast.41), calls=%async_computation.3 | async-start | bytes 5767168
  26.2 14.2 %collective-permute-start.3 = (f32[2,18,1,48]{3,2,1,0:T(1,128)S(1)}, f32[2,18,1,48]{3,2,1,0:T(1,128)S(1)}, u32[]{:S(2)}, u32[]{:S(2)}) collective-permute-start(f32[2,18,1,48]{3,2,1,0:T(1,128)S(1)} %get-tuple-element.99), channel_id=1, source_target_pairs={{2,0},{4,2},{6,4},{8,6},{10,8},{12,10},{14,12},{16,14},{18,16},{20... | collective-permute-start | bytes 20744 | tf_op jit(solution)/shard_map/ppermute | solution.py:22
  27.8 14.4 %collective-permute-start.2 = (f32[2,18,1,48]{3,2,1,0:T(1,128)S(1)}, f32[2,18,1,48]{3,2,1,0:T(1,128)S(1)}, u32[]{:S(2)}, u32[]{:S(2)}) collective-permute-start(f32[2,18,1,48]{3,2,1,0:T(1,128)S(1)} %get-tuple-element.98), channel_id=1, source_target_pairs={{0,2},{2,4},{4,6},{6,8},{8,10},{10,12},{12,14},{14,16},{16,18},{18... | collective-permute-start | bytes 20744 | tf_op jit(solution)/shard_map/ppermute | solution.py:20
  43.2 10.6 %collective-permute-start.5 = (f32[2,18,10,1]{3,2,1,0:T(8,128)}, f32[2,18,10,1]{3,2,1,0:T(8,128)S(1)}, u32[]{:S(2)}, u32[]{:S(2)}) collective-permute-start(f32[2,18,10,1]{3,2,1,0:T(8,128)} %get-tuple-element.97), channel_id=1, source_target_pairs={{1,0},{3,2},{5,4},{7,6},{9,8},{11,10},{13,12},{15,14},{17,16},{19,... | collective-permute-start | bytes 4328 | tf_op jit(solution)/shard_map/ppermute | solution.py:22
  44.5 11.2 %collective-permute-start.4 = (f32[2,18,10,1]{3,2,1,0:T(8,128)}, f32[2,18,10,1]{3,2,1,0:T(8,128)}, u32[]{:S(2)}, u32[]{:S(2)}) collective-permute-start(f32[2,18,10,1]{3,2,1,0:T(8,128)} %get-tuple-element.96), channel_id=1, source_target_pairs={{0,1},{2,3},{4,5},{6,7},{8,9},{10,11},{12,13},{14,15},{16,17},{18,... | collective-permute-start | bytes 4328 | tf_op jit(solution)/shard_map/ppermute | solution.py:20
  53.8 0.7 copy-start.2
  57.0 17.5 %slice-start.1 = ((s8[7077888]{0:T(1024)(128)(4,1)}), s8[4194304]{0:T(1024)(128)(4,1)S(1)}, s32[]{:S(2)}) async-start(s8[7077888]{0:T(1024)(128)(4,1)} %bitcast.41), calls=%async_computation.4 | async-start | bytes 8388608
  59.6 13.1 %collective-permute-start.11 = (bf16[18,10,1,512]{3,2,1,0:T(2,128)(2,1)S(1)}, bf16[18,10,1,512]{3,2,1,0:T(2,128)(2,1)S(1)}, u32[]{:S(2)}, u32[]{:S(2)}) collective-permute-start(bf16[18,10,1,512]{3,2,1,0:T(2,128)(2,1)S(1)} %get-tuple-element.91), channel_id=1, source_target_pairs={{1,0},{3,2},{5,4},{7,6},{9,8},{11,10},{13,12},{15,14},{17,16},{19,... | collective-permute-start | bytes 552968 | tf_op jit(solution)/shard_map/ppermute | solution.py:22
  60.9 13.6 %collective-permute-start.10 = (bf16[18,10,1,512]{3,2,1,0:T(2,128)(2,1)S(1)}, bf16[18,10,1,512]{3,2,1,0:T(2,128)(2,1)S(1)}, u32[]{:S(2)}, u32[]{:S(2)}) collective-permute-start(bf16[18,10,1,512]{3,2,1,0:T(2,128)(2,1)S(1)} %get-tuple-element.90), channel_id=1, source_target_pairs={{0,1},{2,3},{4,5},{6,7},{8,9},{10,11},{12,13},{14,15},{16,17},{18,... | collective-permute-start | bytes 552968 | tf_op jit(solution)/shard_map/ppermute | solution.py:20
  107.0 3.6 %copy-start = (bf16[16,8,48,128]{3,2,1,0:T(8,128)(2,1)S(1)}, bf16[16,8,48,128]{3,2,1,0:T(8,128)(2,1)}, u32[]{:S(2)}) copy-start(bf16[16,8,48,128]{3,2,1,0:T(8,128)(2,1)} %fusion.57) | copy-start | bytes 4718596 | tf_op jit(solution)/shard_map/while
  135.7 3.6 %copy-start = (bf16[16,8,48,128]{3,2,1,0:T(8,128)(2,1)S(1)}, bf16[16,8,48,128]{3,2,1,0:T(8,128)(2,1)}, u32[]{:S(2)}) copy-start(bf16[16,8,48,128]{3,2,1,0:T(8,128)(2,1)} %fusion.57) | copy-start | bytes 4718596 | tf_op jit(solution)/shard_map/while
  164.3 3.6 %copy-start = (bf16[16,8,48,128]{3,2,1,0:T(8,128)(2,1)S(1)}, bf16[16,8,48,128]{3,2,1,0:T(8,128)(2,1)}, u32[]{:S(2)}) copy-start(bf16[16,8,48,128]{3,2,1,0:T(8,128)(2,1)} %fusion.57) | copy-start | bytes 4718596 | tf_op jit(solution)/shard_map/while
  192.9 3.6 %copy-start = (bf16[16,8,48,128]{3,2,1,0:T(8,128)(2,1)S(1)}, bf16[16,8,48,128]{3,2,1,0:T(8,128)(2,1)}, u32[]{:S(2)}) copy-start(bf16[16,8,48,128]{3,2,1,0:T(8,128)(2,1)} %fusion.57) | copy-start | bytes 4718596 | tf_op jit(solution)/shard_map/while
where the time goes:
time: 279 us; the launch traced here: 277 us
  other arithmetic  116 us (42%)
  blocking collectives  61.6 us (22%)
  starting transfers between devices  37 us (13%)
  local copies, waits for them, and re-layouts  23 us (8%)
  waiting for transfers between devices  20.8 us (7%)
  matrix products  15.2 us (5%)
  loops' own time  3.05 us (1%)
    all_to_all x3, blocking collectives, sum_at_owner(): parts = lax.all_to_all(split_up(x, dim, devices), axis, 0, 0, tiled=True)  61.6 us
    add x37, other arithmetic, three_taps(): field = side * (lower + upper) + middle * centre  42.4 us
    ppermute x6, starting transfers between devices, with_halo(): lax.ppermute(tail, axis, [(i, (i + 1) % count) for i in range(ends)])  29 us
    convert_element_type x8, other arithmetic, apply_operators(): return (stiff_sum.astype(jnp.bfloat16), mass_sum.astype(jnp.bfloat16))  26.6 us
    mul x4, other arithmetic, apply_operators(): rho_values = rho[..., None] * values  23.2 us
    ppermute x6, waiting for transfers between devices, with_halo(): lax.ppermute(head, axis, [((i + 1) % count, i) for i in range(ends)])  16.2 us
    concatenate x3, other arithmetic, with_halo(): jnp.concatenate([lax.ppermute(tail, axis, [(i, (i + 1) % count) for i in...  10.9 us
    convert_element_type x4, other arithmetic, apply_operators(): values = padded.astype(jnp.float32)  8.28 us
  transfers between devices with their start and end apart: 12, of which 6 were waited for; matrix products, arithmetic and copies ran while one was open for 3% of the time, Pallas kernels for 0%

commit v1 on v0

v1 whole, which is shorter than its diff:
```python
import jax
import jax.numpy as jnp
from jax import lax
from jax.experimental import pallas as pl
from jax.experimental.pallas import tpu as pltpu
from jax.sharding import PartitionSpec as P

ALL = ("gx", "gy", "gz")
NGX, NGY, NGZ = 4, 16, 2
SX, SY, SZ, K = 16, 8, 48, 512
PLANES, LINES = SX + 1, SY + 1
GROUPS = (((8, 0, 1, 2, 3), (0, 1, 2)), ((2, 3, 4, 5, 6), (3, 4, 5)), ((5, 6, 7, 8, 0), (6, 7, 8)))
CELLS = LINES * SZ


def linear(x, y, z):
    return (x * NGY + y) * NGZ + z


def pairs(move):
    out = []
    for x in range(NGX):
        for y in range(NGY):
            for z in range(NGZ):
                to = move(x, y, z)
                if 0 <= to[0] < NGX and 0 <= to[1] < NGY and 0 <= to[2] < NGZ:
                    out.append((linear(x, y, z), linear(*to)))
    return out


def send(value, move):
    return lax.ppermute(value, ALL, pairs(move))


def to_z(x, y, z):
    return (x, y, 1 - z)


def to_x(x, y, z):
    return (x - 1, y, z)


def to_y(x, y, z):
    return (x, y + 1, z) if x % 2 else (x, y - 1, z)


def line_links(odd):
    here = jnp.arange(LINES)[:, None]
    there = jnp.arange(LINES)[None, :]
    near = (jnp.abs(here - there) == 1) & (here != 8) & (there != 8)
    inner = jnp.where(odd, 0, 7)
    near = near | ((here == 8) & (there == inner)) | ((there == 8) & (here == inner))
    same = (here == there) & (here != 8)
    return near.astype(jnp.float32), same.astype(jnp.float32)


def band_matrices(odd, upper):
    row = lax.broadcasted_iota(jnp.int32, (3, 6 * SZ, 256), 1)
    col = lax.broadcasted_iota(jnp.int32, (3, 6 * SZ, 256), 2)
    grp = lax.broadcasted_iota(jnp.int32, (3, 6 * SZ, 256), 0)
    mid = jnp.where(row < 3 * SZ, 2.0, 4.0)
    cell = row % (3 * SZ)
    line_out = grp * 3 + cell // SZ
    z_out = cell % SZ
    halo = col >= 5 * SZ
    slot = col // SZ
    first = jnp.where(grp == 0, 8, jnp.where(grp == 1, 2, 5))
    line_in = jnp.where(halo, col - 5 * SZ, (first + slot) % LINES)
    z_in = jnp.where(halo, jnp.where(upper, -1, SZ), col % SZ)
    z_gap = jnp.abs(z_out - z_in)
    z_part = jnp.where(z_gap == 0, mid, jnp.where(z_gap == 1, 1.0, 0.0))
    both_own = (line_out != 8) & (line_in != 8)
    inner = jnp.where(odd, 0, 7)
    near = (both_own & (jnp.abs(line_out - line_in) == 1)) | (
        ((line_out == 8) & (line_in == inner)) | ((line_in == 8) & (line_out == inner))
    )
    same = both_own & (line_out == line_in)
    y_part = jnp.where(same, mid, jnp.where(near, 1.0, 0.0))
    return (y_part * z_part).astype(jnp.bfloat16)


def coefficients(kappa, rho, kappa_z, odd, upper):
    zero = jnp.zeros((PLANES, LINES, 1), jnp.float32)
    edge = kappa_z[..., None]
    below = jnp.concatenate([jnp.where(upper, edge, zero), kappa[..., :-1]], axis=2)
    above = jnp.concatenate([kappa[..., 1:], jnp.where(upper, zero, edge)], axis=2)
    f = 2.0 * kappa + below + above
    own_line = (jnp.arange(LINES) != 8)[None, :, None]
    own_plane = (jnp.arange(PLANES) != SX)[:, None, None]
    zline = jnp.zeros((PLANES, 1, SZ), jnp.float32)
    own = f[:, :8]
    halo = f[:, 8:9]
    lower = jnp.concatenate([jnp.where(odd, halo, zline), own[:, :-1]], axis=1)
    higher = jnp.concatenate([own[:, 1:], jnp.where(odd, zline, halo)], axis=1)
    inner = jnp.where(odd, own[:, 0:1], own[:, 7:8])
    f = jnp.concatenate([2.0 * own + lower + higher, inner], axis=1)
    zplane = jnp.zeros((1, LINES, SZ), jnp.float32)
    before = jnp.concatenate([zplane, f[:-1]], axis=0)
    after = jnp.concatenate([f[1:], zplane], axis=0)
    f = jnp.where(own_plane, 2.0 * f, 0.0) + before + after
    alpha = jnp.where(own_plane & own_line, 2.0 * kappa, 0.0) + f * (1.0 / 32.0)
    table = jnp.stack([alpha, kappa * (1.0 / 16.0), rho * (1.0 / 216.0)], axis=1)
    table = table.reshape(PLANES, 3, CELLS)
    return jnp.pad(table, ((0, 0), (0, 5), (0, 512 - CELLS)))


def project_kernel(v_hbm, xh_hbm, yh_hbm, zt_ref, coef_ref, band_ref, out_ref, ve, w2, t2, u, acc, sem):
    def copies(p):
        own = pltpu.make_async_copy(v_hbm.at[p], ve.at[p, pl.ds(0, 8)], sem.at[p])
        return own

    halo_copies = [
        pltpu.make_async_copy(xh_hbm, ve.at[SX, pl.ds(0, 8)], sem.at[SX]),
        pltpu.make_async_copy(yh_hbm, ve.at[:, 8], sem.at[SX + 1]),
    ]
    for c in halo_copies:
        c.start()
    for p in range(SX):
        copies(p).start()
    acc[...] = jnp.zeros(acc.shape, jnp.float32)
    w2[2] = jnp.zeros(w2.shape[1:], jnp.float32)
    t2[2] = jnp.zeros(t2.shape[1:], jnp.float32)
    for c in halo_copies:
        c.wait()

    def filter_plane(p, slot):
        ztile = zt_ref[p]
        for g, (ins, outs) in enumerate(GROUPS):
            block = jnp.concatenate([ve[p, l] for l in ins] + [ztile], axis=0)
            r = jnp.dot(band_ref[g], block, preferred_element_type=jnp.float32)
            w2[slot, pl.ds(g * 3 * SZ, 3 * SZ)] = r[: 3 * SZ]
            t2[slot, pl.ds(g * 3 * SZ, 3 * SZ)] = r[3 * SZ :]

    def project_plane(p, prev, cur, nxt):
        coef = jnp.transpose(coef_ref[p])
        for l in range(LINES):
            rows = pl.ds(l * SZ, SZ)
            c = coef[l * SZ : (l + 1) * SZ]
            wide = (SZ, K)
            if nxt is None:
                w3 = w2[prev, rows]
                t3 = t2[prev, rows]
            else:
                mid = w2[cur, rows]
                w3 = w2[prev, rows] + (mid + mid) + w2[nxt, rows]
                t3 = t2[prev, rows] + 4.0 * t2[cur, rows] + t2[nxt, rows]
            v = ve[p, l].astype(jnp.float32)
            alpha = jnp.broadcast_to(c[:, 0:1], wide)
            kap = jnp.broadcast_to(c[:, 1:2], wide)
            rho = jnp.broadcast_to(c[:, 2:3], wide)
            u[rows, 0:K] = (alpha * v - kap * w3).astype(jnp.bfloat16)
            u[rows, K : 2 * K] = (rho * t3).astype(jnp.bfloat16)
        left = ve[p].reshape(CELLS, K)
        acc[...] += lax.dot_general(
            left, u[...], (((0,), (0,)), ((), ())), preferred_element_type=jnp.float32
        )

    copies(0).wait()
    filter_plane(0, 0)

    def step(p, carry):
        @pl.when(p + 1 < SX)
        def _():
            copies(p + 1).wait()

        prev = lax.rem(p + 2, 3)
        cur = lax.rem(p, 3)
        nxt = lax.rem(p + 1, 3)
        filter_plane(p + 1, nxt)
        project_plane(p, prev, cur, nxt)
        return carry

    lax.fori_loop(0, SX, step, 0)
    project_plane(SX, (SX + 2) % 3, None, None)
    for half in range(2):
        for i in range(4):
            for j in range(i, 4):
                a = acc[i * 128 : (i + 1) * 128, half * K + j * 128 : half * K + (j + 1) * 128]
                b = acc[j * 128 : (j + 1) * 128, half * K + i * 128 : half * K + (i + 1) * 128]
                s = a + b.T
                out_ref[i * 128 : (i + 1) * 128, half * K + j * 128 : half * K + (j + 1) * 128] = s
                if i != j:
                    out_ref[j * 128 : (j + 1) * 128, half * K + i * 128 : half * K + (i + 1) * 128] = s.T


def project(v, xh, yh, zt, coef, band):
    hbm = pl.BlockSpec(memory_space=pl.ANY)
    vmem = pl.BlockSpec(memory_space=pltpu.VMEM)
    return pl.pallas_call(
        project_kernel,
        out_shape=jax.ShapeDtypeStruct((K, 2 * K), jnp.float32),
        in_specs=[hbm, hbm, hbm, vmem, vmem, vmem],
        out_specs=vmem,
        scratch_shapes=[
            pltpu.VMEM((PLANES, LINES, SZ, K), jnp.bfloat16),
            pltpu.VMEM((3, CELLS, K), jnp.float32),
            pltpu.VMEM((3, CELLS, K), jnp.float32),
            pltpu.VMEM((CELLS, 2 * K), jnp.bfloat16),
            pltpu.VMEM((K, 2 * K), jnp.float32),
            pltpu.SemaphoreType.DMA((SX + 2,)),
        ],
        compiler_params=pltpu.CompilerParams(vmem_limit_bytes=40 * 1024 * 1024),
        cost_estimate=pl.CostEstimate(flops=13_000_000_000, transcendentals=0, bytes_accessed=12_000_000),
        name="project",
    )(v, xh, yh, zt, coef, band)


def pick(x, index, dim):
    return lax.dynamic_index_in_dim(x, index, dim, keepdims=False)


def reduce_to_owner(part):
    ix = lax.axis_index("gx")
    iy = lax.axis_index("gy")
    core = ix % 2
    z_lo = ix // 2
    z_hi = lax.axis_index("gz")
    cx = iy // 4
    cy = iy % 4
    v = part.reshape(2, 2, 4, 4, 8, 2 * K)
    v = pick(v, core, 1) + send(pick(v, 1 - core, 1), lambda x, y, z: (x ^ 1, y, z))
    v = pick(v, z_lo, 0) + send(pick(v, 1 - z_lo, 0), lambda x, y, z: (x ^ 2, y, z))
    parts = [send(pick(v, (cx + d) % 4, 0), lambda x, y, z, d=d: (x, (y + 4 * d) % 16, z)) for d in (1, 2, 3)]
    v = pick(v, cx, 0) + parts[0] + parts[1] + parts[2]
    parts = [send(pick(v, (cy + d) % 4, 0), lambda x, y, z, d=d: (x, y // 4 * 4 + (y + d) % 4, z)) for d in (1, 2, 3)]
    v = pick(v, cy, 0) + parts[0] + parts[1] + parts[2]
    v = v.reshape(2, 4, 2 * K)
    return pick(v, z_hi, 0) + send(pick(v, 1 - z_hi, 0), to_z)


def per_device(eigvecs, material):
    ix = lax.axis_index("gx")
    odd = ix % 2 == 1
    upper = lax.axis_index("gz") == 1
    rho = material[1]
    kappa = material[0]
    kz = send(jnp.where(upper, kappa[:, :, 0], kappa[:, :, SZ - 1]), to_z)
    zh = send(jnp.where(upper, eigvecs[:, :, 0], eigvecs[:, :, SZ - 1]), to_z)
    mx = send(jnp.concatenate([kappa[0], rho[0], kz[0][:, None]], axis=1), to_x)
    vx = send(jnp.concatenate([eigvecs[0].reshape(SY * SZ, K), zh[0]], axis=0), to_x)
    xh = vx[: SY * SZ].reshape(SY, SZ, K)
    xz = vx[SY * SZ :]
    kappa = jnp.concatenate([kappa, mx[None, :, :SZ]], axis=0)
    rho = jnp.concatenate([rho, mx[None, :, SZ : 2 * SZ]], axis=0)
    kz = jnp.concatenate([kz, mx[None, :, 2 * SZ]], axis=0)
    zt = jnp.concatenate([zh, xz[None]], axis=0)
    side = jnp.where(odd, SY - 1, 0)
    my = send(jnp.concatenate([pick(kappa, side, 1), pick(rho, side, 1), pick(kz, side, 1)[:, None]], axis=1), to_y)
    yrow = jnp.concatenate([pick(eigvecs, side, 1), pick(xh, side, 0)[None]], axis=0)
    vy = send(jnp.concatenate([yrow.reshape(PLANES * SZ, K), pick(zt, side, 1)], axis=0), to_y)
    yh = vy[: PLANES * SZ].reshape(PLANES, SZ, K)
    yz = vy[PLANES * SZ :]
    kappa = jnp.concatenate([kappa, my[:, None, :SZ]], axis=1)
    rho = jnp.concatenate([rho, my[:, None, SZ : 2 * SZ]], axis=1)
    kz = jnp.concatenate([kz, my[:, None, 2 * SZ]], axis=1)
    zt = jnp.concatenate([zt, yz[:, None], jnp.zeros((PLANES, 16 - LINES, K), jnp.bfloat16)], axis=1)
    coef = coefficients(kappa, rho, kz, odd, upper)
    band = band_matrices(odd, upper)
    part = project(eigvecs, xh, yh, zt, coef, band)
    total = SX * SY * SZ * NGX * NGY * NGZ
    summed = reduce_to_owner(part) * (0.5 / total)
    return summed[:, :K], summed[:, K:]


def solution(mesh):
    return jax.shard_map(
        per_device,
        mesh=mesh,
        in_specs=(P("gx", "gy", "gz", None), P(None, "gx", "gy", "gz")),
        out_specs=(P(ALL, None), P(ALL, None)),
        check_vma=False,
    )
```

time: 279 us -> 123 us (0.44)
  other arithmetic: 116 us -> 5.58 us
  blocking collectives: 61.6 us -> 0 us
  Pallas kernels: 0 us -> 27 us
  waiting for transfers between devices: 20.8 us -> 44 us
  matrix products: 15.2 us -> 0 us
  local copies, waits for them, and re-layouts: 23 us -> 12.4 us
  starting transfers between devices: 37 us -> 32.5 us
  loops' own time: 3.05 us -> 0 us
    all_to_all x3 -> x0, blocking collectives: 61.6 us -> none  [sum_at_owner(): parts = lax.all_to_all(split_up(x, dim, devices), axis, 0, 0, tiled=True)]
    add x37 -> x7, other arithmetic: 42.4 us -> 1.74 us  [the longest x1 1.36 us: reduce_to_owner(): pick(v, core, 1) + send(pick(v, 1 - core, 1), lambda x, y, z: (x ^ 1, y, z))]
    convert_element_type x12 -> x1, other arithmetic: 34.9 us -> 1.16 us  [band_matrices(): return (y_part * z_part).astype(jnp.bfloat16)]
    pallas_call x0 -> x1, Pallas kernels: none -> 27 us  [project(): pl.pallas_call(project_kernel, out_shape=jax.ShapeDtypeStruct((K, 2 * K),...]
    mul x12 -> x3, other arithmetic: 24 us -> 0.29 us  [the longest x1 0.26 us: coefficients(): kappa * (1.0 / 16.0)]
    ppermute x12 -> x15, waiting for transfers between devices: 20.8 us -> 44 us  [send(): return lax.ppermute(value, ALL, pairs(move))]
    dot_general x2 -> x0, matrix products: 15.2 us -> none  [the longest x1 7.74 us: per_device(): jnp.einsum('cp,bcq->pbq', flat_vectors, stiff_blocks, preferred_element_t...]
    concatenate x4 -> x16, other arithmetic: 11 us -> 2.03 us  [the longest x1 0.97 us: per_device(): jnp.concatenate([yrow.reshape(PLANES * SZ, K), pick(zt, side, 1)], axis=0)]
  transfers between devices with their start and end apart: 12 -> 15, of which waited for: 6 -> 11; matrix products, arithmetic and copies ran while one was open for 3% -> 9% of each run, Pallas kernels for 0% -> 0%
where the time goes in v1:
time: 123 us
  waiting for transfers between devices  44 us (36%)
  starting transfers between devices  32.5 us (26%)
  Pallas kernels  27 us (22%)
  local copies, waits for them, and re-layouts  12.4 us (10%)
  other arithmetic  5.58 us (5%)
  between operations  1.24 us (1%)
    ppermute x15, waiting for transfers between devices, send(): return lax.ppermute(value, ALL, pairs(move))  44 us
    ppermute x15, starting transfers between devices, send(): return lax.ppermute(value, ALL, pairs(move))  32.5 us
    pallas_call x1, Pallas kernels, project(): pl.pallas_call(project_kernel, out_shape=jax.ShapeDtypeStruct((K, 2 * K),...  27 us
    unnamed x13, local copies, waits for them, and re-layouts  2.94 us
  transfers between devices with their start and end apart: 15, of which 11 were waited for; matrix products, arithmetic and copies ran while one was open for 9% of the time, Pallas kernels for 0%

profile of v1, /device:TPU:0, one launch (start us, length us, event | category | flops | bytes accessed | tf_op | source)
XLA Modules:
  0.0 122.8 jit_solution(3972169609214630991)
XLA Ops:
  0.6 0.9 slice_bitcast_fusion
  1.5 0.1 copy.130
  1.7 4.1 %collective-permute-start.3 = (f32[16,8]{0,1:T(8,128)S(1)}, f32[16,8]{0,1:T(8,128)S(1)}, u32[]{:S(2)}, u32[]{:S(2)}) collective-permute-start(f32[16,8]{0,1:T(8,128)S(1)} %fusion.43), channel_id=1, source_target_pairs={{0,1},{1,0},{2,3},{3,2},{4,5},{5,4},{6,7},{7,6},{8,9},{9,8},{10,11... | collective-permute-start | bytes 1544 | tf_op jit(solution)/shard_map/ppermute | solution.py:32
  5.7 2.1 %fusion.51 = (bf16[16,8,1,512]{3,2,1,0:T(2,128)(2,1)S(1)}, bf16[16,8,1,512]{3,2,1,0:T(2,128)(2,1)S(1)}) fusion(bf16[16,8,48,512]{3,2,1,0:T(8,128)(2,1)} %v_hbm.1), kind=kLoop, calls=%fused_computation.145 | loop fusion | bytes 524288 | tf_op jit(solution)/shard_map/slice | solution.py:238
  8.0 0.7 slice_bitcast_fusion.12
  8.8 1.2 multiply_convert_fusion.band_ref
  10.2 1.3 %collective-permute-start.4 = (f32[8,97]{1,0:T(8,128)S(1)}, f32[8,97]{1,0:T(8,128)S(1)}, u32[]{:S(2)}, u32[]{:S(2)}) collective-permute-start(f32[8,97]{1,0:T(8,128)S(1)} %pad_maximum_fusion.9), channel_id=1, source_target_pairs={{32,0},{33,1},{34,2},{35,3},{36,4},{37,5},{38,6},{39,7},{40,8},{41... | collective-permute-start | bytes 9320 | tf_op jit(solution)/shard_map/ppermute | solution.py:32
  11.5 1.2 dynamic-slice_bitcast_fusion.1
  12.7 0.6 pad.43.clone
  13.4 0.2 copy.113
  14.4 1.3 %collective-permute-start.5 = (f32[17,97]{1,0:T(8,128)S(1)}, f32[17,97]{1,0:T(8,128)S(1)}, u32[]{:S(2)}, u32[]{:S(2)}) collective-permute-start(f32[17,97]{1,0:T(8,128)S(1)} %pad_maximum_fusion.7), channel_id=1, source_target_pairs={{2,0},{3,1},{4,2},{5,3},{6,4},{7,5},{8,6},{9,7},{10,8},{11,9},{12,... | collective-permute-start | bytes 19796 | tf_op jit(solution)/shard_map/ppermute | solution.py:32
  15.7 0.1 copy.117
  15.9 0.8 copy.122
  16.7 3.3 %collective-permute-done.5 = f32[17,97]{1,0:T(8,128)S(1)} collective-permute-done((f32[17,97]{1,0:T(8,128)S(1)}, f32[17,97]{1,0:T(8,128)S(1)}, u32[]{:S(2)}, u32[]{:S(2)}) %collective-permute-start.5) | collective-permute-done | bytes 6628 | tf_op jit(solution)/shard_map/ppermute | solution.py:32
  19.9 0.7 slice_bitcast_fusion.4
  20.6 0.2 slice_reduce_fusion
  21.0 1.3 %collective-permute-start.1 = (bf16[392,512]{1,0:T(8,128)(2,1)S(1)}, bf16[392,512]{1,0:T(8,128)(2,1)S(1)}, u32[]{:S(2)}, u32[]{:S(2)}) collective-permute-start(bf16[392,512]{1,0:T(8,128)(2,1)S(1)} %pad_maximum_fusion.2), channel_id=1, source_target_pairs={{32,0},{33,1},{34,2},{35,3},{36,4},{37,5},{38,6},{39,7},{40,8},{41... | collective-permute-start | bytes 1204232 | tf_op jit(solution)/shard_map/ppermute | solution.py:32
  22.3 0.1 copy.119
  22.4 0.1 copy.120
  22.6 0.1 fusion.28
  22.7 1.9 %collective-permute-done.1 = bf16[392,512]{1,0:T(8,128)(2,1)S(1)} collective-permute-done((bf16[392,512]{1,0:T(8,128)(2,1)S(1)}, bf16[392,512]{1,0:T(8,128)(2,1)S(1)}, u32[]{:S(2)}, u32[]{:S(2)}) %collective-permute-start.1) | collective-permute-done | bytes 401440 | tf_op jit(solution)/shard_map/ppermute | solution.py:32
  24.8 1.0 pad_maximum_fusion
  25.8 1.3 %collective-permute-start.2 = (bf16[833,512]{1,0:T(8,128)(2,1)}, bf16[833,512]{1,0:T(8,128)(2,1)S(1)}, u32[]{:S(2)}, u32[]{:S(2)}) collective-permute-start(bf16[833,512]{1,0:T(8,128)(2,1)} %pad_maximum_fusion), channel_id=1, source_target_pairs={{2,0},{3,1},{4,2},{5,3},{6,4},{7,5},{8,6},{9,7},{10,8},{11,9},{12,... | collective-permute-start | bytes 2558984 | tf_op jit(solution)/shard_map/ppermute | solution.py:32
  27.3 0.1 stack.10
  27.5 0.3 fusion.31
  27.8 0.1 mul.83
  28.0 0.1 mul.86
  28.1 0.1 select_maximum_fusion.coef_ref
  28.3 12.4 %collective-permute-done.2 = bf16[833,512]{1,0:T(8,128)(2,1)S(1)} collective-permute-done((bf16[833,512]{1,0:T(8,128)(2,1)}, bf16[833,512]{1,0:T(8,128)(2,1)S(1)}, u32[]{:S(2)}, u32[]{:S(2)}) %collective-permute-start.2) | collective-permute-done | bytes 853024 | tf_op jit(solution)/shard_map/ppermute | solution.py:32
  40.9 2.8 %copy-done = bf16[16,8,48,512]{3,2,1,0:T(8,128)(2,1)S(1)} copy-done((bf16[16,8,48,512]{3,2,1,0:T(8,128)(2,1)S(1)}, bf16[16,8,48,512]{3,2,1,0:T(8,128)(2,1)}, u32[]{:S(2)}) %copy-start) | copy-done | bytes 6291480
  43.7 27.0 %project.1 = f32[512,1024]{1,0:T(8,128)S(1)} custom-call(bf16[16,8,48,512]{3,2,1,0:T(8,128)(2,1)S(1)} %copy-done, bf16[8,48,512]{2,1,0:T(8,128)(2,1)S(1)} %bitcast.98, bf16[17,48,512]{2,1,0:T(8,128)(2,1)S(1)} %bitcast.96, bf16[17,16,512]{2,1,0:T(8,128)(2,1)S(1)} %maximum_maximum_fusion.zt_ref, f32[17,8,512]{2,1,0:T(8,128)S(1)} %select_maximum_fusion.coef_ref, ...), custom_call_target="tpu_custom_call" | custom-call | flops 12999999488 | bytes 12000000 | tf_op jit(solution)/shard_map/project/pallas_call | solution.py:189
  70.8 4.6 %collective-permute-start.6 = (f32[2,4,4,8,1024]{4,3,2,1,0:T(8,128)S(1)}, f32[2,4,4,8,1024]{4,3,2,1,0:T(8,128)}, u32[]{:S(2)}, u32[]{:S(2)}) collective-permute-start(f32[2,4,4,8,1024]{4,3,2,1,0:T(8,128)S(1)} %dynamic-slice_bitcast_fusion), channel_id=1, source_target_pairs={{0,32},{1,33},{2,34},{3,35},{4,36},{5,37},{6,38},{7,39},{8,40},{9,... | collective-permute-start | bytes 3145736 | tf_op jit(solution)/shard_map/ppermute | solution.py:32
  75.4 2.4 %collective-permute-done.6 = f32[2,4,4,8,1024]{4,3,2,1,0:T(8,128)} collective-permute-done((f32[2,4,4,8,1024]{4,3,2,1,0:T(8,128)S(1)}, f32[2,4,4,8,1024]{4,3,2,1,0:T(8,128)}, u32[]{:S(2)}, u32[]{:S(2)}) %collective-permute-start.6) | collective-permute-done | bytes 1048608 | tf_op jit(solution)/shard_map/ppermute | solution.py:32
  77.8 1.4 %bitcast_add_fusion = f32[2,4,4,8,1024]{4,3,2,1,0:T(8,128)S(1)} fusion(f32[2,4,4,8,1024]{4,3,2,1,0:T(8,128)} %collective-permute-done.6, f32[2,2,4,4,8,1024]{5,4,3,2,1,0:T(8,128)S(1)} %bitcast.95, s32[]{:T(128)S(6)} %select_n.326), kind=kLoop, calls=%fused_computation.9 | loop fusion | flops 262144 | bytes 3145732 | tf_op jit(solution)/shard_map/add | solution.py:221
  79.2 1.8 %collective-permute-start.7 = (f32[4,4,8,1024]{3,2,1,0:T(8,128)S(1)}, f32[4,4,8,1024]{3,2,1,0:T(8,128)S(1)}, u32[]{:S(2)}, u32[]{:S(2)}) collective-permute-start(f32[4,4,8,1024]{3,2,1,0:T(8,128)S(1)} %dynamic-slice_bitcast_fusion.2), channel_id=1, source_target_pairs={{0,64},{1,65},{2,66},{3,67},{4,68},{5,69},{6,70},{7,71},{8,72},{9,... | collective-permute-start | bytes 1572872 | tf_op jit(solution)/shard_map/ppermute | solution.py:32
  81.0 12.5 %collective-permute-done.7 = f32[4,4,8,1024]{3,2,1,0:T(8,128)S(1)} collective-permute-done((f32[4,4,8,1024]{3,2,1,0:T(8,128)S(1)}, f32[4,4,8,1024]{3,2,1,0:T(8,128)S(1)}, u32[]{:S(2)}, u32[]{:S(2)}) %collective-permute-start.7) | collective-permute-done | bytes 524320 | tf_op jit(solution)/shard_map/ppermute | solution.py:32
  93.6 7.6 %collective-permute-start.10 = (f32[4,8,1024]{2,1,0:T(8,128)S(1)}, f32[4,8,1024]{2,1,0:T(8,128)S(1)}, u32[]{:S(2)}, u32[]{:S(2)}) collective-permute-start(f32[4,8,1024]{2,1,0:T(8,128)S(1)} %get-tuple-element.5), channel_id=1, source_target_pairs={{0,24},{1,25},{2,26},{3,27},{4,28},{5,29},{6,30},{7,31},{8,0},{9,1... | collective-permute-start | bytes 393224 | tf_op jit(solution)/shard_map/ppermute | solution.py:32
  101.2 2.3 %collective-permute-start.9 = (f32[4,8,1024]{2,1,0:T(8,128)S(1)}, f32[4,8,1024]{2,1,0:T(8,128)S(1)}, u32[]{:S(2)}, u32[]{:S(2)}) collective-permute-start(f32[4,8,1024]{2,1,0:T(8,128)S(1)} %get-tuple-element.6), channel_id=1, source_target_pairs={{0,16},{1,17},{2,18},{3,19},{4,20},{5,21},{6,22},{7,23},{8,24},{9,... | collective-permute-start | bytes 393224 | tf_op jit(solution)/shard_map/ppermute | solution.py:32
  103.5 0.2 collective-permute-done.10
  103.7 6.1 %collective-permute-done.8 = f32[4,8,1024]{2,1,0:T(8,128)S(1)} collective-permute-done((f32[4,8,1024]{2,1,0:T(8,128)S(1)}, f32[4,8,1024]{2,1,0:T(8,128)S(1)}, u32[]{:S(2)}, u32[]{:S(2)}) %collective-permute-start.8) | collective-permute-done | bytes 131104 | tf_op jit(solution)/shard_map/ppermute | solution.py:32
  110.0 2.8 %collective-permute-start.12 = (f32[8,1024]{1,0:T(8,128)S(1)}, f32[8,1024]{1,0:T(8,128)S(1)}, u32[]{:S(2)}, u32[]{:S(2)}) collective-permute-start(f32[8,1024]{1,0:T(8,128)S(1)} %get-tuple-element.9), channel_id=1, source_target_pairs={{0,4},{1,5},{2,6},{3,7},{4,0},{5,1},{6,2},{7,3},{8,12},{9,13},{10,... | collective-permute-start | bytes 98312 | tf_op jit(solution)/shard_map/ppermute | solution.py:32
  112.8 0.4 collective-permute-start.13
  113.2 1.9 %collective-permute-done.11 = f32[8,1024]{1,0:T(8,128)S(1)} collective-permute-done((f32[8,1024]{1,0:T(8,128)S(1)}, f32[8,1024]{1,0:T(8,128)S(1)}, u32[]{:S(2)}, u32[]{:S(2)}) %collective-permute-start.11) | collective-permute-done | bytes 32800 | tf_op jit(solution)/shard_map/ppermute | solution.py:32
  115.1 0.4 collective-permute-done.12
  115.5 1.2 collective-permute-done.13
  116.8 3.7 %collective-permute-start.14 = (f32[4,1024]{1,0:T(4,128)S(1)}, f32[4,1024]{1,0:T(4,128)S(1)}, u32[]{:S(2)}, u32[]{:S(2)}) collective-permute-start(f32[4,1024]{1,0:T(4,128)S(1)} %dynamic-slice_bitcast_fusion.9), channel_id=1, source_target_pairs={{0,1},{1,0},{2,3},{3,2},{4,5},{5,4},{6,7},{7,6},{8,9},{9,8},{10,11... | collective-permute-start | bytes 49160 | tf_op jit(solution)/shard_map/ppermute | solution.py:32
  120.4 1.7 %collective-permute-done.14 = f32[4,1024]{1,0:T(4,128)S(1)} collective-permute-done((f32[4,1024]{1,0:T(4,128)S(1)}, f32[4,1024]{1,0:T(4,128)S(1)}, u32[]{:S(2)}, u32[]{:S(2)}) %collective-permute-start.14) | collective-permute-done | bytes 16416 | tf_op jit(solution)/shard_map/ppermute | solution.py:32
  122.2 0.6 fusion.53
  (83 shorter events, 2.5 us)
Async XLA Ops:
  1.7 8.4 %collective-permute-start.3 = (f32[16,8]{0,1:T(8,128)S(1)}, f32[16,8]{0,1:T(8,128)S(1)}, u32[]{:S(2)}, u32[]{:S(2)}) collective-permute-start(f32[16,8]{0,1:T(8,128)S(1)} %fusion.43), channel_id=1, source_target_pairs={{0,1},{1,0},{2,3},{3,2},{4,5},{5,4},{6,7},{7,6},{8,9},{9,8},{10,11... | collective-permute-start | bytes 1544 | tf_op jit(solution)/shard_map/ppermute | solution.py:32
  7.9 13.0 %collective-permute-start = (bf16[16,8,512]{2,1,0:T(8,128)(2,1)S(1)}, bf16[16,8,512]{2,1,0:T(8,128)(2,1)S(1)}, u32[]{:S(2)}, u32[]{:S(2)}) collective-permute-start(bf16[16,8,512]{2,1,0:T(8,128)(2,1)S(1)} %fusion.16), channel_id=1, source_target_pairs={{0,1},{1,0},{2,3},{3,2},{4,5},{5,4},{6,7},{7,6},{8,9},{9,8},{10,11... | collective-permute-start | bytes 393224 | tf_op jit(solution)/shard_map/ppermute | solution.py:32
  10.2 3.1 %collective-permute-start.4 = (f32[8,97]{1,0:T(8,128)S(1)}, f32[8,97]{1,0:T(8,128)S(1)}, u32[]{:S(2)}, u32[]{:S(2)}) collective-permute-start(f32[8,97]{1,0:T(8,128)S(1)} %pad_maximum_fusion.9), channel_id=1, source_target_pairs={{32,0},{33,1},{34,2},{35,3},{36,4},{37,5},{38,6},{39,7},{40,8},{41... | collective-permute-start | bytes 9320 | tf_op jit(solution)/shard_map/ppermute | solution.py:32
  12.7 8.3 %slice-start = ((bf16[16,8,48,512]{3,2,1,0:T(8,128)(2,1)}), bf16[1,8,48,512]{3,2,1,0:T(8,128)(2,1)S(1)}, s32[]{:S(2)}) async-start(bf16[16,8,48,512]{3,2,1,0:T(8,128)(2,1)} %v_hbm.1), calls=%async_computation | async-start | bytes 786432 | tf_op jit(solution)/shard_map/slice | solution.py:240
  14.4 5.6 %collective-permute-start.5 = (f32[17,97]{1,0:T(8,128)S(1)}, f32[17,97]{1,0:T(8,128)S(1)}, u32[]{:S(2)}, u32[]{:S(2)}) collective-permute-start(f32[17,97]{1,0:T(8,128)S(1)} %pad_maximum_fusion.7), channel_id=1, source_target_pairs={{2,0},{3,1},{4,2},{5,3},{6,4},{7,5},{8,6},{9,7},{10,8},{11,9},{12,... | collective-permute-start | bytes 19796 | tf_op jit(solution)/shard_map/ppermute | solution.py:32
  21.0 3.6 %collective-permute-start.1 = (bf16[392,512]{1,0:T(8,128)(2,1)S(1)}, bf16[392,512]{1,0:T(8,128)(2,1)S(1)}, u32[]{:S(2)}, u32[]{:S(2)}) collective-permute-start(bf16[392,512]{1,0:T(8,128)(2,1)S(1)} %pad_maximum_fusion.2), channel_id=1, source_target_pairs={{32,0},{33,1},{34,2},{35,3},{36,4},{37,5},{38,6},{39,7},{40,8},{41... | collective-permute-start | bytes 1204232 | tf_op jit(solution)/shard_map/ppermute | solution.py:32
  24.8 2.7 %copy-start.3 = (f32[17,1,1,48]{3,0,2,1:T(8,128)S(1)}, f32[17,1,1,48]{3,0,2,1:T(8,128)}, u32[]{:S(2)}) copy-start(f32[17,1,1,48]{3,0,2,1:T(8,128)} %get-tuple-element.26) | copy-start | bytes 9796
  24.8 2.7 %copy-start.1 = (f32[17,1,8,48]{3,1,2,0:T(1,128)S(1)}, f32[17,1,8,48]{3,1,2,0:T(1,128)}, u32[]{:S(2)}) copy-start(f32[17,1,8,48]{3,1,2,0:T(1,128)} %copy.122) | copy-start | bytes 78340
  24.8 3.1 %copy-start.2 = (f32[17,1,1,48]{3,0,2,1:T(8,128)S(1)}, f32[17,1,1,48]{3,0,2,1:T(8,128)}, u32[]{:S(2)}) copy-start(f32[17,1,1,48]{3,0,2,1:T(8,128)} %get-tuple-element.27) | copy-start | bytes 9796
  25.8 14.9 %collective-permute-start.2 = (bf16[833,512]{1,0:T(8,128)(2,1)}, bf16[833,512]{1,0:T(8,128)(2,1)S(1)}, u32[]{:S(2)}, u32[]{:S(2)}) collective-permute-start(bf16[833,512]{1,0:T(8,128)(2,1)} %pad_maximum_fusion), channel_id=1, source_target_pairs={{2,0},{3,1},{4,2},{5,3},{6,4},{7,5},{8,6},{9,7},{10,8},{11,9},{12,... | collective-permute-start | bytes 2558984 | tf_op jit(solution)/shard_map/ppermute | solution.py:32
  27.1 13.6 %copy-start.4 = (bf16[16]{0:T(256)(128)(2,1)S(1)}, bf16[16]{0:T(256)(128)(2,1)}, u32[]{:S(2)}) copy-start(bf16[16]{0:T(256)(128)(2,1)} %pad.43.clone) | copy-start | bytes 100
  40.9 2.8 %copy-start = (bf16[16,8,48,512]{3,2,1,0:T(8,128)(2,1)S(1)}, bf16[16,8,48,512]{3,2,1,0:T(8,128)(2,1)}, u32[]{:S(2)}) copy-start(bf16[16,8,48,512]{3,2,1,0:T(8,128)(2,1)} %v_hbm.1) | copy-start | bytes 18874372
  70.8 7.0 %collective-permute-start.6 = (f32[2,4,4,8,1024]{4,3,2,1,0:T(8,128)S(1)}, f32[2,4,4,8,1024]{4,3,2,1,0:T(8,128)}, u32[]{:S(2)}, u32[]{:S(2)}) collective-permute-start(f32[2,4,4,8,1024]{4,3,2,1,0:T(8,128)S(1)} %dynamic-slice_bitcast_fusion), channel_id=1, source_target_pairs={{0,32},{1,33},{2,34},{3,35},{4,36},{5,37},{6,38},{7,39},{8,40},{9,... | collective-permute-start | bytes 3145736 | tf_op jit(solution)/shard_map/ppermute | solution.py:32
  79.2 14.3 %collective-permute-start.7 = (f32[4,4,8,1024]{3,2,1,0:T(8,128)S(1)}, f32[4,4,8,1024]{3,2,1,0:T(8,128)S(1)}, u32[]{:S(2)}, u32[]{:S(2)}) collective-permute-start(f32[4,4,8,1024]{3,2,1,0:T(8,128)S(1)} %dynamic-slice_bitcast_fusion.2), channel_id=1, source_target_pairs={{0,64},{1,65},{2,66},{3,67},{4,68},{5,69},{6,70},{7,71},{8,72},{9,... | collective-permute-start | bytes 1572872 | tf_op jit(solution)/shard_map/ppermute | solution.py:32
  93.6 10.1 %collective-permute-start.10 = (f32[4,8,1024]{2,1,0:T(8,128)S(1)}, f32[4,8,1024]{2,1,0:T(8,128)S(1)}, u32[]{:S(2)}, u32[]{:S(2)}) collective-permute-start(f32[4,8,1024]{2,1,0:T(8,128)S(1)} %get-tuple-element.5), channel_id=1, source_target_pairs={{0,24},{1,25},{2,26},{3,27},{4,28},{5,29},{6,30},{7,31},{8,0},{9,1... | collective-permute-start | bytes 393224 | tf_op jit(solution)/shard_map/ppermute | solution.py:32
  101.2 8.7 %collective-permute-start.8 = (f32[4,8,1024]{2,1,0:T(8,128)S(1)}, f32[4,8,1024]{2,1,0:T(8,128)S(1)}, u32[]{:S(2)}, u32[]{:S(2)}) collective-permute-start(f32[4,8,1024]{2,1,0:T(8,128)S(1)} %get-tuple-element.4), channel_id=1, source_target_pairs={{0,8},{1,9},{2,10},{3,11},{4,12},{5,13},{6,14},{7,15},{8,16},{9,17... | collective-permute-start | bytes 393224 | tf_op jit(solution)/shard_map/ppermute | solution.py:32
  101.2 8.7 %collective-permute-start.9 = (f32[4,8,1024]{2,1,0:T(8,128)S(1)}, f32[4,8,1024]{2,1,0:T(8,128)S(1)}, u32[]{:S(2)}, u32[]{:S(2)}) collective-permute-start(f32[4,8,1024]{2,1,0:T(8,128)S(1)} %get-tuple-element.6), channel_id=1, source_target_pairs={{0,16},{1,17},{2,18},{3,19},{4,20},{5,21},{6,22},{7,23},{8,24},{9,... | collective-permute-start | bytes 393224 | tf_op jit(solution)/shard_map/ppermute | solution.py:32
  109.9 5.2 %collective-permute-start.11 = (f32[8,1024]{1,0:T(8,128)S(1)}, f32[8,1024]{1,0:T(8,128)S(1)}, u32[]{:S(2)}, u32[]{:S(2)}) collective-permute-start(f32[8,1024]{1,0:T(8,128)S(1)} %get-tuple-element.7), channel_id=1, source_target_pairs={{0,2},{1,3},{2,4},{3,5},{4,6},{5,7},{6,0},{7,1},{8,10},{9,11},{10,... | collective-permute-start | bytes 98312 | tf_op jit(solution)/shard_map/ppermute | solution.py:32
  110.0 5.5 %collective-permute-start.12 = (f32[8,1024]{1,0:T(8,128)S(1)}, f32[8,1024]{1,0:T(8,128)S(1)}, u32[]{:S(2)}, u32[]{:S(2)}) collective-permute-start(f32[8,1024]{1,0:T(8,128)S(1)} %get-tuple-element.9), channel_id=1, source_target_pairs={{0,4},{1,5},{2,6},{3,7},{4,0},{5,1},{6,2},{7,3},{8,12},{9,13},{10,... | collective-permute-start | bytes 98312 | tf_op jit(solution)/shard_map/ppermute | solution.py:32
  112.8 3.9 %collective-permute-start.13 = (f32[8,1024]{1,0:T(8,128)S(1)}, f32[8,1024]{1,0:T(8,128)S(1)}, u32[]{:S(2)}, u32[]{:S(2)}) collective-permute-start(f32[8,1024]{1,0:T(8,128)S(1)} %get-tuple-element.8), channel_id=1, source_target_pairs={{0,6},{1,7},{2,0},{3,1},{4,2},{5,3},{6,4},{7,5},{8,14},{9,15},{10,... | collective-permute-start | bytes 98312 | tf_op jit(solution)/shard_map/ppermute | solution.py:32
  116.8 5.4 %collective-permute-start.14 = (f32[4,1024]{1,0:T(4,128)S(1)}, f32[4,1024]{1,0:T(4,128)S(1)}, u32[]{:S(2)}, u32[]{:S(2)}) collective-permute-start(f32[4,1024]{1,0:T(4,128)S(1)} %dynamic-slice_bitcast_fusion.9), channel_id=1, source_target_pairs={{0,1},{1,0},{2,3},{3,2},{4,5},{5,4},{6,7},{7,6},{8,9},{9,8},{10,11... | collective-permute-start | bytes 49160 | tf_op jit(solution)/shard_map/ppermute | solution.py:32

commit v2 on v0

v2 whole, which is shorter than its diff:
```python
import jax
import jax.numpy as jnp
from jax import lax
from jax.experimental import pallas as pl
from jax.experimental.pallas import tpu as pltpu
from jax.sharding import PartitionSpec as P

ALL = ("gx", "gy", "gz")
NGX, NGY, NGZ = 4, 16, 2
SX, SY, SZ, K = 16, 8, 48, 512
NEAR = (((0, 1, 2, 3), (0, 1, 2)), ((2, 3, 4, 5, 6), (3, 4, 5)), ((5, 6, 7), (6,)))
EDGE = ((6, 7, 8), (7, 8))
INNER = 7 * SZ
OUTER = 2 * SZ
BATCH = 3


def linear(x, y, z):
    return (x * NGY + y) * NGZ + z


def send(value, move):
    links = []
    for x in range(NGX):
        for y in range(NGY):
            for z in range(NGZ):
                to = move(x, y, z)
                if 0 <= to[0] < NGX and 0 <= to[1] < NGY and 0 <= to[2] < NGZ:
                    links.append((linear(x, y, z), linear(*to)))
    return lax.ppermute(value, ALL, links)


def to_z(x, y, z):
    return (x, y, 1 - z)


def to_x(x, y, z):
    return (x - 1, y, z)


def to_y(x, y, z):
    return (x, y + 1, z) if x % 2 else (x, y - 1, z)


def band_matrix(lines_in, lines_out, upper):
    size = len(lines_out) * SZ
    wide = len(lines_in) * SZ + 16
    row = lax.broadcasted_iota(jnp.int32, (2 * size, wide), 0)
    col = lax.broadcasted_iota(jnp.int32, (2 * size, wide), 1)
    mid = jnp.where(row < size, 2.0, 4.0)
    cell = row % size
    line_out = lines_out[0] + cell // SZ
    halo = col >= len(lines_in) * SZ
    line_in = jnp.where(halo, col - len(lines_in) * SZ, lines_in[0] + col // SZ)
    z_in = jnp.where(halo, jnp.where(upper, -1, SZ), col % SZ)
    z_gap = jnp.abs(cell % SZ - z_in)
    z_part = jnp.where(z_gap == 0, mid, jnp.where(z_gap == 1, 1.0, 0.0))
    y_gap = jnp.abs(line_out - line_in)
    y_part = jnp.where((y_gap == 0) & (line_out != 8), mid, jnp.where(y_gap == 1, 1.0, 0.0))
    return (y_part * z_part).astype(jnp.bfloat16)


def apply_band(band, lines, ztile, size):
    block = jnp.concatenate(lines + [ztile], axis=0)
    r = jnp.dot(band, block, preferred_element_type=jnp.float32)
    return r[:size], r[size:]


def kappa_yz(kappa, lines):
    f = 2.0 * kappa + pltpu.roll(kappa, 1, 1) + pltpu.roll(kappa, 127, 1)
    rows = lax.broadcasted_iota(jnp.int32, f.shape, 0)
    below = jnp.where(rows == 0, 0.0, pltpu.roll(f, 1, 0))
    above = jnp.where(rows == f.shape[0] - 1, 0.0, pltpu.roll(f, f.shape[0] - 1, 0))
    mid = jnp.where(rows == 8, 0.0, 2.0 * f)
    return mid + below + above


def weights(kappa, rho, f, plane_own):
    own = 2.0 * kappa if plane_own else jnp.zeros_like(kappa)
    rows = lax.broadcasted_iota(jnp.int32, f.shape, 0)
    alpha = jnp.where(rows == 8, 0.0, own) + f * (1.0 / 32.0)
    return jnp.concatenate([alpha, kappa * (1.0 / 16.0), rho * (1.0 / 216.0)], axis=0).T[:SZ]


def store_products(u, row, v, w3, t3, c, line, stride):
    wide = (SZ, K)
    alpha = jnp.broadcast_to(c[:, line : line + 1], wide)
    kap = jnp.broadcast_to(c[:, stride + line : stride + line + 1], wide)
    rho = jnp.broadcast_to(c[:, 2 * stride + line : 2 * stride + line + 1], wide)
    u[row : row + SZ, 0:K] = (alpha * v.astype(jnp.float32) - kap * w3).astype(jnp.bfloat16)
    u[row : row + SZ, K : 2 * K] = (rho * t3).astype(jnp.bfloat16)


def gram(left, right):
    return lax.dot_general(left, right, (((0,), (0,)), ((), ())), preferred_element_type=jnp.float32)


def line_index(odd, c):
    return c + odd * (7 - 2 * c)


def inner_kernel(odd_ref, v_hbm, zt_ref, mat_ref, band0, band1, band2, out_ref, ve, w2, t2, u, sem):
    odd = odd_ref[0]
    bands = (band0, band1, band2)
    cuts = ((0, 2), (2, 4), (4, 7), (7, 10), (10, 13), (13, 16))
    loads = []
    for n, (a, b) in enumerate(cuts):
        loads.append(
            [
                pltpu.make_async_copy(
                    v_hbm.at[pl.ds(a, b - a), line_index(odd, c)], ve.at[pl.ds(a, b - a), c], sem.at[n, c]
                )
                for c in range(8)
            ]
        )
        for load in loads[-1]:
            load.start()

    def arrive(n):
        for load in loads[n]:
            load.wait()

    def filter_plane(p):
        slot = p % 4
        for g, (ins, outs) in enumerate(NEAR):
            size = len(outs) * SZ
            a, b = apply_band(bands[g][...], [ve[p, l] for l in ins], zt_ref[p], size)
            w2[slot, outs[0] * SZ : outs[0] * SZ + size] = a
            t2[slot, outs[0] * SZ : outs[0] * SZ + size] = b

    yz = {}

    def kappa_of(p):
        if p not in yz:
            yz[p] = kappa_yz(mat_ref[0, p], 8)
        return yz[p]

    def make_products(p, buf, base):
        f = 2.0 * kappa_of(p) + kappa_of(p + 1)
        if p:
            f = f + kappa_of(p - 1)
        c = weights(mat_ref[0, p], mat_ref[1, p], f, True)
        for l in range(7):
            rows = slice(l * SZ, (l + 1) * SZ)
            mid = w2[p % 4, rows]
            w3 = (mid + mid) + w2[(p + 1) % 4, rows]
            t3 = 4.0 * t2[p % 4, rows] + t2[(p + 1) % 4, rows]
            if p:
                w3 = w3 + w2[(p - 1) % 4, rows]
                t3 = t3 + t2[(p - 1) % 4, rows]
            store_products(u.at[buf], base + l * SZ, ve[p, l], w3, t3, c, l, 8)

    arrive(0)
    filter_plane(0)
    for k in range(5):
        arrive(k + 1)
        if k == 0:
            filter_plane(1)
        for q in range(BATCH):
            p = BATCH * k + q
            if p + 1 > 1:
                filter_plane(p + 1)
            make_products(p, k % 2, q * INNER)
        left = jnp.concatenate([ve[BATCH * k + q, 0:7].reshape(INNER, K) for q in range(BATCH)], axis=0)
        m = gram(left, u[k % 2])
        if k == 0:
            out_ref[...] = m
        else:
            out_ref[...] += m


def tile_row(x, y, z_lo, core):
    a = {0: (0, 0), 3: (0, 1), 1: (1, 0), 2: (1, 1)}
    xa, xb = a[x]
    ya, yb = a[y]
    bits = (z_lo, xa, xb, ya, yb) if core == 0 else (xa, z_lo, ya, xb, yb)
    at = core
    for bit in bits:
        at = at * 2 + bit
    return at * 8


def outer_kernel(
    odd_ref, m_ref, v_hbm, xh_hbm, ym_hbm, ye_hbm, zt_ref, mat_ref, band0, band1, band2, band3, out_ref,
    v6, v78, v14, v15, v16, w78, t78, w06, t06, u, sem,
):
    odd = odd_ref[0]
    bands = (band0, band1, band2)
    loads = [
        pltpu.make_async_copy(v_hbm.at[pl.ds(0, 15), line_index(odd, 6)], v6, sem.at[0]),
        pltpu.make_async_copy(v_hbm.at[pl.ds(0, 15), line_index(odd, 7)], v78.at[:, 0], sem.at[1]),
        pltpu.make_async_copy(ym_hbm.at[pl.ds(0, 15)], v78.at[:, 1], sem.at[2]),
        pltpu.make_async_copy(ym_hbm.at[15], v15.at[8], sem.at[3]),
        pltpu.make_async_copy(ye_hbm.at[pl.ds(0, SZ)], v16.at[8], sem.at[4]),
    ]
    for c in range(8):
        loads.append(pltpu.make_async_copy(v_hbm.at[15, line_index(odd, c)], v15.at[c], sem.at[5 + c]))
        loads.append(pltpu.make_async_copy(xh_hbm.at[line_index(odd, c)], v16.at[c], sem.at[13 + c]))
        if c < 6:
            loads.append(pltpu.make_async_copy(v_hbm.at[14, line_index(odd, c)], v14.at[c], sem.at[21 + c]))
    for load in loads:
        load.start()
    for load in loads:
        load.wait()

    def line(p, l):
        if p == 15:
            return v15[l]
        if p == 16:
            return v16[l]
        if l >= 7:
            return v78[p, l - 7]
        if l == 6:
            return v6[p]
        return v14[l]

    def filter_near(p):
        for g, (ins, outs) in enumerate(NEAR):
            size = len(outs) * SZ
            a, b = apply_band(bands[g][...], [line(p, l) for l in ins], zt_ref[p], size)
            w06[p - 14, outs[0] * SZ : outs[0] * SZ + size] = a
            t06[p - 14, outs[0] * SZ : outs[0] * SZ + size] = b

    def filter_edge(p):
        a, b = apply_band(band3[...], [line(p, l) for l in EDGE[0]], zt_ref[p], OUTER)
        w78[p] = a
        t78[p] = b

    def along_x(ref, p, lo, hi, rows, mid):
        if p == hi:
            return ref[p - 1 - lo, rows]
        r = mid * ref[p - lo, rows] + ref[p + 1 - lo, rows]
        if p > 0:
            r = r + ref[p - 1 - lo, rows]
        return r

    yz = [kappa_yz(mat_ref[0, p], 16) for p in range(17)]
    for p in range(17):
        filter_edge(p)
        if p >= 14:
            filter_near(p)
    for p in range(17):
        if p == 16:
            f = yz[15]
        else:
            f = 2.0 * yz[p] + yz[p + 1]
            if p:
                f = f + yz[p - 1]
        c = weights(mat_ref[0, p], mat_ref[1, p], f, p != 16)
        for l in range(0 if p >= 15 else 7, 9):
            if p < 15:
                row = p * OUTER + (l - 7) * SZ
            else:
                row = 15 * OUTER + (p - 15) * 9 * SZ + l * SZ
            if l >= 7:
                rows = slice((l - 7) * SZ, (l - 6) * SZ)
                w3 = along_x(w78, p, 0, 16, rows, 2.0)
                t3 = along_x(t78, p, 0, 16, rows, 4.0)
            else:
                rows = slice(l * SZ, (l + 1) * SZ)
                w3 = along_x(w06, p, 14, 16, rows, 2.0)
                t3 = along_x(t06, p, 14, 16, rows, 4.0)
            store_products(u, row, line(p, l), w3, t3, c, l, 16)
    left = jnp.concatenate(
        [v78[...].reshape(15 * OUTER, K), v15[...].reshape(9 * SZ, K), v16[...].reshape(9 * SZ, K)], axis=0
    )
    m_ref[...] += gram(left, u[...])

    def put(i, j, half, s):
        for x in range(4):
            for y in range(4):
                t = (x * 4 + y) * 8
                at = tile_row(x, y, i // 2, i % 2)
                out_ref[at : at + 8, half * K + j * 128 : half * K + (j + 1) * 128] = s[t : t + 8]

    for half in range(2):
        for i in range(4):
            for j in range(i, 4):
                a = m_ref[i * 128 : (i + 1) * 128, half * K + j * 128 : half * K + (j + 1) * 128]
                b = m_ref[j * 128 : (j + 1) * 128, half * K + i * 128 : half * K + (i + 1) * 128]
                s = a + b.T
                put(i, j, half, s)
                if i != j:
                    put(j, i, half, s.T)


HBM = pl.BlockSpec(memory_space=pl.ANY)
VMEM = pl.BlockSpec(memory_space=pltpu.VMEM)
SMEM = pl.BlockSpec(memory_space=pltpu.SMEM)


def inner_part(odd, v, zt, mat, bands):
    return pl.pallas_call(
        inner_kernel,
        out_shape=jax.ShapeDtypeStruct((K, 2 * K), jnp.float32),
        in_specs=[SMEM, HBM, VMEM, VMEM, VMEM, VMEM, VMEM],
        out_specs=VMEM,
        scratch_shapes=[
            pltpu.VMEM((SX, SY, SZ, K), jnp.bfloat16),
            pltpu.VMEM((4, INNER, K), jnp.float32),
            pltpu.VMEM((4, INNER, K), jnp.float32),
            pltpu.VMEM((2, BATCH * INNER, 2 * K), jnp.bfloat16),
            pltpu.SemaphoreType.DMA((6, 8)),
        ],
        compiler_params=pltpu.CompilerParams(vmem_limit_bytes=36 * 1024 * 1024),
        cost_estimate=pl.CostEstimate(flops=9_000_000_000, transcendentals=0, bytes_accessed=10_000_000),
        name="inner",
    )(odd, v, zt, mat, *bands)


def outer_part(odd, m, v, xh, ym, ye, zt, mat, bands):
    return pl.pallas_call(
        outer_entry,
        out_shape=jax.ShapeDtypeStruct((K, 2 * K), jnp.float32),
        in_specs=[SMEM, VMEM, HBM, HBM, HBM, HBM, VMEM, VMEM, VMEM, VMEM, VMEM, VMEM],
        out_specs=VMEM,
        scratch_shapes=[
            pltpu.VMEM((15, SZ, K), jnp.bfloat16),
            pltpu.VMEM((15, 2, SZ, K), jnp.bfloat16),
            pltpu.VMEM((6, SZ, K), jnp.bfloat16),
            pltpu.VMEM((9, SZ, K), jnp.bfloat16),
            pltpu.VMEM((9, SZ, K), jnp.bfloat16),
            pltpu.VMEM((17, OUTER, K), jnp.float32),
            pltpu.VMEM((17, OUTER, K), jnp.float32),
            pltpu.VMEM((3, INNER, K), jnp.float32),
            pltpu.VMEM((3, INNER, K), jnp.float32),
            pltpu.VMEM((15 * OUTER + 18 * SZ, 2 * K), jnp.bfloat16),
            pltpu.SemaphoreType.DMA((27,)),
            pltpu.VMEM((K, 2 * K), jnp.float32),
        ],
        compiler_params=pltpu.CompilerParams(vmem_limit_bytes=48 * 1024 * 1024),
        cost_estimate=pl.CostEstimate(flops=4_000_000_000, transcendentals=0, bytes_accessed=6_000_000),
        name="outer",
    )(odd, m, v, xh, ym, ye, zt, mat, *bands)


def outer_entry(odd_ref, m_in, *rest):
    *rest, acc = rest
    acc[...] = m_in[...]
    outer_kernel(odd_ref, acc, *rest)


def pick(x, index, dim):
    return lax.dynamic_index_in_dim(x, index, dim, keepdims=False)


def reduce_to_owner(part):
    ix = lax.axis_index("gx")
    iy = lax.axis_index("gy")
    core = ix % 2
    z_lo = ix // 2
    z_hi = lax.axis_index("gz")

    def bits(r):
        return ((r == 1) | (r == 2)).astype(jnp.int32), (r >= 2).astype(jnp.int32)

    def flip_z(x, y, z):
        return (x ^ 2, y, z)

    def flip_xa(x, y, z):
        return (x, (y // 4 ^ 1) * 4 + y % 4, z)

    def flip_xb(x, y, z):
        return (x, (3 - y // 4) * 4 + y % 4, z)

    def flip_ya(x, y, z):
        return (x, y ^ 1, z)

    def flip_yb(x, y, z):
        return (x, y // 4 * 4 + 3 - y % 4, z)

    xa, xb = bits(iy // 4)
    ya, yb = bits(iy % 4)
    stages = (
        (core, core, lambda x, y, z: (x ^ 1, y, z), lambda x, y, z: (x ^ 1, y, z)),
        (z_lo, xa, flip_z, flip_xa),
        (xa, z_lo, flip_xa, flip_z),
        (xb, ya, flip_xb, flip_ya),
        (ya, xb, flip_ya, flip_xb),
        (yb, yb, flip_yb, flip_yb),
    )
    v = part
    for even_bit, odd_bit, even_move, odd_move in stages:
        bit = jnp.where(core == 0, even_bit, odd_bit)
        v = v.reshape(2, v.shape[0] // 2, 2 * K)
        v = pick(v, bit, 0) + send(
            pick(v, 1 - bit, 0),
            lambda x, y, z, e=even_move, o=odd_move: o(x, y, z) if x % 2 else e(x, y, z),
        )
    v = v.reshape(2, 4, 2 * K)
    return pick(v, z_hi, 0) + send(pick(v, 1 - z_hi, 0), to_z)


def per_device(eigvecs, material):
    odd = lax.axis_index("gx") % 2 == 1
    upper = lax.axis_index("gz") == 1
    side = jnp.where(odd, SY - 1, 0)
    odd_flag = odd.astype(jnp.int32).reshape(1)

    def chain(x, dim):
        return jnp.where(odd, lax.rev(x, (dim,)), x)

    ym = send(pick(eigvecs, side, 1), to_y)
    face = jnp.where(upper, 0, SZ - 1)
    kz = send(pick(material[0], face, 2), to_z)
    zh = send(pick(eigvecs, face, 2), to_z)
    lanes = jnp.arange(128)
    halo_lane = jnp.where(upper, 127, SZ)
    own = jnp.pad(material, ((0, 0), (0, 0), (0, 0), (0, 128 - SZ)))
    kap = jnp.where(lanes == halo_lane, kz[..., None], own[0])
    mat = jnp.stack([kap, own[1]])
    mx = send(mat[:, 0], to_x)
    vx = send(jnp.concatenate([eigvecs[0].reshape(SY * SZ, K), zh[0]], axis=0), to_x)
    zt = jnp.pad(chain(zh, 1), ((0, 0), (0, 16 - SY), (0, 0)))
    bands = [band_matrix(ins, outs, upper) for ins, outs in NEAR]
    edge_band = band_matrix(*EDGE, upper)
    m = inner_part(odd_flag, eigvecs, zt, chain(mat, 2), bands)
    xh = vx[: SY * SZ].reshape(SY, SZ, K)
    xz = vx[SY * SZ :]
    mat = chain(jnp.concatenate([mat, mx[:, None]], axis=1), 2)
    zrows = chain(jnp.concatenate([zh, xz[None]], axis=0), 1)
    my = send(mat[:, :, 0], to_y)
    ye = send(jnp.concatenate([pick(xh, side, 0), zrows[:, 0]], axis=0), to_y)
    mat = jnp.pad(jnp.concatenate([mat, my[:, :, None]], axis=2), ((0, 0), (0, 0), (0, 7), (0, 0)))
    zt = jnp.pad(jnp.concatenate([zrows, ye[SZ:][:, None]], axis=1), ((0, 0), (0, 7), (0, 0)))
    part = outer_part(odd_flag, m, eigvecs, xh, ym, ye, zt, mat, bands + [edge_band])
    total = SX * SY * SZ * NGX * NGY * NGZ
    summed = reduce_to_owner(part) * (0.5 / total)
    return summed[:, :K], summed[:, K:]


def solution(mesh):
    return jax.shard_map(
        per_device,
        mesh=mesh,
        in_specs=(P("gx", "gy", "gz", None), P(None, "gx", "gy", "gz")),
        out_specs=(P(ALL, None), P(ALL, None)),
        check_vma=False,
    )
```

time: 279 us -> 112 us (0.40)
  other arithmetic: 116 us -> 4.07 us
  blocking collectives: 61.6 us -> 0 us
  Pallas kernels: 0 us -> 24.4 us
  waiting for transfers between devices: 20.8 us -> 37 us
  matrix products: 15.2 us -> 0 us
  local copies, waits for them, and re-layouts: 23 us -> 13.2 us
  starting transfers between devices: 37 us -> 31.5 us
  loops' own time: 3.05 us -> 0 us
    all_to_all x3 -> x0, blocking collectives: 61.6 us -> none  [sum_at_owner(): parts = lax.all_to_all(split_up(x, dim, devices), axis, 0, 0, tiled=True)]
    add x37 -> x5, other arithmetic: 42.4 us -> 1.48 us  [reduce_to_owner(): pick(v, bit, 0)]
    convert_element_type x12 -> x4, other arithmetic: 34.9 us -> 1.32 us  [band_matrix(): return (y_part * z_part).astype(jnp.bfloat16)]
    pallas_call x0 -> x2, Pallas kernels: none -> 24.4 us  [the longest x1 15.5 us: inner_part(): pl.pallas_call(inner_kernel, out_shape=jax.ShapeDtypeStruct((K, 2 * K), j...]
    mul x12 -> x1, other arithmetic: 24 us -> 0.01 us  [per_device(): summed = reduce_to_owner(part) * (0.5 / total)]
    ppermute x12 -> x14, waiting for transfers between devices: 20.8 us -> 37 us  [send(): return lax.ppermute(value, ALL, links)]
    dot_general x2 -> x0, matrix products: 15.2 us -> none  [the longest x1 7.74 us: per_device(): jnp.einsum('cp,bcq->pbq', flat_vectors, stiff_blocks, preferred_element_t...]
    concatenate x4 -> x6, other arithmetic: 11 us -> 0.89 us  [the longest x1 0.77 us: per_device(): jnp.concatenate([eigvecs[0].reshape(SY * SZ, K), zh[0]], axis=0)]
  transfers between devices with their start and end apart: 12 -> 14, of which waited for: 6 -> 11; matrix products, arithmetic and copies ran while one was open for 3% -> 6% of each run, Pallas kernels for 0% -> 14%
where the time goes in v2:
time: 112 us; the launch traced here: 111 us
  waiting for transfers between devices  37 us (33%)
  starting transfers between devices  31.5 us (28%)
  Pallas kernels  24.4 us (22%)
  local copies, waits for them, and re-layouts  13.2 us (12%)
  other arithmetic  4.07 us (4%)
  between operations  1.28 us (1%)
    ppermute x14, waiting for transfers between devices, send(): return lax.ppermute(value, ALL, links)  37 us
    ppermute x14, starting transfers between devices, send(): return lax.ppermute(value, ALL, links)  31.5 us
    pallas_call x1, Pallas kernels, inner_part(): pl.pallas_call(inner_kernel, out_shape=jax.ShapeDtypeStruct((K, 2 * K), j...  15.5 us
    pallas_call x1, Pallas kernels, outer_part(): pl.pallas_call(outer_entry, out_shape=jax.ShapeDtypeStruct((K, 2 * K), jn...  8.91 us
    unnamed x13, local copies, waits for them, and re-layouts  6.29 us
  transfers between devices with their start and end apart: 14, of which 11 were waited for; matrix products, arithmetic and copies ran while one was open for 6% of the time, Pallas kernels for 14%

profile of v2, /device:TPU:0, one launch (start us, length us, event | category | flops | bytes accessed | tf_op | source)
XLA Modules:
  0.0 111.5 jit_solution(14670831373032400690)
XLA Ops:
  0.6 1.6 %constant_dynamic-slice_fusion.1 = bf16[16,8,1,512]{3,2,1,0:T(2,128)(2,1)S(1)} fusion(bf16[16,8,48,512]{3,2,1,0:T(8,128)(2,1)} %rest_0_.1, s32[]{:T(128)S(6)} %select_n.350), kind=kLoop, calls=%fused_computation.110 | loop fusion | bytes 262148 | tf_op jit(solution)/shard_map/jit(dynamic_index_in_dim)/dynamic_slice | solution.py:344
  2.3 4.1 %collective-permute-start = (bf16[16,8,512]{2,1,0:T(8,128)(2,1)S(1)}, bf16[16,8,512]{2,1,0:T(8,128)(2,1)S(1)}, u32[]{:S(2)}, u32[]{:S(2)}) collective-permute-start(bf16[16,8,512]{2,1,0:T(8,128)(2,1)S(1)} %bitcast.79), channel_id=1, source_target_pairs={{0,1},{1,0},{2,3},{3,2},{4,5},{5,4},{6,7},{7,6},{8,9},{9,8},{10,11... | collective-permute-start | bytes 393224 | tf_op jit(solution)/shard_map/ppermute | solution.py:30
  6.3 0.8 slice.39
  7.2 0.1 constant_dynamic-slice_fusion
  7.3 0.1 copy.33
  7.5 1.3 %dynamic-slice_bitcast_fusion.1 = bf16[16,48,512]{2,1,0:T(8,128)(2,1)S(1)} fusion(bf16[16,8,48,512]{3,2,1,0:T(8,128)(2,1)} %rest_0_.1, s32[]{:T(128)S(6)} %select_n.392), kind=kLoop, calls=%fused_computation.2 | loop fusion | bytes 1572868 | tf_op jit(solution)/shard_map/jit(dynamic_index_in_dim)/squeeze | solution.py:344
  8.7 1.3 %collective-permute-start.3 = (bf16[16,48,512]{2,1,0:T(8,128)(2,1)S(1)}, bf16[16,48,512]{2,1,0:T(8,128)(2,1)S(1)}, u32[]{:S(2)}, u32[]{:S(2)}) collective-permute-start(bf16[16,48,512]{2,1,0:T(8,128)(2,1)S(1)} %dynamic-slice_bitcast_fusion.1), channel_id=1, source_target_pairs={{2,0},{3,1},{4,2},{5,3},{6,4},{7,5},{8,6},{9,7},{10,8},{11,9},{12,... | collective-permute-start | bytes 2359304 | tf_op jit(solution)/shard_map/ppermute | solution.py:30
  10.4 0.2 multiply_convert_fusion.3.band2.rest_8_
  10.6 0.3 multiply_convert_fusion.2.rest_9_
  10.9 0.4 multiply_convert_fusion.band1.rest_7_
  11.3 0.4 multiply_convert_fusion.1.band0.rest_6_
  11.7 0.8 collective-permute-done.1
  12.6 0.1 fusion.42
  12.7 1.3 %collective-permute-start.5 = (f32[2,8,128]{2,1,0:T(8,128)S(1)}, f32[2,8,128]{2,1,0:T(8,128)S(1)}, u32[]{:S(2)}, u32[]{:S(2)}) collective-permute-start(f32[2,8,128]{2,1,0:T(8,128)S(1)} %fusion.46), channel_id=1, source_target_pairs={{32,0},{33,1},{34,2},{35,3},{36,4},{37,5},{38,6},{39,7},{40,8},{41... | collective-permute-start | bytes 24584 | tf_op jit(solution)/shard_map/ppermute | solution.py:30
  14.1 1.9 %collective-permute-done.5 = f32[2,8,128]{2,1,0:T(8,128)S(1)} collective-permute-done((f32[2,8,128]{2,1,0:T(8,128)S(1)}, f32[2,8,128]{2,1,0:T(8,128)S(1)}, u32[]{:S(2)}, u32[]{:S(2)}) %collective-permute-start.5) | collective-permute-done | bytes 8224 | tf_op jit(solution)/shard_map/ppermute | solution.py:30
  16.1 1.3 %collective-permute-start.6 = (f32[2,17,128]{2,0,1:T(2,128)S(1)}, f32[2,17,128]{2,0,1:T(2,128)S(1)}, u32[]{:S(2)}, u32[]{:S(2)}) collective-permute-start(f32[2,17,128]{2,0,1:T(2,128)S(1)} %bitcast.83), channel_id=1, source_target_pairs={{2,0},{3,1},{4,2},{5,3},{6,4},{7,5},{8,6},{9,7},{10,8},{11,9},{12,... | collective-permute-start | bytes 52232 | tf_op jit(solution)/shard_map/ppermute | solution.py:30
  17.4 0.8 pad_maximum_fusion
  18.2 1.3 %collective-permute-start.2 = (bf16[392,512]{1,0:T(8,128)(2,1)}, bf16[392,512]{1,0:T(8,128)(2,1)}, u32[]{:S(2)}, u32[]{:S(2)}) collective-permute-start(bf16[392,512]{1,0:T(8,128)(2,1)} %pad_maximum_fusion), channel_id=1, source_target_pairs={{32,0},{33,1},{34,2},{35,3},{36,4},{37,5},{38,6},{39,7},{40,8},{41... | collective-permute-start | bytes 1204232 | tf_op jit(solution)/shard_map/ppermute | solution.py:30
  19.5 3.3 %collective-permute-done.6 = f32[2,17,128]{2,0,1:T(2,128)S(1)} collective-permute-done((f32[2,17,128]{2,0,1:T(2,128)S(1)}, f32[2,17,128]{2,0,1:T(2,128)S(1)}, u32[]{:S(2)}, u32[]{:S(2)}) %collective-permute-start.6) | collective-permute-done | bytes 17440 | tf_op jit(solution)/shard_map/ppermute | solution.py:30
  22.9 0.2 rev.12
  23.1 3.1 %collective-permute-done.2 = bf16[392,512]{1,0:T(8,128)(2,1)} collective-permute-done((bf16[392,512]{1,0:T(8,128)(2,1)}, bf16[392,512]{1,0:T(8,128)(2,1)}, u32[]{:S(2)}, u32[]{:S(2)}) %collective-permute-start.2) | collective-permute-done | bytes 401440 | tf_op jit(solution)/shard_map/ppermute | solution.py:30
  26.2 0.7 slice_bitcast_fusion.1
  26.9 0.2 rev.14
  27.2 1.0 slice.53
  28.3 1.5 %collective-permute-start.4 = (bf16[65,512]{1,0:T(8,128)(2,1)S(1)}, bf16[65,512]{1,0:T(8,128)(2,1)S(1)}, u32[]{:S(2)}, u32[]{:S(2)}) collective-permute-start(bf16[65,512]{1,0:T(8,128)(2,1)S(1)} %pad_maximum_fusion.4), channel_id=1, source_target_pairs={{2,0},{3,1},{4,2},{5,3},{6,4},{7,5},{8,6},{9,7},{10,8},{11,9},{12,... | collective-permute-start | bytes 199688 | tf_op jit(solution)/shard_map/ppermute | solution.py:30
  29.8 2.8 %copy-done = bf16[16,8,48,512]{3,2,1,0:T(8,128)(2,1)S(1)} copy-done((bf16[16,8,48,512]{3,2,1,0:T(8,128)(2,1)S(1)}, bf16[16,8,48,512]{3,2,1,0:T(8,128)(2,1)}, u32[]{:S(2)}) %copy-start) | copy-done | bytes 6291480
  32.5 15.5 %inner.1.m_in = f32[512,1024]{1,0:T(8,128)S(1)} custom-call(s32[1]{0:T(128)} %bitcast.odd_ref, bf16[16,8,48,512]{3,2,1,0:T(8,128)(2,1)S(1)} %copy-done, bf16[16,16,512]{2,1,0:T(8,128)(2,1)S(1)} %pad.16.zt_ref, f32[2,16,8,128]{3,2,1,0:T(8,128)S(1)} %copy.25.mat_ref, bf16[288,208]{1,0:T(8,128)(2,1)S(1)} %multiply_convert_fusion.1.band0.rest_6_, ...), custom_call_target="tpu_custom_call" | custom-call | flops 8999999488 | bytes 10000000 | tf_op jit(solution)/shard_map/inner/pallas_call | solution.py:293
  48.1 1.3 %copy-done.3 = f32[512,1024]{1,0:T(8,128)} copy-done((f32[512,1024]{1,0:T(8,128)}, f32[512,1024]{1,0:T(8,128)S(1)}, u32[]{:S(2)}) %copy-start.3) | copy-done | bytes 2097176
  49.5 0.9 copy-done.1
  50.4 1.1 %copy-done.2 = bf16[16,48,512]{2,1,0:T(8,128)(2,1)S(1)} copy-done((bf16[16,48,512]{2,1,0:T(8,128)(2,1)S(1)}, bf16[16,48,512]{2,1,0:T(8,128)(2,1)}, u32[]{:S(2)}) %copy-start.2) | copy-done | bytes 786456
  51.5 8.9 %outer.1 = f32[512,1024]{1,0:T(8,128)S(1)} custom-call(s32[1]{0:T(128)} %bitcast.odd_ref, f32[512,1024]{1,0:T(8,128)} %copy-done.3, bf16[16,8,48,512]{3,2,1,0:T(8,128)(2,1)} %rest_0_.1, bf16[8,48,512]{2,1,0:T(8,128)(2,1)S(1)} %bitcast.69, bf16[16,48,512]{2,1,0:T(8,128)(2,1)S(1)} %copy-done.2, bf16[65,512]{1,0:T(8,128)(2,1)S(1)} %collective-permute-done.4.rest_3_, ...), custom_call_target="tpu_custom_call" | custom-call | flops 4000000000 | bytes 6000000 | tf_op jit(solution)/shard_map/outer/pallas_call | solution.py:312
  60.4 0.1 dynamic-slice_bitcast_fusion
  60.6 7.7 %collective-permute-start.7 = (f32[256,1024]{1,0:T(8,128)S(1)}, f32[256,1024]{1,0:T(8,128)}, u32[]{:S(2)}, u32[]{:S(2)}) collective-permute-start(f32[256,1024]{1,0:T(8,128)S(1)} %dynamic-slice_bitcast_fusion), channel_id=1, source_target_pairs={{0,32},{1,33},{2,34},{3,35},{4,36},{5,37},{6,38},{7,39},{8,40},{9,... | collective-permute-start | bytes 3145736 | tf_op jit(solution)/shard_map/ppermute | solution.py:30
  68.3 2.4 %collective-permute-done.7 = f32[256,1024]{1,0:T(8,128)} collective-permute-done((f32[256,1024]{1,0:T(8,128)S(1)}, f32[256,1024]{1,0:T(8,128)}, u32[]{:S(2)}, u32[]{:S(2)}) %collective-permute-start.7) | collective-permute-done | bytes 1048608 | tf_op jit(solution)/shard_map/ppermute | solution.py:30
  70.7 1.4 %bitcast_add_fusion = f32[256,1024]{1,0:T(8,128)S(1)} fusion(f32[256,1024]{1,0:T(8,128)} %collective-permute-done.7, f32[2,256,1024]{2,1,0:T(8,128)S(1)} %bitcast.67, s32[]{:T(128)S(6)} %select_n.409), kind=kLoop, calls=%fused_computation | loop fusion | flops 262144 | bytes 3145732 | tf_op jit(solution)/shard_map/add | solution.py:386
  72.1 0.1 collective-permute-start.8
  72.2 9.1 %collective-permute-done.8 = f32[128,1024]{1,0:T(8,128)S(1)} collective-permute-done((f32[128,1024]{1,0:T(8,128)S(1)}, f32[128,1024]{1,0:T(8,128)S(1)}, u32[]{:S(2)}, u32[]{:S(2)}) %collective-permute-start.8) | collective-permute-done | bytes 524320 | tf_op jit(solution)/shard_map/ppermute | solution.py:30
  81.5 3.3 %collective-permute-start.9 = (f32[64,1024]{1,0:T(8,128)S(1)}, f32[64,1024]{1,0:T(8,128)S(1)}, u32[]{:S(2)}, u32[]{:S(2)}) collective-permute-start(f32[64,1024]{1,0:T(8,128)S(1)} %dynamic-slice_bitcast_fusion.3), channel_id=1, source_target_pairs={{0,8},{1,9},{2,10},{3,11},{4,12},{5,13},{6,14},{7,15},{8,0},{9,1},... | collective-permute-start | bytes 786440 | tf_op jit(solution)/shard_map/ppermute | solution.py:30
  84.8 4.4 %collective-permute-done.9 = f32[64,1024]{1,0:T(8,128)S(1)} collective-permute-done((f32[64,1024]{1,0:T(8,128)S(1)}, f32[64,1024]{1,0:T(8,128)S(1)}, u32[]{:S(2)}, u32[]{:S(2)}) %collective-permute-start.9) | collective-permute-done | bytes 262176 | tf_op jit(solution)/shard_map/ppermute | solution.py:30
  89.2 3.7 %collective-permute-start.10 = (f32[32,1024]{1,0:T(8,128)S(1)}, f32[32,1024]{1,0:T(8,128)S(1)}, u32[]{:S(2)}, u32[]{:S(2)}) collective-permute-start(f32[32,1024]{1,0:T(8,128)S(1)} %dynamic-slice_bitcast_fusion.4), channel_id=1, source_target_pairs={{0,24},{1,25},{2,26},{3,27},{4,28},{5,29},{6,30},{7,31},{8,16},{9,... | collective-permute-start | bytes 393224 | tf_op jit(solution)/shard_map/ppermute | solution.py:30
  92.8 2.9 %collective-permute-done.10 = f32[32,1024]{1,0:T(8,128)S(1)} collective-permute-done((f32[32,1024]{1,0:T(8,128)S(1)}, f32[32,1024]{1,0:T(8,128)S(1)}, u32[]{:S(2)}, u32[]{:S(2)}) %collective-permute-start.10) | collective-permute-done | bytes 131104 | tf_op jit(solution)/shard_map/ppermute | solution.py:30
  95.8 0.1 collective-permute-start.11
  95.9 4.2 %collective-permute-done.11 = f32[16,1024]{1,0:T(8,128)S(1)} collective-permute-done((f32[16,1024]{1,0:T(8,128)S(1)}, f32[16,1024]{1,0:T(8,128)S(1)}, u32[]{:S(2)}, u32[]{:S(2)}) %collective-permute-start.11) | collective-permute-done | bytes 65568 | tf_op jit(solution)/shard_map/ppermute | solution.py:30
  100.2 2.2 %collective-permute-start.12 = (f32[8,1024]{1,0:T(8,128)S(1)}, f32[8,1024]{1,0:T(8,128)S(1)}, u32[]{:S(2)}, u32[]{:S(2)}) collective-permute-start(f32[8,1024]{1,0:T(8,128)S(1)} %dynamic-slice_bitcast_fusion.7), channel_id=1, source_target_pairs={{0,6},{1,7},{2,4},{3,5},{4,2},{5,3},{6,0},{7,1},{8,14},{9,15},{10,... | collective-permute-start | bytes 98312 | tf_op jit(solution)/shard_map/ppermute | solution.py:30
  102.4 3.0 %collective-permute-done.12 = f32[8,1024]{1,0:T(8,128)S(1)} collective-permute-done((f32[8,1024]{1,0:T(8,128)S(1)}, f32[8,1024]{1,0:T(8,128)S(1)}, u32[]{:S(2)}, u32[]{:S(2)}) %collective-permute-start.12) | collective-permute-done | bytes 32800 | tf_op jit(solution)/shard_map/ppermute | solution.py:30
  105.5 3.7 %collective-permute-start.13 = (f32[4,1024]{1,0:T(4,128)S(1)}, f32[4,1024]{1,0:T(4,128)S(1)}, u32[]{:S(2)}, u32[]{:S(2)}) collective-permute-start(f32[4,1024]{1,0:T(4,128)S(1)} %dynamic-slice_bitcast_fusion.8), channel_id=1, source_target_pairs={{0,1},{1,0},{2,3},{3,2},{4,5},{5,4},{6,7},{7,6},{8,9},{9,8},{10,11... | collective-permute-start | bytes 49160 | tf_op jit(solution)/shard_map/ppermute | solution.py:30
  109.1 1.7 %collective-permute-done.13 = f32[4,1024]{1,0:T(4,128)S(1)} collective-permute-done((f32[4,1024]{1,0:T(4,128)S(1)}, f32[4,1024]{1,0:T(4,128)S(1)}, u32[]{:S(2)}, u32[]{:S(2)}) %collective-permute-start.13) | collective-permute-done | bytes 16416 | tf_op jit(solution)/shard_map/ppermute | solution.py:30
  110.8 0.6 fusion.59
  (76 shorter events, 1.1 us)
Async XLA Ops:
  0.6 12.0 %copy-start.4 = (f32[2,16,8,48]{3,2,1,0:T(8,128)S(1)}, f32[2,16,8,48]{3,2,1,0:T(8,128)}, u32[]{:S(2)}) copy-start(f32[2,16,8,48]{3,2,1,0:T(8,128)} %param.3) | copy-start | bytes 147460
  2.3 15.1 %collective-permute-start = (bf16[16,8,512]{2,1,0:T(8,128)(2,1)S(1)}, bf16[16,8,512]{2,1,0:T(8,128)(2,1)S(1)}, u32[]{:S(2)}, u32[]{:S(2)}) collective-permute-start(bf16[16,8,512]{2,1,0:T(8,128)(2,1)S(1)} %bitcast.79), channel_id=1, source_target_pairs={{0,1},{1,0},{2,3},{3,2},{4,5},{5,4},{6,7},{7,6},{8,9},{9,8},{10,11... | collective-permute-start | bytes 393224 | tf_op jit(solution)/shard_map/ppermute | solution.py:30
  7.4 5.2 %collective-permute-start.1 = (f32[16,8]{0,1:T(8,128)S(1)}, f32[16,8]{0,1:T(8,128)S(1)}, u32[]{:S(2)}, u32[]{:S(2)}) collective-permute-start(f32[16,8]{0,1:T(8,128)S(1)} %bitcast.85), channel_id=1, source_target_pairs={{0,1},{1,0},{2,3},{3,2},{4,5},{5,4},{6,7},{7,6},{8,9},{9,8},{10,11... | collective-permute-start | bytes 1544 | tf_op jit(solution)/shard_map/ppermute | solution.py:30
  7.5 10.0 %slice-start = ((bf16[16,8,48,512]{3,2,1,0:T(8,128)(2,1)}), bf16[1,8,48,512]{3,2,1,0:T(8,128)(2,1)S(1)}, s32[]{:S(2)}) async-start(bf16[16,8,48,512]{3,2,1,0:T(8,128)(2,1)} %rest_0_.1), calls=%async_computation | async-start | bytes 786432 | tf_op jit(solution)/shard_map/slice | solution.py:413
  8.7 40.8 %collective-permute-start.3 = (bf16[16,48,512]{2,1,0:T(8,128)(2,1)S(1)}, bf16[16,48,512]{2,1,0:T(8,128)(2,1)S(1)}, u32[]{:S(2)}, u32[]{:S(2)}) collective-permute-start(bf16[16,48,512]{2,1,0:T(8,128)(2,1)S(1)} %dynamic-slice_bitcast_fusion.1), channel_id=1, source_target_pairs={{2,0},{3,1},{4,2},{5,3},{6,4},{7,5},{8,6},{9,7},{10,8},{11,9},{12,... | collective-permute-start | bytes 2359304 | tf_op jit(solution)/shard_map/ppermute | solution.py:30
  12.7 3.3 %collective-permute-start.5 = (f32[2,8,128]{2,1,0:T(8,128)S(1)}, f32[2,8,128]{2,1,0:T(8,128)S(1)}, u32[]{:S(2)}, u32[]{:S(2)}) collective-permute-start(f32[2,8,128]{2,1,0:T(8,128)S(1)} %fusion.46), channel_id=1, source_target_pairs={{32,0},{33,1},{34,2},{35,3},{36,4},{37,5},{38,6},{39,7},{40,8},{41... | collective-permute-start | bytes 24584 | tf_op jit(solution)/shard_map/ppermute | solution.py:30
  16.1 6.7 %collective-permute-start.6 = (f32[2,17,128]{2,0,1:T(2,128)S(1)}, f32[2,17,128]{2,0,1:T(2,128)S(1)}, u32[]{:S(2)}, u32[]{:S(2)}) collective-permute-start(f32[2,17,128]{2,0,1:T(2,128)S(1)} %bitcast.83), channel_id=1, source_target_pairs={{2,0},{3,1},{4,2},{5,3},{6,4},{7,5},{8,6},{9,7},{10,8},{11,9},{12,... | collective-permute-start | bytes 52232 | tf_op jit(solution)/shard_map/ppermute | solution.py:30
  18.2 8.0 %collective-permute-start.2 = (bf16[392,512]{1,0:T(8,128)(2,1)}, bf16[392,512]{1,0:T(8,128)(2,1)}, u32[]{:S(2)}, u32[]{:S(2)}) collective-permute-start(bf16[392,512]{1,0:T(8,128)(2,1)} %pad_maximum_fusion), channel_id=1, source_target_pairs={{32,0},{33,1},{34,2},{35,3},{36,4},{37,5},{38,6},{39,7},{40,8},{41... | collective-permute-start | bytes 1204232 | tf_op jit(solution)/shard_map/ppermute | solution.py:30
  28.3 21.1 %collective-permute-start.4 = (bf16[65,512]{1,0:T(8,128)(2,1)S(1)}, bf16[65,512]{1,0:T(8,128)(2,1)S(1)}, u32[]{:S(2)}, u32[]{:S(2)}) collective-permute-start(bf16[65,512]{1,0:T(8,128)(2,1)S(1)} %pad_maximum_fusion.4), channel_id=1, source_target_pairs={{2,0},{3,1},{4,2},{5,3},{6,4},{7,5},{8,6},{9,7},{10,8},{11,9},{12,... | collective-permute-start | bytes 199688 | tf_op jit(solution)/shard_map/ppermute | solution.py:30
  29.7 2.8 %copy-start = (bf16[16,8,48,512]{3,2,1,0:T(8,128)(2,1)S(1)}, bf16[16,8,48,512]{3,2,1,0:T(8,128)(2,1)}, u32[]{:S(2)}) copy-start(bf16[16,8,48,512]{3,2,1,0:T(8,128)(2,1)} %rest_0_.1) | copy-start | bytes 18874372
  48.1 1.4 %copy-start.3 = (f32[512,1024]{1,0:T(8,128)}, f32[512,1024]{1,0:T(8,128)S(1)}, u32[]{:S(2)}) copy-start(f32[512,1024]{1,0:T(8,128)S(1)} %inner.1.m_in) | copy-start | bytes 6291460
  49.5 0.9 copy-start.1
  50.4 1.1 %copy-start.2 = (bf16[16,48,512]{2,1,0:T(8,128)(2,1)S(1)}, bf16[16,48,512]{2,1,0:T(8,128)(2,1)}, u32[]{:S(2)}) copy-start(bf16[16,48,512]{2,1,0:T(8,128)(2,1)} %copy-done.1) | copy-start | bytes 2359300
  60.6 10.1 %collective-permute-start.7 = (f32[256,1024]{1,0:T(8,128)S(1)}, f32[256,1024]{1,0:T(8,128)}, u32[]{:S(2)}, u32[]{:S(2)}) collective-permute-start(f32[256,1024]{1,0:T(8,128)S(1)} %dynamic-slice_bitcast_fusion), channel_id=1, source_target_pairs={{0,32},{1,33},{2,34},{3,35},{4,36},{5,37},{6,38},{7,39},{8,40},{9,... | collective-permute-start | bytes 3145736 | tf_op jit(solution)/shard_map/ppermute | solution.py:30
  72.1 9.3 %collective-permute-start.8 = (f32[128,1024]{1,0:T(8,128)S(1)}, f32[128,1024]{1,0:T(8,128)S(1)}, u32[]{:S(2)}, u32[]{:S(2)}) collective-permute-start(f32[128,1024]{1,0:T(8,128)S(1)} %dynamic-slice_bitcast_fusion.2), channel_id=1, source_target_pairs={{0,64},{1,65},{2,66},{3,67},{4,68},{5,69},{6,70},{7,71},{8,72},{9,... | collective-permute-start | bytes 1572872 | tf_op jit(solution)/shard_map/ppermute | solution.py:30
  81.5 7.6 %collective-permute-start.9 = (f32[64,1024]{1,0:T(8,128)S(1)}, f32[64,1024]{1,0:T(8,128)S(1)}, u32[]{:S(2)}, u32[]{:S(2)}) collective-permute-start(f32[64,1024]{1,0:T(8,128)S(1)} %dynamic-slice_bitcast_fusion.3), channel_id=1, source_target_pairs={{0,8},{1,9},{2,10},{3,11},{4,12},{5,13},{6,14},{7,15},{8,0},{9,1},... | collective-permute-start | bytes 786440 | tf_op jit(solution)/shard_map/ppermute | solution.py:30
  89.2 6.6 %collective-permute-start.10 = (f32[32,1024]{1,0:T(8,128)S(1)}, f32[32,1024]{1,0:T(8,128)S(1)}, u32[]{:S(2)}, u32[]{:S(2)}) collective-permute-start(f32[32,1024]{1,0:T(8,128)S(1)} %dynamic-slice_bitcast_fusion.4), channel_id=1, source_target_pairs={{0,24},{1,25},{2,26},{3,27},{4,28},{5,29},{6,30},{7,31},{8,16},{9,... | collective-permute-start | bytes 393224 | tf_op jit(solution)/shard_map/ppermute | solution.py:30
  95.8 4.3 %collective-permute-start.11 = (f32[16,1024]{1,0:T(8,128)S(1)}, f32[16,1024]{1,0:T(8,128)S(1)}, u32[]{:S(2)}, u32[]{:S(2)}) collective-permute-start(f32[16,1024]{1,0:T(8,128)S(1)} %dynamic-slice_bitcast_fusion.5), channel_id=1, source_target_pairs={{0,2},{1,3},{2,0},{3,1},{4,6},{5,7},{6,4},{7,5},{8,10},{9,11},{10,... | collective-permute-start | bytes 196616 | tf_op jit(solution)/shard_map/ppermute | solution.py:30
  100.2 5.2 %collective-permute-start.12 = (f32[8,1024]{1,0:T(8,128)S(1)}, f32[8,1024]{1,0:T(8,128)S(1)}, u32[]{:S(2)}, u32[]{:S(2)}) collective-permute-start(f32[8,1024]{1,0:T(8,128)S(1)} %dynamic-slice_bitcast_fusion.7), channel_id=1, source_target_pairs={{0,6},{1,7},{2,4},{3,5},{4,2},{5,3},{6,0},{7,1},{8,14},{9,15},{10,... | collective-permute-start | bytes 98312 | tf_op jit(solution)/shard_map/ppermute | solution.py:30
  105.5 5.4 %collective-permute-start.13 = (f32[4,1024]{1,0:T(4,128)S(1)}, f32[4,1024]{1,0:T(4,128)S(1)}, u32[]{:S(2)}, u32[]{:S(2)}) collective-permute-start(f32[4,1024]{1,0:T(4,128)S(1)} %dynamic-slice_bitcast_fusion.8), channel_id=1, source_target_pairs={{0,1},{1,0},{2,3},{3,2},{4,5},{5,4},{6,7},{7,6},{8,9},{9,8},{10,11... | collective-permute-start | bytes 49160 | tf_op jit(solution)/shard_map/ppermute | solution.py:30

commit v3 on v2

--- a/solution.py
+++ b/solution.py
@@ -13,6 +13,8 @@
 INNER = 7 * SZ
 OUTER = 2 * SZ
 BATCH = 3
+FACE = 224
+PIECES = ((0, 1), (1, 3), (3, 5))
 
 
 def linear(x, y, z):
@@ -42,31 +44,40 @@
     return (x, y + 1, z) if x % 2 else (x, y - 1, z)
 
 
-def band_matrix(lines_in, lines_out, upper):
+def chain_part(gap, ends, mid):
+    return jnp.where(gap == 0, jnp.where(ends, 0.0, mid), jnp.where(gap == 1, 1.0, 0.0))
+
+
+def band_matrix(lines_in, lines_out):
     size = len(lines_out) * SZ
-    wide = len(lines_in) * SZ + 16
-    row = lax.broadcasted_iota(jnp.int32, (2 * size, wide), 0)
-    col = lax.broadcasted_iota(jnp.int32, (2 * size, wide), 1)
+    row = lax.broadcasted_iota(jnp.int32, (2 * size, len(lines_in) * SZ), 0)
+    col = lax.broadcasted_iota(jnp.int32, (2 * size, len(lines_in) * SZ), 1)
     mid = jnp.where(row < size, 2.0, 4.0)
     cell = row % size
     line_out = lines_out[0] + cell // SZ
-    halo = col >= len(lines_in) * SZ
-    line_in = jnp.where(halo, col - len(lines_in) * SZ, lines_in[0] + col // SZ)
-    z_in = jnp.where(halo, jnp.where(upper, -1, SZ), col % SZ)
-    z_gap = jnp.abs(cell % SZ - z_in)
-    z_part = jnp.where(z_gap == 0, mid, jnp.where(z_gap == 1, 1.0, 0.0))
-    y_gap = jnp.abs(line_out - line_in)
-    y_part = jnp.where((y_gap == 0) & (line_out != 8), mid, jnp.where(y_gap == 1, 1.0, 0.0))
+    line_in = lines_in[0] + col // SZ
+    z_part = chain_part(jnp.abs(cell % SZ - col % SZ), False, mid)
+    y_part = chain_part(jnp.abs(line_out - line_in), line_out == 8, mid)
     return (y_part * z_part).astype(jnp.bfloat16)
 
 
-def apply_band(band, lines, ztile, size):
-    block = jnp.concatenate(lines + [ztile], axis=0)
-    r = jnp.dot(band, block, preferred_element_type=jnp.float32)
+def face_matrix():
+    row = lax.broadcasted_iota(jnp.int32, (2 * FACE, FACE), 0)
+    col = lax.broadcasted_iota(jnp.int32, (2 * FACE, FACE), 1)
+    mid = jnp.where(row < FACE, 2.0, 4.0)
+    cell = row % FACE
+    x_part = chain_part(jnp.abs(cell % 24 - col % 24), cell % 24 == SX, mid)
+    y_part = chain_part(jnp.abs(cell // 24 - col // 24), cell // 24 == SY, mid)
+    inside = (cell % 24 <= SX) & (col % 24 <= SX) & (cell // 24 <= SY) & (col // 24 <= SY)
+    return jnp.where(inside, x_part * y_part, 0.0).astype(jnp.bfloat16)
+
+
+def apply_band(band, lines, size):
+    r = jnp.dot(band, jnp.concatenate(lines, axis=0), preferred_element_type=jnp.float32)
     return r[:size], r[size:]
 
 
-def kappa_yz(kappa, lines):
+def kappa_yz(kappa):
     f = 2.0 * kappa + pltpu.roll(kappa, 1, 1) + pltpu.roll(kappa, 127, 1)
     rows = lax.broadcasted_iota(jnp.int32, f.shape, 0)
     below = jnp.where(rows == 0, 0.0, pltpu.roll(f, 1, 0))
@@ -99,41 +110,40 @@
     return c + odd * (7 - 2 * c)
 
 
-def inner_kernel(odd_ref, v_hbm, zt_ref, mat_ref, band0, band1, band2, out_ref, ve, w2, t2, u, sem):
+def inner_kernel(first, last, odd_ref, m_hbm, v_hbm, mat_ref, band0, band1, band2, out_hbm, ve, w2, t2, u, acc, sem, sem_m):
     odd = odd_ref[0]
     bands = (band0, band1, band2)
-    cuts = ((0, 2), (2, 4), (4, 7), (7, 10), (10, 13), (13, 16))
+    low = max(BATCH * first - 1, 0)
+    cuts = [low] + [BATCH * k + 1 for k in range(first + 1, last + 1)]
     loads = []
-    for n, (a, b) in enumerate(cuts):
+    for n in range(last - first):
+        a, b = cuts[n], cuts[n + 1]
         loads.append(
             [
                 pltpu.make_async_copy(
-                    v_hbm.at[pl.ds(a, b - a), line_index(odd, c)], ve.at[pl.ds(a, b - a), c], sem.at[n, c]
+                    v_hbm.at[pl.ds(a, b - a), line_index(odd, c)], ve.at[pl.ds(a - low, b - a), c], sem.at[n, c]
                 )
                 for c in range(8)
             ]
         )
         for load in loads[-1]:
             load.start()
-
-    def arrive(n):
-        for load in loads[n]:
-            load.wait()
+    if m_hbm is not None:
+        load_m = pltpu.make_async_copy(m_hbm, acc, sem_m.at[2])
+        load_m.start()
+    yz = {}
+
+    def kappa_of(p):
+        if p not in yz:
+            yz[p] = kappa_yz(mat_ref[0, p])
+        return yz[p]
 
     def filter_plane(p):
-        slot = p % 4
         for g, (ins, outs) in enumerate(NEAR):
             size = len(outs) * SZ
-            a, b = apply_band(bands[g][...], [ve[p, l] for l in ins], zt_ref[p], size)
-            w2[slot, outs[0] * SZ : outs[0] * SZ + size] = a
-            t2[slot, outs[0] * SZ : outs[0] * SZ + size] = b
-
-    yz = {}
-
-    def kappa_of(p):
-        if p not in yz:
-            yz[p] = kappa_yz(mat_ref[0, p], 8)
-        return yz[p]
+            a, b = apply_band(bands[g][...], [ve[p - low, l] for l in ins], size)
+            w2[p % 4, outs[0] * SZ : outs[0] * SZ + size] = a
+            t2[p % 4, outs[0] * SZ : outs[0] * SZ + size] = b
 
     def make_products(p, buf, base):
         f = 2.0 * kappa_of(p) + kappa_of(p + 1)
@@ -148,25 +158,35 @@
             if p:
                 w3 = w3 + w2[(p - 1) % 4, rows]
                 t3 = t3 + t2[(p - 1) % 4, rows]
-            store_products(u.at[buf], base + l * SZ, ve[p, l], w3, t3, c, l, 8)
-
-    arrive(0)
-    filter_plane(0)
-    for k in range(5):
-        arrive(k + 1)
-        if k == 0:
-            filter_plane(1)
+            store_products(u.at[buf], base + l * SZ, ve[p - low, l], w3, t3, c, l, 8)
+
+    done = low
+    for n, k in enumerate(range(first, last)):
+        for load in loads[n]:
+            load.wait()
         for q in range(BATCH):
             p = BATCH * k + q
-            if p + 1 > 1:
-                filter_plane(p + 1)
+            while done <= p + 1:
+                filter_plane(done)
+                done += 1
             make_products(p, k % 2, q * INNER)
-        left = jnp.concatenate([ve[BATCH * k + q, 0:7].reshape(INNER, K) for q in range(BATCH)], axis=0)
-        m = gram(left, u[k % 2])
-        if k == 0:
-            out_ref[...] = m
-        else:
-            out_ref[...] += m
+        left = jnp.concatenate(
+            [ve[BATCH * k + q - low, 0:7].reshape(INNER, K) for q in range(BATCH)], axis=0
+        )
+        if n == 0 and m_hbm is not None:
+            load_m.wait()
+        for half in range(2):
+            cols = slice(half * K, (half + 1) * K)
+            part = gram(left, u[k % 2, :, cols])
+            if n == 0 and m_hbm is None:
+                acc[:, cols] = part
+            else:
+                acc[:, cols] += part
+            if k == last - 1:
+                pltpu.make_async_copy(acc.at[:, cols], out_hbm.at[:, cols], sem_m.at[half]).start()
+    for half in range(2):
+        cols = slice(half * K, (half + 1) * K)
+        pltpu.make_async_copy(acc.at[:, cols], out_hbm.at[:, cols], sem_m.at[half]).wait()
 
 
 def tile_row(x, y, z_lo, core):
@@ -181,8 +201,9 @@
 
 
 def outer_kernel(
-    odd_ref, m_ref, v_hbm, xh_hbm, ym_hbm, ye_hbm, zt_ref, mat_ref, band0, band1, band2, band3, out_ref,
-    v6, v78, v14, v15, v16, w78, t78, w06, t06, u, sem,
+    odd_ref, m_hbm, v_hbm, vx_hbm, ym_hbm, ye_hbm, zf_ref, zh_ref, face_ref, mat_ref,
+    band0, band1, band2, band3, bandz, out_ref,
+    v6, v78, v14, v15, v16, w78, t78, w06, t06, u, sem, acc,
 ):
     odd = odd_ref[0]
     bands = (band0, band1, band2)
@@ -192,16 +213,37 @@
         pltpu.make_async_copy(ym_hbm.at[pl.ds(0, 15)], v78.at[:, 1], sem.at[2]),
         pltpu.make_async_copy(ym_hbm.at[15], v15.at[8], sem.at[3]),
         pltpu.make_async_copy(ye_hbm.at[pl.ds(0, SZ)], v16.at[8], sem.at[4]),
+        pltpu.make_async_copy(m_hbm, acc, sem.at[27]),
     ]
     for c in range(8):
         loads.append(pltpu.make_async_copy(v_hbm.at[15, line_index(odd, c)], v15.at[c], sem.at[5 + c]))
-        loads.append(pltpu.make_async_copy(xh_hbm.at[line_index(odd, c)], v16.at[c], sem.at[13 + c]))
+        row = pl.multiple_of(line_index(odd, c) * SZ, SZ)
+        loads.append(pltpu.make_async_copy(vx_hbm.at[pl.ds(row, SZ)], v16.at[c], sem.at[13 + c]))
         if c < 6:
             loads.append(pltpu.make_async_copy(v_hbm.at[14, line_index(odd, c)], v14.at[c], sem.at[21 + c]))
     for load in loads:
         load.start()
+    wz, tz = apply_band(bandz[...], [zh_ref[...]], FACE)
+    kap_face, rho_face, kap_halo = face_ref[0], face_ref[1], face_ref[2]
+    planes = lax.broadcasted_iota(jnp.int32, kap_halo.shape, 0)
+    lines = lax.broadcasted_iota(jnp.int32, kap_halo.shape, 1)
+    f = jnp.where(planes == SX, 0.0, 2.0 * kap_halo) + pltpu.roll(kap_halo, 1, 0) + pltpu.roll(kap_halo, 23, 0)
+    f = jnp.where(planes <= SX, f, 0.0)
+    f = jnp.where(lines == SY, 0.0, 2.0 * f) + pltpu.roll(f, 1, 1) + pltpu.roll(f, 127, 1)
+    f = f * (1.0 / 32.0)
+    kap_face = kap_face * (1.0 / 16.0)
+    rho_face = rho_face * (1.0 / 216.0)
+
+    def column(grid):
+        parts = [jnp.broadcast_to(grid[:, l : l + 1], (24, K)) for l in range(9)]
+        return jnp.concatenate(parts + [jnp.zeros((8, K), jnp.float32)], axis=0)
+
+    zf = zf_ref[...]
+    uz = jnp.concatenate([column(f) * zf.astype(jnp.float32) - column(kap_face) * wz, column(rho_face) * tz], axis=1)
+    zpart = gram(zf, uz.astype(jnp.bfloat16))
     for load in loads:
         load.wait()
+    acc[...] += zpart
 
     def line(p, l):
         if p == 15:
@@ -217,12 +259,12 @@
     def filter_near(p):
         for g, (ins, outs) in enumerate(NEAR):
             size = len(outs) * SZ
-            a, b = apply_band(bands[g][...], [line(p, l) for l in ins], zt_ref[p], size)
+            a, b = apply_band(bands[g][...], [line(p, l) for l in ins], size)
             w06[p - 14, outs[0] * SZ : outs[0] * SZ + size] = a
             t06[p - 14, outs[0] * SZ : outs[0] * SZ + size] = b
 
     def filter_edge(p):
-        a, b = apply_band(band3[...], [line(p, l) for l in EDGE[0]], zt_ref[p], OUTER)
+        a, b = apply_band(band3[...], [line(p, l) for l in EDGE[0]], OUTER)
         w78[p] = a
         t78[p] = b
 
@@ -234,7 +276,7 @@
             r = r + ref[p - 1 - lo, rows]
         return r
 
-    yz = [kappa_yz(mat_ref[0, p], 16) for p in range(17)]
+    yz = [kappa_yz(mat_ref[0, p]) for p in range(17)]
     for p in range(17):
         filter_edge(p)
         if p >= 14:
@@ -264,7 +306,7 @@
     left = jnp.concatenate(
         [v78[...].reshape(15 * OUTER, K), v15[...].reshape(9 * SZ, K), v16[...].reshape(9 * SZ, K)], axis=0
     )
-    m_ref[...] += gram(left, u[...])
+    acc[...] += gram(left, u[...])
 
     def put(i, j, half, s):
         for x in range(4):
@@ -276,43 +318,55 @@
     for half in range(2):
         for i in range(4):
             for j in range(i, 4):
-                a = m_ref[i * 128 : (i + 1) * 128, half * K + j * 128 : half * K + (j + 1) * 128]
-                b = m_ref[j * 128 : (j + 1) * 128, half * K + i * 128 : half * K + (i + 1) * 128]
+                a = acc[i * 128 : (i + 1) * 128, half * K + j * 128 : half * K + (j + 1) * 128]
+                b = acc[j * 128 : (j + 1) * 128, half * K + i * 128 : half * K + (i + 1) * 128]
                 s = a + b.T
                 put(i, j, half, s)
                 if i != j:
                     put(j, i, half, s.T)
 
 
-HBM = pl.BlockSpec(memory_space=pl.ANY)
+HBM = pl.BlockSpec(memory_space=pltpu.HBM)
 VMEM = pl.BlockSpec(memory_space=pltpu.VMEM)
 SMEM = pl.BlockSpec(memory_space=pltpu.SMEM)
 
 
-def inner_part(odd, v, zt, mat, bands):
+def inner_part(first, last, odd, m, v, mat, bands):
+    def body(odd_ref, *refs):
+        if m is None:
+            refs = (None,) + refs
+        inner_kernel(first, last, odd_ref, *refs)
+
+    planes = BATCH * (last - first) + (2 if first else 1)
+    operands = (odd,) + (() if m is None else (m,)) + (v, mat) + tuple(bands)
+    specs = [SMEM] + ([] if m is None else [HBM]) + [HBM] + [VMEM] * 4
     return pl.pallas_call(
-        inner_kernel,
-        out_shape=jax.ShapeDtypeStruct((K, 2 * K), jnp.float32),
-        in_specs=[SMEM, HBM, VMEM, VMEM, VMEM, VMEM, VMEM],
-        out_specs=VMEM,
+        body,
+        out_shape=pltpu.HBM((K, 2 * K), jnp.float32),
+        in_specs=specs,
+        out_specs=HBM,
         scratch_shapes=[
-            pltpu.VMEM((SX, SY, SZ, K), jnp.bfloat16),
+            pltpu.VMEM((planes, SY, SZ, K), jnp.bfloat16),
             pltpu.VMEM((4, INNER, K), jnp.float32),
             pltpu.VMEM((4, INNER, K), jnp.float32),
             pltpu.VMEM((2, BATCH * INNER, 2 * K), jnp.bfloat16),
-            pltpu.SemaphoreType.DMA((6, 8)),
+            pltpu.VMEM((K, 2 * K), jnp.float32),
+            pltpu.SemaphoreType.DMA((last - first, 8)),
+            pltpu.SemaphoreType.DMA((3,)),
         ],
-        compiler_params=pltpu.CompilerParams(vmem_limit_bytes=36 * 1024 * 1024),
-        cost_estimate=pl.CostEstimate(flops=9_000_000_000, transcendentals=0, bytes_accessed=10_000_000),
-        name="inner",
-    )(odd, v, zt, mat, *bands)
-
-
-def outer_part(odd, m, v, xh, ym, ye, zt, mat, bands):
+        compiler_params=pltpu.CompilerParams(vmem_limit_bytes=26 * 1024 * 1024),
+        cost_estimate=pl.CostEstimate(
+            flops=1_800_000_000 * (last - first), transcendentals=0, bytes_accessed=2_000_000 * (last - first)
+        ),
+        name=f"inner{first}",
+    )(*operands)
+
+
+def outer_part(odd, m, v, vx, ym, ye, zf, zh, face, mat, bands):
     return pl.pallas_call(
-        outer_entry,
+        outer_kernel,
         out_shape=jax.ShapeDtypeStruct((K, 2 * K), jnp.float32),
-        in_specs=[SMEM, VMEM, HBM, HBM, HBM, HBM, VMEM, VMEM, VMEM, VMEM, VMEM, VMEM],
+        in_specs=[SMEM, HBM, HBM, HBM, HBM, HBM] + [VMEM] * 9,
         out_specs=VMEM,
         scratch_shapes=[
             pltpu.VMEM((15, SZ, K), jnp.bfloat16),
@@ -325,19 +379,13 @@
             pltpu.VMEM((3, INNER, K), jnp.float32),
             pltpu.VMEM((3, INNER, K), jnp.float32),
             pltpu.VMEM((15 * OUTER + 18 * SZ, 2 * K), jnp.bfloat16),
-            pltpu.SemaphoreType.DMA((27,)),
+            pltpu.SemaphoreType.DMA((28,)),
             pltpu.VMEM((K, 2 * K), jnp.float32),
         ],
-        compiler_params=pltpu.CompilerParams(vmem_limit_bytes=48 * 1024 * 1024),
+        compiler_params=pltpu.CompilerParams(vmem_limit_bytes=32 * 1024 * 1024),
         cost_estimate=pl.CostEstimate(flops=4_000_000_000, transcendentals=0, bytes_accessed=6_000_000),
         name="outer",
-    )(odd, m, v, xh, ym, ye, zt, mat, *bands)
-
-
-def outer_entry(odd_ref, m_in, *rest):
-    *rest, acc = rest
-    acc[...] = m_in[...]
-    outer_kernel(odd_ref, acc, *rest)
+    )(odd, m, v, vx, ym, ye, zf, zh, face, mat, *bands)
 
 
 def pick(x, index, dim):
@@ -391,39 +439,75 @@
     return pick(v, z_hi, 0) + send(pick(v, 1 - z_hi, 0), to_z)
 
 
+def to_parts(x):
+    high = lax.reduce_precision(x, 8, 7)
+    rest = x - high
+    mid = lax.reduce_precision(rest, 8, 7)
+    parts = jnp.concatenate([high, mid, rest - mid, jnp.zeros_like(x)], axis=1)
+    return parts.astype(jnp.bfloat16)
+
+
+def from_parts(rows):
+    x = rows.astype(jnp.float32)
+    return (x[:, 256:384] + x[:, 128:256]) + x[:, :128]
+
+
 def per_device(eigvecs, material):
     odd = lax.axis_index("gx") % 2 == 1
     upper = lax.axis_index("gz") == 1
     side = jnp.where(odd, SY - 1, 0)
+    face = jnp.where(upper, 0, SZ - 1)
     odd_flag = odd.astype(jnp.int32).reshape(1)
+    in_hbm = lambda x: pltpu.with_memory_space_constraint(x, pltpu.HBM)
+    vectors = in_hbm(eigvecs)
 
     def chain(x, dim):
         return jnp.where(odd, lax.rev(x, (dim,)), x)
 
     ym = send(pick(eigvecs, side, 1), to_y)
-    face = jnp.where(upper, 0, SZ - 1)
-    kz = send(pick(material[0], face, 2), to_z)
-    zh = send(pick(eigvecs, face, 2), to_z)
+    zf = pick(eigvecs, face, 2)
+    kface = jnp.pad(pick(material[0], face, 2), ((0, 0), (0, 120)))
+    zm = send(jnp.concatenate([zf.reshape(SX * SY, K), to_parts(kface)], axis=0), to_z)
+    own = jnp.pad(material, ((0, 0), (0, 0), (0, 0), (0, 128 - SZ)))
+    mat = chain(own, 2)
+    bands = [band_matrix(ins, outs) for ins, outs in NEAR]
+    m = inner_part(*PIECES[0], odd_flag, None, vectors, mat, bands)
+    zm, m = lax.optimization_barrier((zm, m))
+    zh = zm[: SX * SY].reshape(SX, SY, K)
+    kz = from_parts(zm[SX * SY :])[:, :SY]
     lanes = jnp.arange(128)
-    halo_lane = jnp.where(upper, 127, SZ)
-    own = jnp.pad(material, ((0, 0), (0, 0), (0, 0), (0, 128 - SZ)))
-    kap = jnp.where(lanes == halo_lane, kz[..., None], own[0])
-    mat = jnp.stack([kap, own[1]])
-    mx = send(mat[:, 0], to_x)
-    vx = send(jnp.concatenate([eigvecs[0].reshape(SY * SZ, K), zh[0]], axis=0), to_x)
-    zt = jnp.pad(chain(zh, 1), ((0, 0), (0, 16 - SY), (0, 0)))
-    bands = [band_matrix(ins, outs, upper) for ins, outs in NEAR]
-    edge_band = band_matrix(*EDGE, upper)
-    m = inner_part(odd_flag, eigvecs, zt, chain(mat, 2), bands)
-    xh = vx[: SY * SZ].reshape(SY, SZ, K)
-    xz = vx[SY * SZ :]
-    mat = chain(jnp.concatenate([mat, mx[:, None]], axis=1), 2)
+    matz = jnp.stack([jnp.where(lanes == 64, kz[..., None], own[0]), own[1]])
+    vx = send(
+        jnp.concatenate([eigvecs[0].reshape(SY * SZ, K), zh[0], to_parts(matz[:, 0].reshape(16, 128))], axis=0),
+        to_x,
+    )
+    m = inner_part(*PIECES[1], odd_flag, in_hbm(m), vectors, mat, bands)
+    vx, m = lax.optimization_barrier((vx, m))
+    xz = vx[SY * SZ : SY * SZ + SY]
+    matz = jnp.concatenate([matz, from_parts(vx[SY * SZ + SY :]).reshape(2, 1, SY, 128)], axis=1)
+    matz = chain(matz, 2)
     zrows = chain(jnp.concatenate([zh, xz[None]], axis=0), 1)
-    my = send(mat[:, :, 0], to_y)
-    ye = send(jnp.concatenate([pick(xh, side, 0), zrows[:, 0]], axis=0), to_y)
-    mat = jnp.pad(jnp.concatenate([mat, my[:, :, None]], axis=2), ((0, 0), (0, 0), (0, 7), (0, 0)))
-    zt = jnp.pad(jnp.concatenate([zrows, ye[SZ:][:, None]], axis=1), ((0, 0), (0, 7), (0, 0)))
-    part = outer_part(odd_flag, m, eigvecs, xh, ym, ye, zt, mat, bands + [edge_band])
+    xline = lax.dynamic_slice_in_dim(vx, side * SZ, SZ, 0)
+    ye = send(jnp.concatenate([xline, zrows[:, 0], to_parts(matz[:, :, 0].reshape(34, 128))], axis=0), to_y)
+    m = inner_part(*PIECES[2], odd_flag, in_hbm(m), vectors, mat, bands)
+    ym, ye, m = lax.optimization_barrier((ym, ye, m))
+    my = from_parts(ye[SZ + 17 :]).reshape(2, 17, 1, 128)
+    matz = jnp.concatenate([matz, my], axis=2)
+    grids = jnp.stack([pick(matz[0], face, 2), pick(matz[1], face, 2), matz[0, :, :, 64]])
+    grids = jnp.pad(grids, ((0, 0), (0, 7), (0, 119)))
+    mat = jnp.pad(matz, ((0, 0), (0, 0), (0, 7), (0, 0)))
+    mat = jnp.where(lanes < SZ, mat, 0.0)
+
+    def face_rows(main, line):
+        rows = jnp.concatenate([main, line[:, None]], axis=1).transpose(1, 0, 2)
+        return jnp.pad(jnp.pad(rows, ((0, 0), (0, 7), (0, 0))).reshape(216, K), ((0, FACE - 216), (0, 0)))
+
+    xf = pick(vx[: SY * SZ].reshape(SY, SZ, K), face, 1)
+    yf = jnp.concatenate([pick(ym, face, 1), lax.dynamic_slice_in_dim(ye, face, 1, 0)], axis=0)
+    zf = face_rows(chain(jnp.concatenate([zf, xf[None]], axis=0), 1), yf)
+    zh = face_rows(zrows, ye[SZ : SZ + 17])
+    bands = bands + [band_matrix(*EDGE), face_matrix()]
+    part = outer_part(odd_flag, in_hbm(m), vectors, vx, in_hbm(ym), ye, zf, zh, grids, mat, bands)
     total = SX * SY * SZ * NGX * NGY * NGZ
     summed = reduce_to_owner(part) * (0.5 / total)
     return summed[:, :K], summed[:, K:]

time: 112 us -> 96.6 us (0.86)
  waiting for transfers between devices: 37 us -> 27.8 us
  local copies, waits for them, and re-layouts: 13.2 us -> 6.95 us
  starting transfers between devices: 31.5 us -> 25.7 us
  Pallas kernels: 24.4 us -> 29.4 us
    ppermute x14 -> x11, waiting for transfers between devices: 37 us -> 27.8 us  [send(): return lax.ppermute(value, ALL, links)]
    unnamed x13 -> x6, local copies, waits for them, and re-layouts: 6.29 us -> 0.08 us
    ppermute x14 -> x11, starting transfers between devices: 31.5 us -> 25.7 us  [send(): return lax.ppermute(value, ALL, links)]
    pallas_call x2 -> x4, Pallas kernels: 24.4 us -> 29.4 us  [the longest x3 21.4 us: inner_part(): pl.pallas_call(body, out_shape=pltpu.HBM((K, 2 * K), jnp.float32), in_spe...]
    dynamic_slice x2 -> x7, local copies, waits for them, and re-layouts: 1.65 us -> 3.03 us  [pick(): return lax.dynamic_index_in_dim(x, index, dim, keepdims=False)]
  transfers between devices with their start and end apart: 14 -> 11, of which waited for: 11 -> 7; matrix products, arithmetic and copies ran while one was open for 6% -> 5% of each run, Pallas kernels for 14% -> 22%
where the time goes in v3:
time: 96.6 us; the launch traced here: 96.1 us
  Pallas kernels  29.4 us (30%)
  waiting for transfers between devices  27.8 us (29%)
  starting transfers between devices  25.7 us (27%)
  local copies, waits for them, and re-layouts  6.95 us (7%)
  other arithmetic  4.83 us (5%)
  between operations  1.47 us (2%)
    ppermute x11, waiting for transfers between devices, send(): return lax.ppermute(value, ALL, links)  27.8 us
    ppermute x11, starting transfers between devices, send(): return lax.ppermute(value, ALL, links)  25.7 us
    pallas_call x3, Pallas kernels, inner_part(): pl.pallas_call(body, out_shape=pltpu.HBM((K, 2 * K), jnp.float32), in_spe...  21.4 us
    pallas_call x1, Pallas kernels, outer_part(): pl.pallas_call(outer_kernel, out_shape=jax.ShapeDtypeStruct((K, 2 * K), j...  8.01 us
    dynamic_slice x7, local copies, waits for them, and re-layouts, pick(): return lax.dynamic_index_in_dim(x, index, dim, keepdims=False)  3.03 us
  transfers between devices with their start and end apart: 11, of which 7 were waited for; matrix products, arithmetic and copies ran while one was open for 5% of the time, Pallas kernels for 22%

profile of v3, /device:TPU:0, one launch (start us, length us, event | category | flops | bytes accessed | tf_op | source)
XLA Modules:
  0.0 96.1 jit_solution(17344509692915250293)
XLA Ops:
  0.6 0.8 slice.93
  1.5 0.1 constant_dynamic-slice_fusion.4
  1.6 0.2 copy.40
  1.7 1.5 %constant_dynamic-slice_fusion.5 = bf16[16,8,1,512]{3,2,1,0:T(2,128)(2,1)S(1)} fusion(bf16[16,8,48,512]{3,2,1,0:T(8,128)(2,1)} %v_hbm.1, s32[]{:T(128)S(6)} %select_n.600), kind=kLoop, calls=%fused_computation.174 | loop fusion | bytes 262148 | tf_op jit(solution)/shard_map/jit(dynamic_index_in_dim)/dynamic_slice | solution.py:392
  3.4 4.1 %collective-permute-start.1 = (bf16[144,512]{1,0:T(8,128)(2,1)S(1)}, bf16[144,512]{1,0:T(8,128)(2,1)S(1)}, u32[]{:S(2)}, u32[]{:S(2)}) collective-permute-start(bf16[144,512]{1,0:T(8,128)(2,1)S(1)} %maximum_maximum_fusion.1), channel_id=1, source_target_pairs={{0,1},{1,0},{2,3},{3,2},{4,5},{5,4},{6,7},{7,6},{8,9},{9,8},{10,11... | collective-permute-start | bytes 442376 | tf_op jit(solution)/shard_map/ppermute | solution.py:32
  7.4 1.2 %dynamic-slice_bitcast_fusion.1 = bf16[16,48,512]{2,1,0:T(8,128)(2,1)S(1)} fusion(bf16[16,8,48,512]{3,2,1,0:T(8,128)(2,1)} %v_hbm.1, s32[]{:T(128)S(6)} %select_n.599), kind=kLoop, calls=%fused_computation.9 | loop fusion | bytes 1572868 | tf_op jit(solution)/shard_map/jit(dynamic_index_in_dim)/squeeze | solution.py:392
  8.6 1.3 %collective-permute-start = (bf16[16,48,512]{2,1,0:T(8,128)(2,1)S(1)}, bf16[16,48,512]{2,1,0:T(8,128)(2,1)}, u32[]{:S(2)}, u32[]{:S(2)}) collective-permute-start(bf16[16,48,512]{2,1,0:T(8,128)(2,1)S(1)} %dynamic-slice_bitcast_fusion.1), channel_id=1, source_target_pairs={{2,0},{3,1},{4,2},{5,3},{6,4},{7,5},{8,6},{9,7},{10,8},{11,9},{12,... | collective-permute-start | bytes 2359304 | tf_op jit(solution)/shard_map/ppermute | solution.py:32
  10.1 0.1 copy.48
  10.5 0.2 multiply_convert_fusion.3.refs_4_.refs_5_.band2
  10.7 0.3 multiply_convert_fusion.2.band3
  11.0 0.4 multiply_convert_fusion.refs_3_.refs_4_.band1
  11.4 0.4 multiply_convert_fusion.1.refs_2_.refs_3_.band0
  11.8 1.0 select_convert_fusion.bandz
  12.8 5.1 %inner0.1.refs_0_ = f32[512,1024]{1,0:T(8,128)} custom-call(s32[1]{0:T(128)} %bitcast.odd_ref, bf16[16,8,48,512]{3,2,1,0:T(8,128)(2,1)} %v_hbm.1, f32[2,16,8,128]{3,2,1,0:T(8,128)S(1)} %broadcast_select_fusion.1.refs_1_.refs_2_, bf16[288,192]{1,0:T(8,128)(2,1)S(1)} %multiply_convert_fusion.1.refs_2_.refs_3_.band0, ...), custom_call_target="tpu_custom_call" | custom-call | flops 1800000000 | bytes 2000000 | tf_op jit(solution)/shard_map/inner0/pallas_call | solution.py:343
  18.0 0.1 slice_select_fusion
  18.1 1.3 %collective-permute-start.2 = (bf16[408,512]{1,0:T(8,128)(2,1)S(1)}, bf16[408,512]{1,0:T(8,128)(2,1)S(1)}, u32[]{:S(2)}, u32[]{:S(2)}) collective-permute-start(bf16[408,512]{1,0:T(8,128)(2,1)S(1)} %maximum_maximum_fusion), channel_id=1, source_target_pairs={{32,0},{33,1},{34,2},{35,3},{36,4},{37,5},{38,6},{39,7},{40,8},{41... | collective-permute-start | bytes 1253384 | tf_op jit(solution)/shard_map/ppermute | solution.py:32
  19.5 8.2 %inner1.1.refs_0_ = f32[512,1024]{1,0:T(8,128)} custom-call(s32[1]{0:T(128)} %bitcast.odd_ref, f32[512,1024]{1,0:T(8,128)} %inner0.1.refs_0_, bf16[16,8,48,512]{3,2,1,0:T(8,128)(2,1)} %v_hbm.1, f32[2,16,8,128]{3,2,1,0:T(8,128)S(1)} %broadcast_select_fusion.1.refs_1_.refs_2_, bf16[288,192]{1,0:T(8,128)(2,1)S(1)} %multiply_convert_fusion.1.refs_2_.refs_3_.band0, ...), custom_call_target="tpu_custom_call" | custom-call | flops 3600000000 | bytes 4000000 | tf_op jit(solution)/shard_map/inner1/pallas_call | solution.py:343
  28.0 1.5 %collective-permute-start.3 = (bf16[99,512]{1,0:T(8,128)(2,1)S(1)}, bf16[99,512]{1,0:T(8,128)(2,1)S(1)}, u32[]{:S(2)}, u32[]{:S(2)}) collective-permute-start(bf16[99,512]{1,0:T(8,128)(2,1)S(1)} %maximum_maximum_fusion.2), channel_id=1, source_target_pairs={{2,0},{3,1},{4,2},{5,3},{6,4},{7,5},{8,6},{9,7},{10,8},{11,9},{12,... | collective-permute-start | bytes 304136 | tf_op jit(solution)/shard_map/ppermute | solution.py:32
  29.7 8.2 %inner3.1.m_hbm = f32[512,1024]{1,0:T(8,128)} custom-call(s32[1]{0:T(128)} %bitcast.odd_ref, f32[512,1024]{1,0:T(8,128)} %inner1.1.refs_0_, bf16[16,8,48,512]{3,2,1,0:T(8,128)(2,1)} %v_hbm.1, f32[2,16,8,128]{3,2,1,0:T(8,128)S(1)} %broadcast_select_fusion.1.refs_1_.refs_2_, bf16[288,192]{1,0:T(8,128)(2,1)S(1)} %multiply_convert_fusion.1.refs_2_.refs_3_.band0, ...), custom_call_target="tpu_custom_call" | custom-call | flops 3600000000 | bytes 4000000 | tf_op jit(solution)/shard_map/inner3/pallas_call | solution.py:343
  38.0 0.1 fusion.47
  38.1 0.1 dynamic-slice_maximum_fusion.1
  38.3 0.1 copy.28
  38.4 0.1 copy.31
  38.5 0.1 dynamic-slice_maximum_fusion
  38.7 0.1 copy.29
  38.8 0.1 copy.32
  38.9 0.1 copy.30
  39.0 0.1 copy.33
  39.2 0.9 constant_dynamic-slice_fusion.1
  40.4 8.0 %outer.1 = f32[512,1024]{1,0:T(8,128)S(1)} custom-call(s32[1]{0:T(128)} %bitcast.odd_ref, f32[512,1024]{1,0:T(8,128)} %inner3.1.m_hbm, bf16[16,8,48,512]{3,2,1,0:T(8,128)(2,1)} %v_hbm.1, bf16[408,512]{1,0:T(8,128)(2,1)S(1)} %collective-permute-done.2.vx_hbm, bf16[16,48,512]{2,1,0:T(8,128)(2,1)} %collective-permute-done.ym_hbm, ...), custom_call_target="tpu_custom_call" | custom-call | flops 4000000000 | bytes 6000000 | tf_op jit(solution)/shard_map/outer/pallas_call | solution.py:366
  48.4 0.1 dynamic-slice_bitcast_fusion
  48.5 4.2 %collective-permute-start.4 = (f32[256,1024]{1,0:T(8,128)S(1)}, f32[256,1024]{1,0:T(8,128)}, u32[]{:S(2)}, u32[]{:S(2)}) collective-permute-start(f32[256,1024]{1,0:T(8,128)S(1)} %dynamic-slice_bitcast_fusion), channel_id=1, source_target_pairs={{0,32},{1,33},{2,34},{3,35},{4,36},{5,37},{6,38},{7,39},{8,40},{9,... | collective-permute-start | bytes 3145736 | tf_op jit(solution)/shard_map/ppermute | solution.py:32
  52.7 2.4 %collective-permute-done.4 = f32[256,1024]{1,0:T(8,128)} collective-permute-done((f32[256,1024]{1,0:T(8,128)S(1)}, f32[256,1024]{1,0:T(8,128)}, u32[]{:S(2)}, u32[]{:S(2)}) %collective-permute-start.4) | collective-permute-done | bytes 1048608 | tf_op jit(solution)/shard_map/ppermute | solution.py:32
  55.1 1.4 %bitcast_add_fusion = f32[256,1024]{1,0:T(8,128)S(1)} fusion(f32[256,1024]{1,0:T(8,128)} %collective-permute-done.4, f32[2,256,1024]{2,1,0:T(8,128)S(1)} %bitcast.83, s32[]{:T(128)S(6)} %select_n.667), kind=kLoop, calls=%fused_computation | loop fusion | flops 262144 | bytes 3145732 | tf_op jit(solution)/shard_map/add | solution.py:434
  56.5 1.1 %collective-permute-start.5 = (f32[128,1024]{1,0:T(8,128)S(1)}, f32[128,1024]{1,0:T(8,128)S(1)}, u32[]{:S(2)}, u32[]{:S(2)}) collective-permute-start(f32[128,1024]{1,0:T(8,128)S(1)} %dynamic-slice_bitcast_fusion.2), channel_id=1, source_target_pairs={{0,64},{1,65},{2,66},{3,67},{4,68},{5,69},{6,70},{7,71},{8,72},{9,... | collective-permute-start | bytes 1572872 | tf_op jit(solution)/shard_map/ppermute | solution.py:32
  57.6 8.1 %collective-permute-done.5 = f32[128,1024]{1,0:T(8,128)S(1)} collective-permute-done((f32[128,1024]{1,0:T(8,128)S(1)}, f32[128,1024]{1,0:T(8,128)S(1)}, u32[]{:S(2)}, u32[]{:S(2)}) %collective-permute-start.5) | collective-permute-done | bytes 524320 | tf_op jit(solution)/shard_map/ppermute | solution.py:32
  65.8 0.1 bitcast_add_fusion.1
  65.9 2.8 %collective-permute-start.6 = (f32[64,1024]{1,0:T(8,128)S(1)}, f32[64,1024]{1,0:T(8,128)S(1)}, u32[]{:S(2)}, u32[]{:S(2)}) collective-permute-start(f32[64,1024]{1,0:T(8,128)S(1)} %dynamic-slice_bitcast_fusion.3), channel_id=1, source_target_pairs={{0,8},{1,9},{2,10},{3,11},{4,12},{5,13},{6,14},{7,15},{8,0},{9,1},... | collective-permute-start | bytes 786440 | tf_op jit(solution)/shard_map/ppermute | solution.py:32
  68.7 4.4 %collective-permute-done.6 = f32[64,1024]{1,0:T(8,128)S(1)} collective-permute-done((f32[64,1024]{1,0:T(8,128)S(1)}, f32[64,1024]{1,0:T(8,128)S(1)}, u32[]{:S(2)}, u32[]{:S(2)}) %collective-permute-start.6) | collective-permute-done | bytes 262176 | tf_op jit(solution)/shard_map/ppermute | solution.py:32
  73.1 3.7 %collective-permute-start.7 = (f32[32,1024]{1,0:T(8,128)S(1)}, f32[32,1024]{1,0:T(8,128)S(1)}, u32[]{:S(2)}, u32[]{:S(2)}) collective-permute-start(f32[32,1024]{1,0:T(8,128)S(1)} %dynamic-slice_bitcast_fusion.4), channel_id=1, source_target_pairs={{0,24},{1,25},{2,26},{3,27},{4,28},{5,29},{6,30},{7,31},{8,16},{9,... | collective-permute-start | bytes 393224 | tf_op jit(solution)/shard_map/ppermute | solution.py:32
  76.8 2.9 %collective-permute-done.7 = f32[32,1024]{1,0:T(8,128)S(1)} collective-permute-done((f32[32,1024]{1,0:T(8,128)S(1)}, f32[32,1024]{1,0:T(8,128)S(1)}, u32[]{:S(2)}, u32[]{:S(2)}) %collective-permute-start.7) | collective-permute-done | bytes 131104 | tf_op jit(solution)/shard_map/ppermute | solution.py:32
  79.7 1.4 %collective-permute-start.8 = (f32[16,1024]{1,0:T(8,128)S(1)}, f32[16,1024]{1,0:T(8,128)S(1)}, u32[]{:S(2)}, u32[]{:S(2)}) collective-permute-start(f32[16,1024]{1,0:T(8,128)S(1)} %dynamic-slice_bitcast_fusion.5), channel_id=1, source_target_pairs={{0,2},{1,3},{2,0},{3,1},{4,6},{5,7},{6,4},{7,5},{8,10},{9,11},{10,... | collective-permute-start | bytes 196616 | tf_op jit(solution)/shard_map/ppermute | solution.py:32
  81.1 3.0 %collective-permute-done.8 = f32[16,1024]{1,0:T(8,128)S(1)} collective-permute-done((f32[16,1024]{1,0:T(8,128)S(1)}, f32[16,1024]{1,0:T(8,128)S(1)}, u32[]{:S(2)}, u32[]{:S(2)}) %collective-permute-start.8) | collective-permute-done | bytes 65568 | tf_op jit(solution)/shard_map/ppermute | solution.py:32
  84.1 4.1 %collective-permute-start.9 = (f32[8,1024]{1,0:T(8,128)S(1)}, f32[8,1024]{1,0:T(8,128)S(1)}, u32[]{:S(2)}, u32[]{:S(2)}) collective-permute-start(f32[8,1024]{1,0:T(8,128)S(1)} %dynamic-slice_bitcast_fusion.6), channel_id=1, source_target_pairs={{0,6},{1,7},{2,4},{3,5},{4,2},{5,3},{6,0},{7,1},{8,14},{9,15},{10,... | collective-permute-start | bytes 98312 | tf_op jit(solution)/shard_map/ppermute | solution.py:32
  88.3 1.9 %collective-permute-done.9 = f32[8,1024]{1,0:T(8,128)S(1)} collective-permute-done((f32[8,1024]{1,0:T(8,128)S(1)}, f32[8,1024]{1,0:T(8,128)S(1)}, u32[]{:S(2)}, u32[]{:S(2)}) %collective-permute-start.9) | collective-permute-done | bytes 32800 | tf_op jit(solution)/shard_map/ppermute | solution.py:32
  90.2 0.3 collective-permute-start.10
  90.5 5.1 %collective-permute-done.10 = f32[4,1024]{1,0:T(4,128)S(1)} collective-permute-done((f32[4,1024]{1,0:T(4,128)S(1)}, f32[4,1024]{1,0:T(4,128)S(1)}, u32[]{:S(2)}, u32[]{:S(2)}) %collective-permute-start.10) | collective-permute-done | bytes 16416 | tf_op jit(solution)/shard_map/ppermute | solution.py:32
  95.5 0.6 fusion.82
  (101 shorter events, 1.3 us)
Async XLA Ops:
  1.6 8.9 %copy-start = (f32[2,16,8,48]{3,2,1,0:T(8,128)S(1)}, f32[2,16,8,48]{3,2,1,0:T(8,128)}, u32[]{:S(2)}) copy-start(f32[2,16,8,48]{3,2,1,0:T(8,128)} %param.3) | copy-start | bytes 147460
  3.4 14.5 %collective-permute-start.1 = (bf16[144,512]{1,0:T(8,128)(2,1)S(1)}, bf16[144,512]{1,0:T(8,128)(2,1)S(1)}, u32[]{:S(2)}, u32[]{:S(2)}) collective-permute-start(bf16[144,512]{1,0:T(8,128)(2,1)S(1)} %maximum_maximum_fusion.1), channel_id=1, source_target_pairs={{0,1},{1,0},{2,3},{3,2},{4,5},{5,4},{6,7},{7,6},{8,9},{9,8},{10,11... | collective-permute-start | bytes 442376 | tf_op jit(solution)/shard_map/ppermute | solution.py:32
  8.6 29.3 %collective-permute-start = (bf16[16,48,512]{2,1,0:T(8,128)(2,1)S(1)}, bf16[16,48,512]{2,1,0:T(8,128)(2,1)}, u32[]{:S(2)}, u32[]{:S(2)}) collective-permute-start(bf16[16,48,512]{2,1,0:T(8,128)(2,1)S(1)} %dynamic-slice_bitcast_fusion.1), channel_id=1, source_target_pairs={{2,0},{3,1},{4,2},{5,3},{6,4},{7,5},{8,6},{9,7},{10,8},{11,9},{12,... | collective-permute-start | bytes 2359304 | tf_op jit(solution)/shard_map/ppermute | solution.py:32
  12.8 5.3 %slice-start = ((bf16[16,8,48,512]{3,2,1,0:T(8,128)(2,1)}), bf16[1,8,48,512]{3,2,1,0:T(8,128)(2,1)S(1)}, s32[]{:S(2)}) async-start(bf16[16,8,48,512]{3,2,1,0:T(8,128)(2,1)} %v_hbm.1), calls=%async_computation | async-start | bytes 786432 | tf_op jit(solution)/shard_map/slice | solution.py:481
  18.1 9.5 %collective-permute-start.2 = (bf16[408,512]{1,0:T(8,128)(2,1)S(1)}, bf16[408,512]{1,0:T(8,128)(2,1)S(1)}, u32[]{:S(2)}, u32[]{:S(2)}) collective-permute-start(bf16[408,512]{1,0:T(8,128)(2,1)S(1)} %maximum_maximum_fusion), channel_id=1, source_target_pairs={{32,0},{33,1},{34,2},{35,3},{36,4},{37,5},{38,6},{39,7},{40,8},{41... | collective-permute-start | bytes 1253384 | tf_op jit(solution)/shard_map/ppermute | solution.py:32
  28.0 9.8 %collective-permute-start.3 = (bf16[99,512]{1,0:T(8,128)(2,1)S(1)}, bf16[99,512]{1,0:T(8,128)(2,1)S(1)}, u32[]{:S(2)}, u32[]{:S(2)}) collective-permute-start(bf16[99,512]{1,0:T(8,128)(2,1)S(1)} %maximum_maximum_fusion.2), channel_id=1, source_target_pairs={{2,0},{3,1},{4,2},{5,3},{6,4},{7,5},{8,6},{9,7},{10,8},{11,9},{12,... | collective-permute-start | bytes 304136 | tf_op jit(solution)/shard_map/ppermute | solution.py:32
  48.5 6.6 %collective-permute-start.4 = (f32[256,1024]{1,0:T(8,128)S(1)}, f32[256,1024]{1,0:T(8,128)}, u32[]{:S(2)}, u32[]{:S(2)}) collective-permute-start(f32[256,1024]{1,0:T(8,128)S(1)} %dynamic-slice_bitcast_fusion), channel_id=1, source_target_pairs={{0,32},{1,33},{2,34},{3,35},{4,36},{5,37},{6,38},{7,39},{8,40},{9,... | collective-permute-start | bytes 3145736 | tf_op jit(solution)/shard_map/ppermute | solution.py:32
  56.5 9.3 %collective-permute-start.5 = (f32[128,1024]{1,0:T(8,128)S(1)}, f32[128,1024]{1,0:T(8,128)S(1)}, u32[]{:S(2)}, u32[]{:S(2)}) collective-permute-start(f32[128,1024]{1,0:T(8,128)S(1)} %dynamic-slice_bitcast_fusion.2), channel_id=1, source_target_pairs={{0,64},{1,65},{2,66},{3,67},{4,68},{5,69},{6,70},{7,71},{8,72},{9,... | collective-permute-start | bytes 1572872 | tf_op jit(solution)/shard_map/ppermute | solution.py:32
  65.9 7.2 %collective-permute-start.6 = (f32[64,1024]{1,0:T(8,128)S(1)}, f32[64,1024]{1,0:T(8,128)S(1)}, u32[]{:S(2)}, u32[]{:S(2)}) collective-permute-start(f32[64,1024]{1,0:T(8,128)S(1)} %dynamic-slice_bitcast_fusion.3), channel_id=1, source_target_pairs={{0,8},{1,9},{2,10},{3,11},{4,12},{5,13},{6,14},{7,15},{8,0},{9,1},... | collective-permute-start | bytes 786440 | tf_op jit(solution)/shard_map/ppermute | solution.py:32
  73.1 6.6 %collective-permute-start.7 = (f32[32,1024]{1,0:T(8,128)S(1)}, f32[32,1024]{1,0:T(8,128)S(1)}, u32[]{:S(2)}, u32[]{:S(2)}) collective-permute-start(f32[32,1024]{1,0:T(8,128)S(1)} %dynamic-slice_bitcast_fusion.4), channel_id=1, source_target_pairs={{0,24},{1,25},{2,26},{3,27},{4,28},{5,29},{6,30},{7,31},{8,16},{9,... | collective-permute-start | bytes 393224 | tf_op jit(solution)/shard_map/ppermute | solution.py:32
  79.7 4.3 %collective-permute-start.8 = (f32[16,1024]{1,0:T(8,128)S(1)}, f32[16,1024]{1,0:T(8,128)S(1)}, u32[]{:S(2)}, u32[]{:S(2)}) collective-permute-start(f32[16,1024]{1,0:T(8,128)S(1)} %dynamic-slice_bitcast_fusion.5), channel_id=1, source_target_pairs={{0,2},{1,3},{2,0},{3,1},{4,6},{5,7},{6,4},{7,5},{8,10},{9,11},{10,... | collective-permute-start | bytes 196616 | tf_op jit(solution)/shard_map/ppermute | solution.py:32
  84.1 6.0 %collective-permute-start.9 = (f32[8,1024]{1,0:T(8,128)S(1)}, f32[8,1024]{1,0:T(8,128)S(1)}, u32[]{:S(2)}, u32[]{:S(2)}) collective-permute-start(f32[8,1024]{1,0:T(8,128)S(1)} %dynamic-slice_bitcast_fusion.6), channel_id=1, source_target_pairs={{0,6},{1,7},{2,4},{3,5},{4,2},{5,3},{6,0},{7,1},{8,14},{9,15},{10,... | collective-permute-start | bytes 98312 | tf_op jit(solution)/shard_map/ppermute | solution.py:32
  90.2 5.3 %collective-permute-start.10 = (f32[4,1024]{1,0:T(4,128)S(1)}, f32[4,1024]{1,0:T(4,128)S(1)}, u32[]{:S(2)}, u32[]{:S(2)}) collective-permute-start(f32[4,1024]{1,0:T(4,128)S(1)} %dynamic-slice_bitcast_fusion.7), channel_id=1, source_target_pairs={{0,1},{1,0},{2,3},{3,2},{4,5},{5,4},{6,7},{7,6},{8,9},{9,8},{10,11... | collective-permute-start | bytes 49160 | tf_op jit(solution)/shard_map/ppermute | solution.py:32

commit v4 on v3

--- a/solution.py
+++ b/solution.py
@@ -1,5 +1,6 @@
 import jax
 import jax.numpy as jnp
+import numpy as np
 from jax import lax
 from jax.experimental import pallas as pl
 from jax.experimental.pallas import tpu as pltpu
@@ -14,6 +15,7 @@
 OUTER = 2 * SZ
 BATCH = 3
 FACE = 224
+MAIN = 15 * OUTER + 18 * SZ
 PIECES = ((0, 1), (1, 3), (3, 5))
 
 
@@ -45,31 +47,29 @@
 
 
 def chain_part(gap, ends, mid):
-    return jnp.where(gap == 0, jnp.where(ends, 0.0, mid), jnp.where(gap == 1, 1.0, 0.0))
+    return np.where(gap == 0, np.where(ends, 0.0, mid), np.where(gap == 1, 1.0, 0.0))
 
 
 def band_matrix(lines_in, lines_out):
     size = len(lines_out) * SZ
-    row = lax.broadcasted_iota(jnp.int32, (2 * size, len(lines_in) * SZ), 0)
-    col = lax.broadcasted_iota(jnp.int32, (2 * size, len(lines_in) * SZ), 1)
-    mid = jnp.where(row < size, 2.0, 4.0)
+    row, col = np.indices((2 * size, len(lines_in) * SZ))
+    mid = np.where(row < size, 2.0, 4.0)
     cell = row % size
     line_out = lines_out[0] + cell // SZ
     line_in = lines_in[0] + col // SZ
-    z_part = chain_part(jnp.abs(cell % SZ - col % SZ), False, mid)
-    y_part = chain_part(jnp.abs(line_out - line_in), line_out == 8, mid)
-    return (y_part * z_part).astype(jnp.bfloat16)
+    z_part = chain_part(np.abs(cell % SZ - col % SZ), False, mid)
+    y_part = chain_part(np.abs(line_out - line_in), line_out == 8, mid)
+    return jnp.asarray(y_part * z_part, jnp.bfloat16)
 
 
 def face_matrix():
-    row = lax.broadcasted_iota(jnp.int32, (2 * FACE, FACE), 0)
-    col = lax.broadcasted_iota(jnp.int32, (2 * FACE, FACE), 1)
-    mid = jnp.where(row < FACE, 2.0, 4.0)
+    row, col = np.indices((2 * FACE, FACE))
+    mid = np.where(row < FACE, 2.0, 4.0)
     cell = row % FACE
-    x_part = chain_part(jnp.abs(cell % 24 - col % 24), cell % 24 == SX, mid)
-    y_part = chain_part(jnp.abs(cell // 24 - col // 24), cell // 24 == SY, mid)
+    x_part = chain_part(np.abs(cell % 24 - col % 24), cell % 24 == SX, mid)
+    y_part = chain_part(np.abs(cell // 24 - col // 24), cell // 24 == SY, mid)
     inside = (cell % 24 <= SX) & (col % 24 <= SX) & (cell // 24 <= SY) & (col // 24 <= SY)
-    return jnp.where(inside, x_part * y_part, 0.0).astype(jnp.bfloat16)
+    return jnp.asarray(np.where(inside, x_part * y_part, 0.0), jnp.bfloat16)
 
 
 def apply_band(band, lines, size):
@@ -114,19 +114,15 @@
     odd = odd_ref[0]
     bands = (band0, band1, band2)
     low = max(BATCH * first - 1, 0)
-    cuts = [low] + [BATCH * k + 1 for k in range(first + 1, last + 1)]
-    loads = []
-    for n in range(last - first):
-        a, b = cuts[n], cuts[n + 1]
-        loads.append(
-            [
-                pltpu.make_async_copy(
-                    v_hbm.at[pl.ds(a, b - a), line_index(odd, c)], ve.at[pl.ds(a - low, b - a), c], sem.at[n, c]
-                )
-                for c in range(8)
-            ]
-        )
-        for load in loads[-1]:
+    loads = {
+        p: [
+            pltpu.make_async_copy(v_hbm.at[p, line_index(odd, c)], ve.at[p - low, c], sem.at[p - low, c])
+            for c in range(8)
+        ]
+        for p in range(low, BATCH * last + 1)
+    }
+    for p in loads:
+        for load in loads[p]:
             load.start()
     if m_hbm is not None:
         load_m = pltpu.make_async_copy(m_hbm, acc, sem_m.at[2])
@@ -139,6 +135,8 @@
         return yz[p]
 
     def filter_plane(p):
+        for load in loads[p]:
+            load.wait()
         for g, (ins, outs) in enumerate(NEAR):
             size = len(outs) * SZ
             a, b = apply_band(bands[g][...], [ve[p - low, l] for l in ins], size)
@@ -162,8 +160,6 @@
 
     done = low
     for n, k in enumerate(range(first, last)):
-        for load in loads[n]:
-            load.wait()
         for q in range(BATCH):
             p = BATCH * k + q
             while done <= p + 1:
@@ -189,17 +185,6 @@
         pltpu.make_async_copy(acc.at[:, cols], out_hbm.at[:, cols], sem_m.at[half]).wait()
 
 
-def tile_row(x, y, z_lo, core):
-    a = {0: (0, 0), 3: (0, 1), 1: (1, 0), 2: (1, 1)}
-    xa, xb = a[x]
-    ya, yb = a[y]
-    bits = (z_lo, xa, xb, ya, yb) if core == 0 else (xa, z_lo, ya, xb, yb)
-    at = core
-    for bit in bits:
-        at = at * 2 + bit
-    return at * 8
-
-
 def outer_kernel(
     odd_ref, m_hbm, v_hbm, vx_hbm, ym_hbm, ye_hbm, zf_ref, zh_ref, face_ref, mat_ref,
     band0, band1, band2, band3, bandz, out_ref,
@@ -213,7 +198,6 @@
         pltpu.make_async_copy(ym_hbm.at[pl.ds(0, 15)], v78.at[:, 1], sem.at[2]),
         pltpu.make_async_copy(ym_hbm.at[15], v15.at[8], sem.at[3]),
         pltpu.make_async_copy(ye_hbm.at[pl.ds(0, SZ)], v16.at[8], sem.at[4]),
-        pltpu.make_async_copy(m_hbm, acc, sem.at[27]),
     ]
     for c in range(8):
         loads.append(pltpu.make_async_copy(v_hbm.at[15, line_index(odd, c)], v15.at[c], sem.at[5 + c]))
@@ -221,7 +205,8 @@
         loads.append(pltpu.make_async_copy(vx_hbm.at[pl.ds(row, SZ)], v16.at[c], sem.at[13 + c]))
         if c < 6:
             loads.append(pltpu.make_async_copy(v_hbm.at[14, line_index(odd, c)], v14.at[c], sem.at[21 + c]))
-    for load in loads:
+    load_m = pltpu.make_async_copy(m_hbm, acc, sem.at[27])
+    for load in loads + [load_m]:
         load.start()
     wz, tz = apply_band(bandz[...], [zh_ref[...]], FACE)
     kap_face, rho_face, kap_halo = face_ref[0], face_ref[1], face_ref[2]
@@ -240,10 +225,9 @@
 
     zf = zf_ref[...]
     uz = jnp.concatenate([column(f) * zf.astype(jnp.float32) - column(kap_face) * wz, column(rho_face) * tz], axis=1)
-    zpart = gram(zf, uz.astype(jnp.bfloat16))
+    u[MAIN:] = uz.astype(jnp.bfloat16)
     for load in loads:
         load.wait()
-    acc[...] += zpart
 
     def line(p, l):
         if p == 15:
@@ -277,11 +261,7 @@
         return r
 
     yz = [kappa_yz(mat_ref[0, p]) for p in range(17)]
-    for p in range(17):
-        filter_edge(p)
-        if p >= 14:
-            filter_near(p)
-    for p in range(17):
+    def make_products(p):
         if p == 16:
             f = yz[15]
         else:
@@ -303,17 +283,25 @@
                 w3 = along_x(w06, p, 14, 16, rows, 2.0)
                 t3 = along_x(t06, p, 14, 16, rows, 4.0)
             store_products(u, row, line(p, l), w3, t3, c, l, 16)
+
+    filter_edge(0)
+    for p in range(17):
+        if p < 16:
+            filter_edge(p + 1)
+            if p + 1 >= 14:
+                filter_near(p + 1)
+        make_products(p)
+        if p == 7:
+            load_m.wait()
+            acc[...] += gram(v78[0:8].reshape(8 * OUTER, K), u[: 8 * OUTER])
     left = jnp.concatenate(
-        [v78[...].reshape(15 * OUTER, K), v15[...].reshape(9 * SZ, K), v16[...].reshape(9 * SZ, K)], axis=0
+        [v78[8:15].reshape(7 * OUTER, K), v15[...].reshape(9 * SZ, K), v16[...].reshape(9 * SZ, K), zf], axis=0
     )
-    acc[...] += gram(left, u[...])
+    acc[...] += gram(left, u[8 * OUTER :])
 
     def put(i, j, half, s):
-        for x in range(4):
-            for y in range(4):
-                t = (x * 4 + y) * 8
-                at = tile_row(x, y, i // 2, i % 2)
-                out_ref[at : at + 8, half * K + j * 128 : half * K + (j + 1) * 128] = s[t : t + 8]
+        at = ((i % 2) * 2 + i // 2) * 128
+        out_ref[half, at : at + 128, j * 128 : (j + 1) * 128] = s
 
     for half in range(2):
         for i in range(4):
@@ -351,7 +339,7 @@
             pltpu.VMEM((4, INNER, K), jnp.float32),
             pltpu.VMEM((2, BATCH * INNER, 2 * K), jnp.bfloat16),
             pltpu.VMEM((K, 2 * K), jnp.float32),
-            pltpu.SemaphoreType.DMA((last - first, 8)),
+            pltpu.SemaphoreType.DMA((planes, 8)),
             pltpu.SemaphoreType.DMA((3,)),
         ],
         compiler_params=pltpu.CompilerParams(vmem_limit_bytes=26 * 1024 * 1024),
@@ -365,7 +353,7 @@
 def outer_part(odd, m, v, vx, ym, ye, zf, zh, face, mat, bands):
     return pl.pallas_call(
         outer_kernel,
-        out_shape=jax.ShapeDtypeStruct((K, 2 * K), jnp.float32),
+        out_shape=jax.ShapeDtypeStruct((2, K, K), jnp.float32),
         in_specs=[SMEM, HBM, HBM, HBM, HBM, HBM] + [VMEM] * 9,
         out_specs=VMEM,
         scratch_shapes=[
@@ -378,7 +366,7 @@
             pltpu.VMEM((17, OUTER, K), jnp.float32),
             pltpu.VMEM((3, INNER, K), jnp.float32),
             pltpu.VMEM((3, INNER, K), jnp.float32),
-            pltpu.VMEM((15 * OUTER + 18 * SZ, 2 * K), jnp.bfloat16),
+            pltpu.VMEM((MAIN + FACE, 2 * K), jnp.bfloat16),
             pltpu.SemaphoreType.DMA((28,)),
             pltpu.VMEM((K, 2 * K), jnp.float32),
         ],
@@ -393,50 +381,15 @@
 
 
 def reduce_to_owner(part):
-    ix = lax.axis_index("gx")
-    iy = lax.axis_index("gy")
-    core = ix % 2
-    z_lo = ix // 2
-    z_hi = lax.axis_index("gz")
-
-    def bits(r):
-        return ((r == 1) | (r == 2)).astype(jnp.int32), (r >= 2).astype(jnp.int32)
-
-    def flip_z(x, y, z):
-        return (x ^ 2, y, z)
-
-    def flip_xa(x, y, z):
-        return (x, (y // 4 ^ 1) * 4 + y % 4, z)
-
-    def flip_xb(x, y, z):
-        return (x, (3 - y // 4) * 4 + y % 4, z)
-
-    def flip_ya(x, y, z):
-        return (x, y ^ 1, z)
-
-    def flip_yb(x, y, z):
-        return (x, y // 4 * 4 + 3 - y % 4, z)
-
-    xa, xb = bits(iy // 4)
-    ya, yb = bits(iy % 4)
-    stages = (
-        (core, core, lambda x, y, z: (x ^ 1, y, z), lambda x, y, z: (x ^ 1, y, z)),
-        (z_lo, xa, flip_z, flip_xa),
-        (xa, z_lo, flip_xa, flip_z),
-        (xb, ya, flip_xb, flip_ya),
-        (ya, xb, flip_ya, flip_xb),
-        (yb, yb, flip_yb, flip_yb),
-    )
-    v = part
-    for even_bit, odd_bit, even_move, odd_move in stages:
-        bit = jnp.where(core == 0, even_bit, odd_bit)
-        v = v.reshape(2, v.shape[0] // 2, 2 * K)
-        v = pick(v, bit, 0) + send(
-            pick(v, 1 - bit, 0),
-            lambda x, y, z, e=even_move, o=odd_move: o(x, y, z) if x % 2 else e(x, y, z),
-        )
-    v = v.reshape(2, 4, 2 * K)
-    return pick(v, z_hi, 0) + send(pick(v, 1 - z_hi, 0), to_z)
+    core = lax.axis_index("gx") % 2
+    halves = []
+    for half in range(2):
+        rows = part[half].reshape(2, K // 2, K)
+        halves.append(pick(rows, core, 0) + send(pick(rows, 1 - core, 0), lambda x, y, z: (x ^ 1, y, z)))
+    groups = [[linear(x, y, z) for x in (c, c + 2) for y in range(NGY) for z in range(NGZ)] for c in range(2)]
+    blocks = jnp.concatenate(halves, axis=1).reshape(64, 4, 2 * K)
+    blocks = lax.all_to_all(blocks, ALL, 0, 0, tiled=True, axis_index_groups=groups)
+    return jnp.sum(blocks, axis=0)
 
 
 def to_parts(x):

time: 96.6 us -> 86.4 us (0.89)
  blocking collectives: 0 us -> 29 us
  waiting for transfers between devices: 27.8 us -> 2.04 us
  starting transfers between devices: 25.7 us -> 12.2 us
  other arithmetic: 4.83 us -> 1.34 us
  local copies, waits for them, and re-layouts: 6.95 us -> 8.9 us
  Pallas kernels: 29.4 us -> 31.2 us
    all_to_all x0 -> x1, blocking collectives: none -> 29 us  [reduce_to_owner(): lax.all_to_all(blocks, ALL, 0, 0, tiled=True, axis_index_groups=groups)]
    ppermute x11 -> x6, waiting for transfers between devices: 27.8 us -> 2.04 us  [send(): return lax.ppermute(value, ALL, links)]
    ppermute x11 -> x6, starting transfers between devices: 25.7 us -> 12.2 us  [send(): return lax.ppermute(value, ALL, links)]
    convert_element_type x5 -> x0, other arithmetic: 2.26 us -> none  [the longest x4 1.3 us: band_matrix(): return (y_part * z_part).astype(jnp.bfloat16)]
    pallas_call x3, Pallas kernels: 21.4 us -> 23.1 us  [inner_part(): pl.pallas_call(body, out_shape=pltpu.HBM((K, 2 * K), jnp.float32), in_spe...]
    squeeze x9 -> x4, local copies, waits for them, and re-layouts: 1.55 us -> 3.02 us  [pick(): return lax.dynamic_index_in_dim(x, index, dim, keepdims=False)]
    add x9 -> x2, other arithmetic: 1.51 us -> 0.17 us  [reduce_to_owner(): pick(rows, core, 0)]
  transfers between devices with their start and end apart: 11 -> 6, of which waited for: 7 -> 2; matrix products, arithmetic and copies ran while one was open for 5% -> 3% of each run, Pallas kernels for 22% -> 27%
where the time goes in v4:
time: 86.4 us; the launch traced here: 86 us
  Pallas kernels  31.2 us (36%)
  blocking collectives  29 us (34%)
  starting transfers between devices  12.2 us (14%)
  local copies, waits for them, and re-layouts  8.9 us (10%)
  waiting for transfers between devices  2.04 us (2%)
  other arithmetic  1.34 us (2%)
  between operations  1.31 us (2%)
    all_to_all x1, blocking collectives, reduce_to_owner(): lax.all_to_all(blocks, ALL, 0, 0, tiled=True, axis_index_groups=groups)  29 us
    pallas_call x3, Pallas kernels, inner_part(): pl.pallas_call(body, out_shape=pltpu.HBM((K, 2 * K), jnp.float32), in_spe...  23.1 us
    ppermute x6, starting transfers between devices, send(): return lax.ppermute(value, ALL, links)  12.2 us
    pallas_call x1, Pallas kernels, outer_part(): pl.pallas_call(outer_kernel, out_shape=jax.ShapeDtypeStruct((2, K, K), jn...  8.01 us
    dynamic_slice x7, local copies, waits for them, and re-layouts, pick(): return lax.dynamic_index_in_dim(x, index, dim, keepdims=False)  3.03 us
    squeeze x4, local copies, waits for them, and re-layouts, pick(): return lax.dynamic_index_in_dim(x, index, dim, keepdims=False)  3.02 us
    ppermute x6, waiting for transfers between devices, send(): return lax.ppermute(value, ALL, links)  2.04 us
  transfers between devices with their start and end apart: 6, of which 2 were waited for; matrix products, arithmetic and copies ran while one was open for 3% of the time, Pallas kernels for 27%

profile of v4, /device:TPU:0, one launch (start us, length us, event | category | flops | bytes accessed | tf_op | source)
XLA Modules:
  0.0 86.0 jit_solution(1799142005468840572)
XLA Ops:
  0.6 0.8 slice.99
  1.5 0.1 constant_dynamic-slice_fusion.4
  1.6 0.2 copy.45
  1.7 1.5 %constant_dynamic-slice_fusion.5 = bf16[16,8,1,512]{3,2,1,0:T(2,128)(2,1)S(1)} fusion(bf16[16,8,48,512]{3,2,1,0:T(8,128)(2,1)} %v_hbm.1, s32[]{:T(128)S(6)} %select_n.81), kind=kLoop, calls=%fused_computation.78 | loop fusion | bytes 262148 | tf_op jit(solution)/shard_map/jit(dynamic_index_in_dim)/dynamic_slice | solution.py:380
  3.3 0.0 copy-start
  3.3 0.0 copy-start.1
  3.3 0.0 copy-start.2
  3.4 4.1 %collective-permute-start.1 = (bf16[144,512]{1,0:T(8,128)(2,1)S(1)}, bf16[144,512]{1,0:T(8,128)(2,1)S(1)}, u32[]{:S(2)}, u32[]{:S(2)}) collective-permute-start(bf16[144,512]{1,0:T(8,128)(2,1)S(1)} %maximum_maximum_fusion.1), channel_id=1, source_target_pairs={{0,1},{1,0},{2,3},{3,2},{4,5},{5,4},{6,7},{7,6},{8,9},{9,8},{10,11... | collective-permute-start | bytes 442376 | tf_op jit(solution)/shard_map/ppermute | solution.py:34
  7.5 1.2 %dynamic-slice_bitcast_fusion = bf16[16,48,512]{2,1,0:T(8,128)(2,1)S(1)} fusion(bf16[16,8,48,512]{3,2,1,0:T(8,128)(2,1)} %v_hbm.1, s32[]{:T(128)S(6)} %select_n.80), kind=kLoop, calls=%fused_computation.1 | loop fusion | bytes 1572868 | tf_op jit(solution)/shard_map/jit(dynamic_index_in_dim)/squeeze | solution.py:380
  8.6 1.3 %collective-permute-start = (bf16[16,48,512]{2,1,0:T(8,128)(2,1)S(1)}, bf16[16,48,512]{2,1,0:T(8,128)(2,1)}, u32[]{:S(2)}, u32[]{:S(2)}) collective-permute-start(bf16[16,48,512]{2,1,0:T(8,128)(2,1)S(1)} %dynamic-slice_bitcast_fusion), channel_id=1, source_target_pairs={{2,0},{3,1},{4,2},{5,3},{6,4},{7,5},{8,6},{9,7},{10,8},{11,9},{12,... | collective-permute-start | bytes 2359304 | tf_op jit(solution)/shard_map/ppermute | solution.py:34
  10.0 0.1 copy.53
  10.3 0.0 slice-start
  10.3 5.3 %inner0.1.refs_0_ = f32[512,1024]{1,0:T(8,128)} custom-call(s32[1]{0:T(128)} %bitcast.odd_ref, bf16[16,8,48,512]{3,2,1,0:T(8,128)(2,1)} %v_hbm.1, f32[2,16,8,128]{3,2,1,0:T(8,128)S(1)} %broadcast_select_fusion.1.refs_1_.refs_2_, bf16[288,192]{1,0:T(8,128)(2,1)S(1)} %copy-done, bf16[288,240]{1,0:T(8,128)(2,1)S(1)} %copy-done.1, bf16[96,144]{1,0:T(8,128)(2,1)S(1)} %copy-done.2), custom_call_target="tpu_custom_call" | custom-call | flops 1800000000 | bytes 2000000 | tf_op jit(solution)/shard_map/inner0/pallas_call | solution.py:331
  15.6 0.0 collective-permute-done.1
  15.7 0.1 slice_select_fusion
  15.8 1.3 %collective-permute-start.2 = (bf16[408,512]{1,0:T(8,128)(2,1)S(1)}, bf16[408,512]{1,0:T(8,128)(2,1)S(1)}, u32[]{:S(2)}, u32[]{:S(2)}) collective-permute-start(bf16[408,512]{1,0:T(8,128)(2,1)S(1)} %maximum_maximum_fusion), channel_id=1, source_target_pairs={{32,0},{33,1},{34,2},{35,3},{36,4},{37,5},{38,6},{39,7},{40,8},{41... | collective-permute-start | bytes 1253384 | tf_op jit(solution)/shard_map/ppermute | solution.py:34
  17.2 8.9 %inner1.1.refs_0_ = f32[512,1024]{1,0:T(8,128)} custom-call(s32[1]{0:T(128)} %bitcast.odd_ref, f32[512,1024]{1,0:T(8,128)} %inner0.1.refs_0_, bf16[16,8,48,512]{3,2,1,0:T(8,128)(2,1)} %v_hbm.1, f32[2,16,8,128]{3,2,1,0:T(8,128)S(1)} %broadcast_select_fusion.1.refs_1_.refs_2_, bf16[288,192]{1,0:T(8,128)(2,1)S(1)} %copy-done, bf16[288,240]{1,0:T(8,128)(2,1)S(1)} %copy-done.1, ...), custom_call_target="tpu_custom_call" | custom-call | flops 3600000000 | bytes 4000000 | tf_op jit(solution)/shard_map/inner1/pallas_call | solution.py:331
  26.1 0.0 collective-permute-done.2.vx_hbm
  26.5 0.1 reverse_select_fusion
  26.6 1.5 %collective-permute-start.3 = (bf16[99,512]{1,0:T(8,128)(2,1)S(1)}, bf16[99,512]{1,0:T(8,128)(2,1)S(1)}, u32[]{:S(2)}, u32[]{:S(2)}) collective-permute-start(bf16[99,512]{1,0:T(8,128)(2,1)S(1)} %maximum_maximum_fusion.2), channel_id=1, source_target_pairs={{2,0},{3,1},{4,2},{5,3},{6,4},{7,5},{8,6},{9,7},{10,8},{11,9},{12,... | collective-permute-start | bytes 304136 | tf_op jit(solution)/shard_map/ppermute | solution.py:34
  28.1 8.9 %inner3.1.m_hbm = f32[512,1024]{1,0:T(8,128)} custom-call(s32[1]{0:T(128)} %bitcast.odd_ref, f32[512,1024]{1,0:T(8,128)} %inner1.1.refs_0_, bf16[16,8,48,512]{3,2,1,0:T(8,128)(2,1)} %v_hbm.1, f32[2,16,8,128]{3,2,1,0:T(8,128)S(1)} %broadcast_select_fusion.1.refs_1_.refs_2_, bf16[288,192]{1,0:T(8,128)(2,1)S(1)} %copy-done, bf16[288,240]{1,0:T(8,128)(2,1)S(1)} %copy-done.1, ...), custom_call_target="tpu_custom_call" | custom-call | flops 3600000000 | bytes 4000000 | tf_op jit(solution)/shard_map/inner3/pallas_call | solution.py:331
  37.1 0.0 collective-permute-done.3.ye_hbm
  37.1 0.0 collective-permute-done.ym_hbm
  37.2 0.1 fusion
  37.3 0.1 dynamic-slice_maximum_fusion.1
  37.5 0.1 copy.33
  37.6 0.1 copy.36
  37.7 0.1 dynamic-slice_maximum_fusion
  37.9 0.1 copy.34
  38.0 0.1 copy.37
  38.1 0.1 copy.35
  38.2 0.1 copy.38
  38.4 0.9 %constant_dynamic-slice_fusion.1 = bf16[16,1,512]{2,1,0:T(2,128)(2,1)S(1)} fusion(bf16[16,48,512]{2,1,0:T(8,128)(2,1)} %collective-permute-done.ym_hbm, s32[]{:T(128)S(6)} %select_n.81), kind=kLoop, calls=%fused_computation.74 | loop fusion | bytes 32772 | tf_op jit(solution)/shard_map/jit(dynamic_index_in_dim)/dynamic_slice | solution.py:380
  39.6 8.0 %outer.1 = f32[2,512,512]{2,1,0:T(8,128)S(1)} custom-call(s32[1]{0:T(128)} %bitcast.odd_ref, f32[512,1024]{1,0:T(8,128)} %inner3.1.m_hbm, bf16[16,8,48,512]{3,2,1,0:T(8,128)(2,1)} %v_hbm.1, bf16[408,512]{1,0:T(8,128)(2,1)S(1)} %collective-permute-done.2.vx_hbm, bf16[16,48,512]{2,1,0:T(8,128)(2,1)} %collective-permute-done.ym_hbm, ...), custom_call_target="tpu_custom_call" | custom-call | flops 4000000000 | bytes 6000000 | tf_op jit(solution)/shard_map/outer/pallas_call | solution.py:354
  47.6 0.2 fusion.7
  47.8 0.8 dynamic-slice_bitcast_fusion.2
  48.6 4.1 %collective-permute-start.4 = (f32[256,512]{1,0:T(8,128)}, f32[256,512]{1,0:T(8,128)S(1)}, u32[]{:S(2)}, u32[]{:S(2)}) collective-permute-start(f32[256,512]{1,0:T(8,128)} %dynamic-slice_bitcast_fusion.2), channel_id=1, source_target_pairs={{0,32},{1,33},{2,34},{3,35},{4,36},{5,37},{6,38},{7,39},{8,40},{9,... | collective-permute-start | bytes 1572872 | tf_op jit(solution)/shard_map/ppermute | solution.py:34
  52.7 0.8 dynamic-slice_bitcast_fusion.1
  53.5 0.0 collective-permute-start.5
  53.5 0.9 %collective-permute-done.4 = f32[256,512]{1,0:T(8,128)S(1)} collective-permute-done((f32[256,512]{1,0:T(8,128)}, f32[256,512]{1,0:T(8,128)S(1)}, u32[]{:S(2)}, u32[]{:S(2)}) %collective-permute-start.4) | collective-permute-done | bytes 524320 | tf_op jit(solution)/shard_map/ppermute | solution.py:34
  54.5 0.1 bitcast_add_fusion.1
  54.5 1.1 %collective-permute-done.5 = f32[256,512]{1,0:T(8,128)S(1)} collective-permute-done((f32[256,512]{1,0:T(8,128)}, f32[256,512]{1,0:T(8,128)S(1)}, u32[]{:S(2)}, u32[]{:S(2)}) %collective-permute-start.5) | collective-permute-done | bytes 524320 | tf_op jit(solution)/shard_map/ppermute | solution.py:34
  55.7 0.1 bitcast_add_fusion
  55.7 0.1 pad_maximum_fusion
  55.8 0.3 reshape.55
  56.2 29.0 %all_to_all.5 = f32[64,4,1024]{2,1,0:T(4,128)S(1)} all-to-all(f32[64,4,1024]{2,1,0:T(4,128)S(1)} %reshape.55), channel_id=1, replica_groups={{0,1,2,3,4,5,6,7,8,9,10,11,12,13,14,15,16,17,18,19,20,21,22,23,24,25,26..., dimensions={0} | all-to-all | bytes 2097152 | tf_op jit(solution)/shard_map/all_to_all | solution.py:391
  85.2 0.2 reduce_sum.9
  85.4 0.6 fusion.9
  (66 shorter events, 0.9 us)
Async XLA Ops:
  1.5 8.7 %copy-start.5 = (f32[2,16,8,48]{3,2,1,0:T(8,128)S(1)}, f32[2,16,8,48]{3,2,1,0:T(8,128)}, u32[]{:S(2)}) copy-start(f32[2,16,8,48]{3,2,1,0:T(8,128)} %param.8) | copy-start | bytes 147460
  3.3 6.9 %copy-start = (bf16[288,192]{1,0:T(8,128)(2,1)S(1)}, bf16[288,192]{1,0:T(8,128)(2,1)}, u32[]{:S(2)}) copy-start(bf16[288,192]{1,0:T(8,128)(2,1)} %constant.102.clone.refs_2_.refs_3_.band0) | copy-start | bytes 331780
  3.3 6.9 %copy-start.1 = (bf16[288,240]{1,0:T(8,128)(2,1)S(1)}, bf16[288,240]{1,0:T(8,128)(2,1)}, u32[]{:S(2)}) copy-start(bf16[288,240]{1,0:T(8,128)(2,1)} %constant.103.clone.refs_3_.refs_4_.band1) | copy-start | bytes 414724
  3.3 6.9 %copy-start.2 = (bf16[96,144]{1,0:T(8,128)(2,1)S(1)}, bf16[96,144]{1,0:T(8,128)(2,1)}, u32[]{:S(2)}) copy-start(bf16[96,144]{1,0:T(8,128)(2,1)} %constant.104.clone.refs_4_.refs_5_.band2) | copy-start | bytes 82948
  3.4 12.2 %collective-permute-start.1 = (bf16[144,512]{1,0:T(8,128)(2,1)S(1)}, bf16[144,512]{1,0:T(8,128)(2,1)S(1)}, u32[]{:S(2)}, u32[]{:S(2)}) collective-permute-start(bf16[144,512]{1,0:T(8,128)(2,1)S(1)} %maximum_maximum_fusion.1), channel_id=1, source_target_pairs={{0,1},{1,0},{2,3},{3,2},{4,5},{5,4},{6,7},{7,6},{8,9},{9,8},{10,11... | collective-permute-start | bytes 442376 | tf_op jit(solution)/shard_map/ppermute | solution.py:34
  8.6 28.4 %collective-permute-start = (bf16[16,48,512]{2,1,0:T(8,128)(2,1)S(1)}, bf16[16,48,512]{2,1,0:T(8,128)(2,1)}, u32[]{:S(2)}, u32[]{:S(2)}) collective-permute-start(bf16[16,48,512]{2,1,0:T(8,128)(2,1)S(1)} %dynamic-slice_bitcast_fusion), channel_id=1, source_target_pairs={{2,0},{3,1},{4,2},{5,3},{6,4},{7,5},{8,6},{9,7},{10,8},{11,9},{12,... | collective-permute-start | bytes 2359304 | tf_op jit(solution)/shard_map/ppermute | solution.py:34
  10.3 5.5 %slice-start = ((bf16[16,8,48,512]{3,2,1,0:T(8,128)(2,1)}), bf16[1,8,48,512]{3,2,1,0:T(8,128)(2,1)S(1)}, s32[]{:S(2)}) async-start(bf16[16,8,48,512]{3,2,1,0:T(8,128)(2,1)} %v_hbm.1), calls=%async_computation.1 | async-start | bytes 786432 | tf_op jit(solution)/shard_map/slice | solution.py:434
  15.8 10.3 %collective-permute-start.2 = (bf16[408,512]{1,0:T(8,128)(2,1)S(1)}, bf16[408,512]{1,0:T(8,128)(2,1)S(1)}, u32[]{:S(2)}, u32[]{:S(2)}) collective-permute-start(bf16[408,512]{1,0:T(8,128)(2,1)S(1)} %maximum_maximum_fusion), channel_id=1, source_target_pairs={{32,0},{33,1},{34,2},{35,3},{36,4},{37,5},{38,6},{39,7},{40,8},{41... | collective-permute-start | bytes 1253384 | tf_op jit(solution)/shard_map/ppermute | solution.py:34
  26.6 10.4 %collective-permute-start.3 = (bf16[99,512]{1,0:T(8,128)(2,1)S(1)}, bf16[99,512]{1,0:T(8,128)(2,1)S(1)}, u32[]{:S(2)}, u32[]{:S(2)}) collective-permute-start(bf16[99,512]{1,0:T(8,128)(2,1)S(1)} %maximum_maximum_fusion.2), channel_id=1, source_target_pairs={{2,0},{3,1},{4,2},{5,3},{6,4},{7,5},{8,6},{9,7},{10,8},{11,9},{12,... | collective-permute-start | bytes 304136 | tf_op jit(solution)/shard_map/ppermute | solution.py:34
  37.7 1.8 %copy-start.3 = (bf16[448,224]{1,0:T(8,128)(2,1)S(1)}, bf16[448,224]{1,0:T(8,128)(2,1)}, u32[]{:S(2)}) copy-start(bf16[448,224]{1,0:T(8,128)(2,1)} %constant.106.clone.bandz) | copy-start | bytes 602116
  37.7 1.8 %copy-start.4 = (bf16[192,144]{1,0:T(8,128)(2,1)S(1)}, bf16[192,144]{1,0:T(8,128)(2,1)}, u32[]{:S(2)}) copy-start(bf16[192,144]{1,0:T(8,128)(2,1)} %constant.105.clone.band3) | copy-start | bytes 165892
  48.6 5.8 %collective-permute-start.4 = (f32[256,512]{1,0:T(8,128)}, f32[256,512]{1,0:T(8,128)S(1)}, u32[]{:S(2)}, u32[]{:S(2)}) collective-permute-start(f32[256,512]{1,0:T(8,128)} %dynamic-slice_bitcast_fusion.2), channel_id=1, source_target_pairs={{0,32},{1,33},{2,34},{3,35},{4,36},{5,37},{6,38},{7,39},{8,40},{9,... | collective-permute-start | bytes 1572872 | tf_op jit(solution)/shard_map/ppermute | solution.py:34
  53.5 2.1 %collective-permute-start.5 = (f32[256,512]{1,0:T(8,128)}, f32[256,512]{1,0:T(8,128)S(1)}, u32[]{:S(2)}, u32[]{:S(2)}) collective-permute-start(f32[256,512]{1,0:T(8,128)} %dynamic-slice_bitcast_fusion.1), channel_id=1, source_target_pairs={{0,32},{1,33},{2,34},{3,35},{4,36},{5,37},{6,38},{7,39},{8,40},{9,... | collective-permute-start | bytes 1572872 | tf_op jit(solution)/shard_map/ppermute | solution.py:34

commit v5 on v4

--- a/solution.py
+++ b/solution.py
@@ -115,17 +115,13 @@
     bands = (band0, band1, band2)
     low = max(BATCH * first - 1, 0)
     loads = {
-        p: [
-            pltpu.make_async_copy(v_hbm.at[p, line_index(odd, c)], ve.at[p - low, c], sem.at[p - low, c])
-            for c in range(8)
-        ]
-        for p in range(low, BATCH * last + 1)
+        p: pltpu.make_async_copy(v_hbm.at[p], ve.at[p - low], sem.at[p - low]) for p in range(low, BATCH * last + 1)
     }
     for p in loads:
-        for load in loads[p]:
-            load.start()
+        loads[p].start()
+    place = [line_index(odd, c) for c in range(8)]
     if m_hbm is not None:
-        load_m = pltpu.make_async_copy(m_hbm, acc, sem_m.at[2])
+        load_m = pltpu.make_async_copy(m_hbm, acc, sem_m.at[4])
         load_m.start()
     yz = {}
 
@@ -135,11 +131,10 @@
         return yz[p]
 
     def filter_plane(p):
-        for load in loads[p]:
-            load.wait()
+        loads[p].wait()
         for g, (ins, outs) in enumerate(NEAR):
             size = len(outs) * SZ
-            a, b = apply_band(bands[g][...], [ve[p - low, l] for l in ins], size)
+            a, b = apply_band(bands[g][...], [ve[p - low, place[l]] for l in ins], size)
             w2[p % 4, outs[0] * SZ : outs[0] * SZ + size] = a
             t2[p % 4, outs[0] * SZ : outs[0] * SZ + size] = b
 
@@ -156,7 +151,7 @@
             if p:
                 w3 = w3 + w2[(p - 1) % 4, rows]
                 t3 = t3 + t2[(p - 1) % 4, rows]
-            store_products(u.at[buf], base + l * SZ, ve[p - low, l], w3, t3, c, l, 8)
+            store_products(u.at[buf], base + l * SZ, ve[p - low, place[l]], w3, t3, c, l, 8)
 
     done = low
     for n, k in enumerate(range(first, last)):
@@ -167,45 +162,42 @@
                 done += 1
             make_products(p, k % 2, q * INNER)
         left = jnp.concatenate(
-            [ve[BATCH * k + q - low, 0:7].reshape(INNER, K) for q in range(BATCH)], axis=0
+            [ve[BATCH * k + q - low, place[l]] for q in range(BATCH) for l in range(7)], axis=0
         )
         if n == 0 and m_hbm is not None:
             load_m.wait()
-        for half in range(2):
-            cols = slice(half * K, (half + 1) * K)
+        for piece in range(4):
+            cols = slice(piece * 256, (piece + 1) * 256)
             part = gram(left, u[k % 2, :, cols])
             if n == 0 and m_hbm is None:
                 acc[:, cols] = part
             else:
                 acc[:, cols] += part
             if k == last - 1:
-                pltpu.make_async_copy(acc.at[:, cols], out_hbm.at[:, cols], sem_m.at[half]).start()
-    for half in range(2):
-        cols = slice(half * K, (half + 1) * K)
-        pltpu.make_async_copy(acc.at[:, cols], out_hbm.at[:, cols], sem_m.at[half]).wait()
+                pltpu.make_async_copy(acc.at[:, cols], out_hbm.at[:, cols], sem_m.at[piece]).start()
+    for piece in range(4):
+        cols = slice(piece * 256, (piece + 1) * 256)
+        pltpu.make_async_copy(acc.at[:, cols], out_hbm.at[:, cols], sem_m.at[piece]).wait()
 
 
 def outer_kernel(
     odd_ref, m_hbm, v_hbm, vx_hbm, ym_hbm, ye_hbm, zf_ref, zh_ref, face_ref, mat_ref,
-    band0, band1, band2, band3, bandz, out_ref,
-    v6, v78, v14, v15, v16, w78, t78, w06, t06, u, sem, acc,
+    band0, band1, band2, band3, bandz, keep_s, send_s, keep_m, send_m,
+    v6, v7, v8, vp, w78, t78, w06, t06, u, sem, acc, res,
 ):
     odd = odd_ref[0]
     bands = (band0, band1, band2)
     loads = [
-        pltpu.make_async_copy(v_hbm.at[pl.ds(0, 15), line_index(odd, 6)], v6, sem.at[0]),
-        pltpu.make_async_copy(v_hbm.at[pl.ds(0, 15), line_index(odd, 7)], v78.at[:, 0], sem.at[1]),
-        pltpu.make_async_copy(ym_hbm.at[pl.ds(0, 15)], v78.at[:, 1], sem.at[2]),
-        pltpu.make_async_copy(ym_hbm.at[15], v15.at[8], sem.at[3]),
-        pltpu.make_async_copy(ye_hbm.at[pl.ds(0, SZ)], v16.at[8], sem.at[4]),
+        pltpu.make_async_copy(v_hbm.at[pl.ds(0, 14), line_index(odd, 6)], v6, sem.at[0]),
+        pltpu.make_async_copy(v_hbm.at[pl.ds(0, 14), line_index(odd, 7)], v7, sem.at[1]),
+        pltpu.make_async_copy(ym_hbm, v8.at[pl.ds(0, 16)], sem.at[2]),
+        pltpu.make_async_copy(v_hbm.at[pl.ds(14, 2)], vp.at[pl.ds(0, 2)], sem.at[3]),
+        pltpu.make_async_copy(ye_hbm.at[pl.ds(0, SZ)], v8.at[16], sem.at[4]),
     ]
-    for c in range(8):
-        loads.append(pltpu.make_async_copy(v_hbm.at[15, line_index(odd, c)], v15.at[c], sem.at[5 + c]))
-        row = pl.multiple_of(line_index(odd, c) * SZ, SZ)
-        loads.append(pltpu.make_async_copy(vx_hbm.at[pl.ds(row, SZ)], v16.at[c], sem.at[13 + c]))
-        if c < 6:
-            loads.append(pltpu.make_async_copy(v_hbm.at[14, line_index(odd, c)], v14.at[c], sem.at[21 + c]))
-    load_m = pltpu.make_async_copy(m_hbm, acc, sem.at[27])
+    for y in range(SY):
+        loads.append(pltpu.make_async_copy(vx_hbm.at[pl.ds(y * SZ, SZ)], vp.at[2, y], sem.at[5 + y]))
+    place = [line_index(odd, c) for c in range(8)]
+    load_m = pltpu.make_async_copy(m_hbm, acc, sem.at[13])
     for load in loads + [load_m]:
         load.start()
     wz, tz = apply_band(bandz[...], [zh_ref[...]], FACE)
@@ -230,15 +222,11 @@
         load.wait()
 
     def line(p, l):
-        if p == 15:
-            return v15[l]
-        if p == 16:
-            return v16[l]
-        if l >= 7:
-            return v78[p, l - 7]
-        if l == 6:
-            return v6[p]
-        return v14[l]
+        if l == 8:
+            return v8[p]
+        if p >= 14:
+            return vp[p - 14, place[l]]
+        return v7[p] if l == 7 else v6[p]
 
     def filter_near(p):
         for g, (ins, outs) in enumerate(NEAR):
@@ -293,15 +281,14 @@
         make_products(p)
         if p == 7:
             load_m.wait()
-            acc[...] += gram(v78[0:8].reshape(8 * OUTER, K), u[: 8 * OUTER])
-    left = jnp.concatenate(
-        [v78[8:15].reshape(7 * OUTER, K), v15[...].reshape(9 * SZ, K), v16[...].reshape(9 * SZ, K), zf], axis=0
-    )
+            left = jnp.concatenate([line(q, l) for q in range(8) for l in (7, 8)], axis=0)
+            acc[...] += gram(left, u[: 8 * OUTER])
+    rows = [line(p, l) for p in range(8, 17) for l in range(0 if p >= 15 else 7, 9)]
+    left = jnp.concatenate(rows + [zf], axis=0)
     acc[...] += gram(left, u[8 * OUTER :])
 
     def put(i, j, half, s):
-        at = ((i % 2) * 2 + i // 2) * 128
-        out_ref[half, at : at + 128, j * 128 : (j + 1) * 128] = s
+        res[i % 2, half, (i // 2) * 128 : (i // 2 + 1) * 128, j * 128 : (j + 1) * 128] = s
 
     for half in range(2):
         for i in range(4):
@@ -312,6 +299,14 @@
                 put(i, j, half, s)
                 if i != j:
                     put(j, i, half, s.T)
+    for core in range(2):
+
+        @pl.when(odd == core)
+        def _():
+            keep_s[...] = res[core, 0]
+            send_s[...] = res[1 - core, 0]
+            keep_m[...] = res[core, 1]
+            send_m[...] = res[1 - core, 1]
 
 
 HBM = pl.BlockSpec(memory_space=pltpu.HBM)
@@ -339,8 +334,8 @@
             pltpu.VMEM((4, INNER, K), jnp.float32),
             pltpu.VMEM((2, BATCH * INNER, 2 * K), jnp.bfloat16),
             pltpu.VMEM((K, 2 * K), jnp.float32),
-            pltpu.SemaphoreType.DMA((planes, 8)),
-            pltpu.SemaphoreType.DMA((3,)),
+            pltpu.SemaphoreType.DMA((planes,)),
+            pltpu.SemaphoreType.DMA((5,)),
         ],
         compiler_params=pltpu.CompilerParams(vmem_limit_bytes=26 * 1024 * 1024),
         cost_estimate=pl.CostEstimate(
@@ -353,22 +348,22 @@
 def outer_part(odd, m, v, vx, ym, ye, zf, zh, face, mat, bands):
     return pl.pallas_call(
         outer_kernel,
-        out_shape=jax.ShapeDtypeStruct((2, K, K), jnp.float32),
+        out_shape=[jax.ShapeDtypeStruct((K // 2, K), jnp.float32)] * 4,
         in_specs=[SMEM, HBM, HBM, HBM, HBM, HBM] + [VMEM] * 9,
-        out_specs=VMEM,
+        out_specs=[VMEM] * 4,
         scratch_shapes=[
-            pltpu.VMEM((15, SZ, K), jnp.bfloat16),
-            pltpu.VMEM((15, 2, SZ, K), jnp.bfloat16),
-            pltpu.VMEM((6, SZ, K), jnp.bfloat16),
-            pltpu.VMEM((9, SZ, K), jnp.bfloat16),
-            pltpu.VMEM((9, SZ, K), jnp.bfloat16),
+            pltpu.VMEM((14, SZ, K), jnp.bfloat16),
+            pltpu.VMEM((14, SZ, K), jnp.bfloat16),
+            pltpu.VMEM((17, SZ, K), jnp.bfloat16),
+            pltpu.VMEM((3, SY, SZ, K), jnp.bfloat16),
             pltpu.VMEM((17, OUTER, K), jnp.float32),
             pltpu.VMEM((17, OUTER, K), jnp.float32),
             pltpu.VMEM((3, INNER, K), jnp.float32),
             pltpu.VMEM((3, INNER, K), jnp.float32),
             pltpu.VMEM((MAIN + FACE, 2 * K), jnp.bfloat16),
-            pltpu.SemaphoreType.DMA((28,)),
+            pltpu.SemaphoreType.DMA((14,)),
             pltpu.VMEM((K, 2 * K), jnp.float32),
+            pltpu.VMEM((2, 2, K // 2, K), jnp.float32),
         ],
         compiler_params=pltpu.CompilerParams(vmem_limit_bytes=32 * 1024 * 1024),
         cost_estimate=pl.CostEstimate(flops=4_000_000_000, transcendentals=0, bytes_accessed=6_000_000),
@@ -381,11 +376,7 @@
 
 
 def reduce_to_owner(part):
-    core = lax.axis_index("gx") % 2
-    halves = []
-    for half in range(2):
-        rows = part[half].reshape(2, K // 2, K)
-        halves.append(pick(rows, core, 0) + send(pick(rows, 1 - core, 0), lambda x, y, z: (x ^ 1, y, z)))
+    halves = [keep + send(other, lambda x, y, z: (x ^ 1, y, z)) for keep, other in (part[:2], part[2:])]
     groups = [[linear(x, y, z) for x in (c, c + 2) for y in range(NGY) for z in range(NGZ)] for c in range(2)]
     blocks = jnp.concatenate(halves, axis=1).reshape(64, 4, 2 * K)
     blocks = lax.all_to_all(blocks, ALL, 0, 0, tiled=True, axis_index_groups=groups)

time: 86.4 us -> 88.8 us (1.028)
  local copies, waits for them, and re-layouts: 8.9 us -> 10.6 us
  Pallas kernels: 31.2 us -> 30.2 us
  other arithmetic: 1.34 us -> 2.24 us
    unnamed x16 -> x22, local copies, waits for them, and re-layouts: 0.11 us -> 2.73 us
    squeeze x4 -> x2, local copies, waits for them, and re-layouts: 3.02 us -> 1.38 us  [pick(): return lax.dynamic_index_in_dim(x, index, dim, keepdims=False)]
    pallas_call x3, Pallas kernels: 23.1 us -> 22.2 us  [inner_part(): pl.pallas_call(body, out_shape=pltpu.HBM((K, 2 * K), jnp.float32), in_spe...]
    pad x1, local copies, waits for them, and re-layouts: 0.01 us -> 0.92 us  [per_device(): own = jnp.pad(material, ((0, 0), (0, 0), (0, 0), (0, 128 - SZ)))]
    select_n x3, other arithmetic: 0.11 us -> 1.01 us  [chain(): return jnp.where(odd, lax.rev(x, (dim,)), x)]
  transfers between devices with their start and end apart: 6 -> 6, of which waited for: 2 -> 2; matrix products, arithmetic and copies ran while one was open for 3% -> 4% of each run, Pallas kernels for 27% -> 25%
where the time goes in v5:
time: 88.8 us; the launch traced here: 88.3 us
  Pallas kernels  30.2 us (34%)
  blocking collectives  29.3 us (33%)
  starting transfers between devices  12.6 us (14%)
  local copies, waits for them, and re-layouts  10.6 us (12%)
  other arithmetic  2.24 us (3%)
  waiting for transfers between devices  2.12 us (2%)
  between operations  1.31 us (1%)
    all_to_all x1, blocking collectives, reduce_to_owner(): lax.all_to_all(blocks, ALL, 0, 0, tiled=True, axis_index_groups=groups)  29.3 us
    pallas_call x3, Pallas kernels, inner_part(): pl.pallas_call(body, out_shape=pltpu.HBM((K, 2 * K), jnp.float32), in_spe...  22.2 us
    ppermute x6, starting transfers between devices, send(): return lax.ppermute(value, ALL, links)  12.6 us
    pallas_call x1, Pallas kernels, outer_part(): pl.pallas_call(outer_kernel, out_shape=[jax.ShapeDtypeStruct((K // 2, K),...  7.99 us
    dynamic_slice x7, local copies, waits for them, and re-layouts, pick(): return lax.dynamic_index_in_dim(x, index, dim, keepdims=False)  3.03 us
    unnamed x22, local copies, waits for them, and re-layouts  2.73 us
    ppermute x6, waiting for transfers between devices, send(): return lax.ppermute(value, ALL, links)  2.12 us
  transfers between devices with their start and end apart: 6, of which 2 were waited for; matrix products, arithmetic and copies ran while one was open for 4% of the time, Pallas kernels for 25%

profile of v5, /device:TPU:0, one launch (start us, length us, event | category | flops | bytes accessed | tf_op | source)
XLA Modules:
  0.0 88.3 jit_solution(13685378119205850302)
XLA Ops:
  0.6 0.8 slice.93
  1.5 0.1 constant_dynamic-slice_fusion.4
  1.6 0.2 copy.45
  1.7 1.5 %constant_dynamic-slice_fusion.5 = bf16[16,8,1,512]{3,2,1,0:T(2,128)(2,1)S(1)} fusion(bf16[16,8,48,512]{3,2,1,0:T(8,128)(2,1)} %v_hbm.1, s32[]{:T(128)S(6)} %select_n.70), kind=kLoop, calls=%fused_computation.74 | loop fusion | bytes 262148 | tf_op jit(solution)/shard_map/jit(dynamic_index_in_dim)/dynamic_slice | solution.py:375
  3.4 4.1 %collective-permute-start.1 = (bf16[144,512]{1,0:T(8,128)(2,1)S(1)}, bf16[144,512]{1,0:T(8,128)(2,1)S(1)}, u32[]{:S(2)}, u32[]{:S(2)}) collective-permute-start(bf16[144,512]{1,0:T(8,128)(2,1)S(1)} %maximum_maximum_fusion.1), channel_id=1, source_target_pairs={{0,1},{1,0},{2,3},{3,2},{4,5},{5,4},{6,7},{7,6},{8,9},{9,8},{10,11... | collective-permute-start | bytes 442376 | tf_op jit(solution)/shard_map/ppermute | solution.py:34
  7.4 1.2 %dynamic-slice_bitcast_fusion = bf16[16,48,512]{2,1,0:T(8,128)(2,1)S(1)} fusion(bf16[16,8,48,512]{3,2,1,0:T(8,128)(2,1)} %v_hbm.1, s32[]{:T(128)S(6)} %select_n.69), kind=kLoop, calls=%fused_computation.1 | loop fusion | bytes 1572868 | tf_op jit(solution)/shard_map/jit(dynamic_index_in_dim)/squeeze | solution.py:375
  8.6 0.0 slice-start
  8.7 1.4 %collective-permute-start = (bf16[16,48,512]{2,1,0:T(8,128)(2,1)S(1)}, bf16[16,48,512]{2,1,0:T(8,128)(2,1)}, u32[]{:S(2)}, u32[]{:S(2)}) collective-permute-start(bf16[16,48,512]{2,1,0:T(8,128)(2,1)S(1)} %dynamic-slice_bitcast_fusion), channel_id=1, source_target_pairs={{2,0},{3,1},{4,2},{5,3},{6,4},{7,5},{8,6},{9,7},{10,8},{11,9},{12,... | collective-permute-start | bytes 2359304 | tf_op jit(solution)/shard_map/ppermute | solution.py:34
  10.1 0.1 copy.53
  10.3 0.9 %pad.31 = f32[2,16,8,128]{3,2,1,0:T(8,128)S(1)} pad(f32[2,16,8,48]{3,2,1,0:T(8,128)} %param.8, f32[]{:T(128)} %constant.82.clone.1), padding=0_0x0_0x0_0x0_80 | pad | bytes 180228 | tf_op jit(solution)/shard_map/jit(_pad)/pad | solution.py:415
  11.2 0.9 %broadcast_select_fusion.1.refs_1_.refs_2_ = f32[2,16,8,128]{3,2,1,0:T(8,128)S(1)} fusion(f32[2,16,8,128]{3,2,1,0:T(8,128)S(1)} %rev.12, pred[]{:T(512)S(6)} %eq.14, f32[2,16,8,48]{3,2,1,0:T(8,128)} %param.8), kind=kLoop, calls=%fused_computation.28 | loop fusion | flops 32768 | bytes 311297 | tf_op jit(solution)/shard_map/jit(_where)/select_n | solution.py:409
  12.2 0.0 copy-start
  12.2 0.9 %copy-done = bf16[288,240]{1,0:T(8,128)(2,1)S(1)} copy-done((bf16[288,240]{1,0:T(8,128)(2,1)S(1)}, bf16[288,240]{1,0:T(8,128)(2,1)}, u32[]{:S(2)}) %copy-start) | copy-done | bytes 138264
  13.1 0.9 %copy-done.2 = bf16[288,192]{1,0:T(8,128)(2,1)S(1)} copy-done((bf16[288,192]{1,0:T(8,128)(2,1)S(1)}, bf16[288,192]{1,0:T(8,128)(2,1)}, u32[]{:S(2)}) %copy-start.2) | copy-done | bytes 110616
  14.0 0.8 copy-done.4
  14.8 5.1 %inner0.1.refs_0_ = f32[512,1024]{1,0:T(8,128)} custom-call(s32[1]{0:T(128)} %bitcast.odd_ref, bf16[16,8,48,512]{3,2,1,0:T(8,128)(2,1)} %v_hbm.1, f32[2,16,8,128]{3,2,1,0:T(8,128)S(1)} %broadcast_select_fusion.1.refs_1_.refs_2_, bf16[288,192]{1,0:T(8,128)(2,1)S(1)} %copy-done.2, bf16[288,240]{1,0:T(8,128)(2,1)S(1)} %copy-done, bf16[96,144]{1,0:T(8,128)(2,1)S(1)} %copy-done.4), custom_call_target="tpu_custom_call" | custom-call | flops 1800000000 | bytes 2000000 | tf_op jit(solution)/shard_map/inner0/pallas_call | solution.py:326
  19.9 0.1 slice_select_fusion
  20.1 1.3 %collective-permute-start.2 = (bf16[408,512]{1,0:T(8,128)(2,1)S(1)}, bf16[408,512]{1,0:T(8,128)(2,1)S(1)}, u32[]{:S(2)}, u32[]{:S(2)}) collective-permute-start(bf16[408,512]{1,0:T(8,128)(2,1)S(1)} %maximum_maximum_fusion), channel_id=1, source_target_pairs={{32,0},{33,1},{34,2},{35,3},{36,4},{37,5},{38,6},{39,7},{40,8},{41... | collective-permute-start | bytes 1253384 | tf_op jit(solution)/shard_map/ppermute | solution.py:34
  21.5 0.0 copy-start.3
  21.5 0.0 copy-start.5
  21.5 8.6 %inner1.1.refs_0_ = f32[512,1024]{1,0:T(8,128)} custom-call(s32[1]{0:T(128)} %bitcast.odd_ref, f32[512,1024]{1,0:T(8,128)} %inner0.1.refs_0_, bf16[16,8,48,512]{3,2,1,0:T(8,128)(2,1)} %v_hbm.1, f32[2,16,8,128]{3,2,1,0:T(8,128)S(1)} %broadcast_select_fusion.1.refs_1_.refs_2_, bf16[288,192]{1,0:T(8,128)(2,1)S(1)} %copy-done.2, bf16[288,240]{1,0:T(8,128)(2,1)S(1)} %copy-done, ...), custom_call_target="tpu_custom_call" | custom-call | flops 3600000000 | bytes 4000000 | tf_op jit(solution)/shard_map/inner1/pallas_call | solution.py:326
  30.5 0.1 reverse_select_fusion
  30.6 1.5 %collective-permute-start.3 = (bf16[99,512]{1,0:T(8,128)(2,1)S(1)}, bf16[99,512]{1,0:T(8,128)(2,1)S(1)}, u32[]{:S(2)}, u32[]{:S(2)}) collective-permute-start(bf16[99,512]{1,0:T(8,128)(2,1)S(1)} %maximum_maximum_fusion.2), channel_id=1, source_target_pairs={{2,0},{3,1},{4,2},{5,3},{6,4},{7,5},{8,6},{9,7},{10,8},{11,9},{12,... | collective-permute-start | bytes 304136 | tf_op jit(solution)/shard_map/ppermute | solution.py:34
  32.1 8.6 %inner3.1.m_hbm = f32[512,1024]{1,0:T(8,128)} custom-call(s32[1]{0:T(128)} %bitcast.odd_ref, f32[512,1024]{1,0:T(8,128)} %inner1.1.refs_0_, bf16[16,8,48,512]{3,2,1,0:T(8,128)(2,1)} %v_hbm.1, f32[2,16,8,128]{3,2,1,0:T(8,128)S(1)} %broadcast_select_fusion.1.refs_1_.refs_2_, bf16[288,192]{1,0:T(8,128)(2,1)S(1)} %copy-done.3, bf16[288,240]{1,0:T(8,128)(2,1)S(1)} %copy-done.1, ...), custom_call_target="tpu_custom_call" | custom-call | flops 3600000000 | bytes 4000000 | tf_op jit(solution)/shard_map/inner3/pallas_call | solution.py:326
  40.7 0.0 copy-start.6
  40.7 0.0 copy-start.7
  40.8 0.1 fusion
  41.1 0.9 %constant_dynamic-slice_fusion.1 = bf16[16,1,512]{2,1,0:T(2,128)(2,1)S(1)} fusion(bf16[16,48,512]{2,1,0:T(8,128)(2,1)} %collective-permute-done.ym_hbm, s32[]{:T(128)S(6)} %select_n.70), kind=kLoop, calls=%fused_computation.70 | loop fusion | bytes 32772 | tf_op jit(solution)/shard_map/jit(dynamic_index_in_dim)/dynamic_slice | solution.py:375
  42.1 0.1 copy.35
  42.3 0.1 copy.38
  42.4 0.1 dynamic-slice_maximum_fusion
  42.5 0.1 copy.34
  42.7 0.1 dynamic-slice_maximum_fusion.1
  42.8 0.1 copy.33
  43.0 0.1 copy.37
  43.1 0.1 copy.36
  43.2 8.0 %outer.1 = (f32[256,512]{1,0:T(8,128)S(1)}, f32[256,512]{1,0:T(8,128)S(1)}, f32[256,512]{1,0:T(8,128)S(1)}, f32[256,512]{1,0:T(8,128)S(1)}) custom-call(s32[1]{0:T(128)} %bitcast.odd_ref, f32[512,1024]{1,0:T(8,128)} %inner3.1.m_hbm, bf16[16,8,48,512]{3,2,1,0:T(8,128)(2,1)} %v_hbm.1, bf16[408,512]{1,0:T(8,128)(2,1)S(1)} %collective-permute-done.2.vx_hbm, ...), custom_call_target="tpu_custom_call" | custom-call | flops 4000000000 | bytes 6000000 | tf_op jit(solution)/shard_map/outer/pallas_call | solution.py:349
  51.2 4.2 %collective-permute-start.4 = (f32[256,512]{1,0:T(8,128)S(1)}, f32[256,512]{1,0:T(8,128)S(1)}, u32[]{:S(2)}, u32[]{:S(2)}) collective-permute-start(f32[256,512]{1,0:T(8,128)S(1)} %get-tuple-element.21), channel_id=1, source_target_pairs={{0,32},{1,33},{2,34},{3,35},{4,36},{5,37},{6,38},{7,39},{8,40},{9,... | collective-permute-start | bytes 1572872 | tf_op jit(solution)/shard_map/ppermute | solution.py:34
  55.4 0.1 collective-permute-start.5
  55.5 1.4 %collective-permute-done.4 = f32[256,512]{1,0:T(8,128)S(1)} collective-permute-done((f32[256,512]{1,0:T(8,128)S(1)}, f32[256,512]{1,0:T(8,128)S(1)}, u32[]{:S(2)}, u32[]{:S(2)}) %collective-permute-start.4) | collective-permute-done | bytes 524320 | tf_op jit(solution)/shard_map/ppermute | solution.py:34
  57.0 0.1 add.69
  57.0 0.7 collective-permute-done.5
  57.7 0.1 add.70
  57.8 0.1 pad_maximum_fusion
  57.9 0.3 reshape.55
  58.2 29.3 %all_to_all.5 = f32[64,4,1024]{2,1,0:T(4,128)S(1)} all-to-all(f32[64,4,1024]{2,1,0:T(4,128)S(1)} %reshape.55), channel_id=1, replica_groups={{0,1,2,3,4,5,6,7,8,9,10,11,12,13,14,15,16,17,18,19,20,21,22,23,24,25,26..., dimensions={0} | all-to-all | bytes 2097152 | tf_op jit(solution)/shard_map/all_to_all | solution.py:382
  87.5 0.2 reduce_sum.9
  87.7 0.6 fusion.8
  (69 shorter events, 0.8 us)
Async XLA Ops:
  3.4 16.5 %collective-permute-start.1 = (bf16[144,512]{1,0:T(8,128)(2,1)S(1)}, bf16[144,512]{1,0:T(8,128)(2,1)S(1)}, u32[]{:S(2)}, u32[]{:S(2)}) collective-permute-start(bf16[144,512]{1,0:T(8,128)(2,1)S(1)} %maximum_maximum_fusion.1), channel_id=1, source_target_pairs={{0,1},{1,0},{2,3},{3,2},{4,5},{5,4},{6,7},{7,6},{8,9},{9,8},{10,11... | collective-permute-start | bytes 442376 | tf_op jit(solution)/shard_map/ppermute | solution.py:34
  7.4 12.5 %copy-start.8 = (f32[2,16,8,48]{3,2,1,0:T(8,128)S(1)}, f32[2,16,8,48]{3,2,1,0:T(8,128)}, u32[]{:S(2)}) copy-start(f32[2,16,8,48]{3,2,1,0:T(8,128)} %param.8) | copy-start | bytes 147460
  8.6 11.4 %slice-start = ((bf16[16,8,48,512]{3,2,1,0:T(8,128)(2,1)}), bf16[1,8,48,512]{3,2,1,0:T(8,128)(2,1)S(1)}, s32[]{:S(2)}) async-start(bf16[16,8,48,512]{3,2,1,0:T(8,128)(2,1)} %v_hbm.1), calls=%async_computation.1 | async-start | bytes 786432 | tf_op jit(solution)/shard_map/slice | solution.py:425
  8.7 32.1 %collective-permute-start = (bf16[16,48,512]{2,1,0:T(8,128)(2,1)S(1)}, bf16[16,48,512]{2,1,0:T(8,128)(2,1)}, u32[]{:S(2)}, u32[]{:S(2)}) collective-permute-start(bf16[16,48,512]{2,1,0:T(8,128)(2,1)S(1)} %dynamic-slice_bitcast_fusion), channel_id=1, source_target_pairs={{2,0},{3,1},{4,2},{5,3},{6,4},{7,5},{8,6},{9,7},{10,8},{11,9},{12,... | collective-permute-start | bytes 2359304 | tf_op jit(solution)/shard_map/ppermute | solution.py:34
  12.2 0.9 %copy-start = (bf16[288,240]{1,0:T(8,128)(2,1)S(1)}, bf16[288,240]{1,0:T(8,128)(2,1)}, u32[]{:S(2)}) copy-start(bf16[288,240]{1,0:T(8,128)(2,1)} %constant.89.clone.refs_3_.refs_4_.band1) | copy-start | bytes 414724
  13.1 0.9 %copy-start.2 = (bf16[288,192]{1,0:T(8,128)(2,1)S(1)}, bf16[288,192]{1,0:T(8,128)(2,1)}, u32[]{:S(2)}) copy-start(bf16[288,192]{1,0:T(8,128)(2,1)} %constant.88.clone.refs_2_.refs_3_.band0) | copy-start | bytes 331780
  14.0 0.8 copy-start.4
  20.1 10.0 %collective-permute-start.2 = (bf16[408,512]{1,0:T(8,128)(2,1)S(1)}, bf16[408,512]{1,0:T(8,128)(2,1)S(1)}, u32[]{:S(2)}, u32[]{:S(2)}) collective-permute-start(bf16[408,512]{1,0:T(8,128)(2,1)S(1)} %maximum_maximum_fusion), channel_id=1, source_target_pairs={{32,0},{33,1},{34,2},{35,3},{36,4},{37,5},{38,6},{39,7},{40,8},{41... | collective-permute-start | bytes 1253384 | tf_op jit(solution)/shard_map/ppermute | solution.py:34
  21.4 10.6 %copy-start.1 = (bf16[288,240]{1,0:T(8,128)(2,1)S(1)}, bf16[288,240]{1,0:T(8,128)(2,1)}, u32[]{:S(2)}) copy-start(bf16[288,240]{1,0:T(8,128)(2,1)} %constant.89.clone.refs_3_.refs_4_.band1) | copy-start | bytes 414724
  21.5 10.6 %copy-start.3 = (bf16[288,192]{1,0:T(8,128)(2,1)S(1)}, bf16[288,192]{1,0:T(8,128)(2,1)}, u32[]{:S(2)}) copy-start(bf16[288,192]{1,0:T(8,128)(2,1)} %constant.88.clone.refs_2_.refs_3_.band0) | copy-start | bytes 331780
  21.5 10.6 %copy-start.5 = (bf16[96,144]{1,0:T(8,128)(2,1)S(1)}, bf16[96,144]{1,0:T(8,128)(2,1)}, u32[]{:S(2)}) copy-start(bf16[96,144]{1,0:T(8,128)(2,1)} %constant.90.clone.refs_4_.refs_5_.band2) | copy-start | bytes 82948
  30.6 10.1 %collective-permute-start.3 = (bf16[99,512]{1,0:T(8,128)(2,1)S(1)}, bf16[99,512]{1,0:T(8,128)(2,1)S(1)}, u32[]{:S(2)}, u32[]{:S(2)}) collective-permute-start(bf16[99,512]{1,0:T(8,128)(2,1)S(1)} %maximum_maximum_fusion.2), channel_id=1, source_target_pairs={{2,0},{3,1},{4,2},{5,3},{6,4},{7,5},{8,6},{9,7},{10,8},{11,9},{12,... | collective-permute-start | bytes 304136 | tf_op jit(solution)/shard_map/ppermute | solution.py:34
  40.7 2.5 %copy-start.6 = (bf16[448,224]{1,0:T(8,128)(2,1)S(1)}, bf16[448,224]{1,0:T(8,128)(2,1)}, u32[]{:S(2)}) copy-start(bf16[448,224]{1,0:T(8,128)(2,1)} %constant.92.clone.bandz) | copy-start | bytes 602116
  40.7 2.5 %copy-start.7 = (bf16[192,144]{1,0:T(8,128)(2,1)S(1)}, bf16[192,144]{1,0:T(8,128)(2,1)}, u32[]{:S(2)}) copy-start(bf16[192,144]{1,0:T(8,128)(2,1)} %constant.91.clone.band3) | copy-start | bytes 165892
  51.2 5.7 %collective-permute-start.4 = (f32[256,512]{1,0:T(8,128)S(1)}, f32[256,512]{1,0:T(8,128)S(1)}, u32[]{:S(2)}, u32[]{:S(2)}) collective-permute-start(f32[256,512]{1,0:T(8,128)S(1)} %get-tuple-element.21), channel_id=1, source_target_pairs={{0,32},{1,33},{2,34},{3,35},{4,36},{5,37},{6,38},{7,39},{8,40},{9,... | collective-permute-start | bytes 1572872 | tf_op jit(solution)/shard_map/ppermute | solution.py:34
  55.4 2.3 %collective-permute-start.5 = (f32[256,512]{1,0:T(8,128)S(1)}, f32[256,512]{1,0:T(8,128)S(1)}, u32[]{:S(2)}, u32[]{:S(2)}) collective-permute-start(f32[256,512]{1,0:T(8,128)S(1)} %get-tuple-element.23), channel_id=1, source_target_pairs={{0,32},{1,33},{2,34},{3,35},{4,36},{5,37},{6,38},{7,39},{8,40},{9,... | collective-permute-start | bytes 1572872 | tf_op jit(solution)/shard_map/ppermute | solution.py:34

commit v6 on v5

--- a/solution.py
+++ b/solution.py
@@ -16,7 +16,7 @@
 BATCH = 3
 FACE = 224
 MAIN = 15 * OUTER + 18 * SZ
-PIECES = ((0, 1), (1, 3), (3, 5))
+PIECES = ((0, 1), (1, 2), (2, 5))
 
 
 def linear(x, y, z):
@@ -110,19 +110,45 @@
     return c + odd * (7 - 2 * c)
 
 
-def inner_kernel(first, last, odd_ref, m_hbm, v_hbm, mat_ref, band0, band1, band2, out_hbm, ve, w2, t2, u, acc, sem, sem_m):
+def mirror(x):
+    rows = lax.broadcasted_iota(jnp.int32, x.shape, 0)
+    for s in (4, 2, 1):
+        x = jnp.where(rows % (2 * s) < s, pltpu.roll(x, 8 - s, 0), pltpu.roll(x, s, 0))
+    return x
+
+
+def inner_kernel(
+    first, last, odd_ref, m_hbm, v_hbm, raw_hbm, hbm0, hbm1, hbm2, out_hbm,
+    ve, w2, t2, u, acc, raw, mat_ref, band0, band1, band2, sem, sem_m,
+):
     odd = odd_ref[0]
     bands = (band0, band1, band2)
     low = max(BATCH * first - 1, 0)
     loads = {
         p: pltpu.make_async_copy(v_hbm.at[p], ve.at[p - low], sem.at[p - low]) for p in range(low, BATCH * last + 1)
     }
-    for p in loads:
+    side = [
+        pltpu.make_async_copy(a, b, sem_m.at[5 + n])
+        for n, (a, b) in enumerate(((hbm0, band0), (hbm1, band1), (hbm2, band2), (raw_hbm, raw)))
+    ]
+    loads[low].start()
+    for load in side:
+        load.start()
+    for p in range(low + 1, BATCH * last + 1):
         loads[p].start()
     place = [line_index(odd, c) for c in range(8)]
     if m_hbm is not None:
         load_m = pltpu.make_async_copy(m_hbm, acc, sem_m.at[4])
         load_m.start()
+    side[3].wait()
+    for i in range(2):
+        for p in range(low, BATCH * last + 1):
+            mat_ref[i, p] = jnp.zeros((SY, 128), jnp.float32)
+            mat_ref[i, p, :, 0:SZ] = raw[i, p]
+            x = mat_ref[i, p]
+            mat_ref[i, p] = jnp.where(odd == 1, mirror(x), x)
+    for load in side[:3]:
+        load.wait()
     yz = {}
 
     def kappa_of(p):
@@ -181,26 +207,33 @@
 
 
 def outer_kernel(
-    odd_ref, m_hbm, v_hbm, vx_hbm, ym_hbm, ye_hbm, zf_ref, zh_ref, face_ref, mat_ref,
-    band0, band1, band2, band3, bandz, keep_s, send_s, keep_m, send_m,
-    v6, v7, v8, vp, w78, t78, w06, t06, u, sem, acc, res,
+    odd_ref, m_hbm, v_hbm, vx_hbm, vy_hbm, hbm0, hbm1, hbm2, hbm3, hbmz, zf_ref, zh_ref, face_ref, mat_ref,
+    keep_s, send_s, keep_m, send_m,
+    v6, v7, v8, vp, zl, w78, t78, w06, t06, u, sem, acc, res, band0, band1, band2, band3, bandz,
 ):
     odd = odd_ref[0]
     bands = (band0, band1, band2)
     loads = [
         pltpu.make_async_copy(v_hbm.at[pl.ds(0, 14), line_index(odd, 6)], v6, sem.at[0]),
         pltpu.make_async_copy(v_hbm.at[pl.ds(0, 14), line_index(odd, 7)], v7, sem.at[1]),
-        pltpu.make_async_copy(ym_hbm, v8.at[pl.ds(0, 16)], sem.at[2]),
+        pltpu.make_async_copy(vy_hbm.at[pl.ds(0, 17 * SZ)], v8, sem.at[2]),
         pltpu.make_async_copy(v_hbm.at[pl.ds(14, 2)], vp.at[pl.ds(0, 2)], sem.at[3]),
-        pltpu.make_async_copy(ye_hbm.at[pl.ds(0, SZ)], v8.at[16], sem.at[4]),
     ]
     for y in range(SY):
         loads.append(pltpu.make_async_copy(vx_hbm.at[pl.ds(y * SZ, SZ)], vp.at[2, y], sem.at[5 + y]))
     place = [line_index(odd, c) for c in range(8)]
     load_m = pltpu.make_async_copy(m_hbm, acc, sem.at[13])
-    for load in loads + [load_m]:
+    early = [
+        pltpu.make_async_copy(hbmz, bandz, sem.at[14]),
+        pltpu.make_async_copy(vy_hbm.at[pl.ds(17 * SZ, 64)], zl, sem.at[15]),
+    ]
+    for n, (a, b) in enumerate(((hbm0, band0), (hbm1, band1), (hbm2, band2), (hbm3, band3))):
+        loads.append(pltpu.make_async_copy(a, b, sem.at[16 + n]))
+    for load in early + loads + [load_m]:
         load.start()
-    wz, tz = apply_band(bandz[...], [zh_ref[...]], FACE)
+    for load in early:
+        load.wait()
+    wz, tz = apply_band(bandz[...], [zh_ref[...], zl[32:64]], FACE)
     kap_face, rho_face, kap_halo = face_ref[0], face_ref[1], face_ref[2]
     planes = lax.broadcasted_iota(jnp.int32, kap_halo.shape, 0)
     lines = lax.broadcasted_iota(jnp.int32, kap_halo.shape, 1)
@@ -215,7 +248,7 @@
         parts = [jnp.broadcast_to(grid[:, l : l + 1], (24, K)) for l in range(9)]
         return jnp.concatenate(parts + [jnp.zeros((8, K), jnp.float32)], axis=0)
 
-    zf = zf_ref[...]
+    zf = jnp.concatenate([zf_ref[...], zl[0:32]], axis=0)
     uz = jnp.concatenate([column(f) * zf.astype(jnp.float32) - column(kap_face) * wz, column(rho_face) * tz], axis=1)
     u[MAIN:] = uz.astype(jnp.bfloat16)
     for load in loads:
@@ -223,7 +256,7 @@
 
     def line(p, l):
         if l == 8:
-            return v8[p]
+            return v8[p * SZ : (p + 1) * SZ]
         if p >= 14:
             return vp[p - 14, place[l]]
         return v7[p] if l == 7 else v6[p]
@@ -322,7 +355,7 @@
 
     planes = BATCH * (last - first) + (2 if first else 1)
     operands = (odd,) + (() if m is None else (m,)) + (v, mat) + tuple(bands)
-    specs = [SMEM] + ([] if m is None else [HBM]) + [HBM] + [VMEM] * 4
+    specs = [SMEM] + [HBM] * (len(operands) - 1)
     return pl.pallas_call(
         body,
         out_shape=pltpu.HBM((K, 2 * K), jnp.float32),
@@ -334,8 +367,13 @@
             pltpu.VMEM((4, INNER, K), jnp.float32),
             pltpu.VMEM((2, BATCH * INNER, 2 * K), jnp.bfloat16),
             pltpu.VMEM((K, 2 * K), jnp.float32),
+            pltpu.VMEM((2, SX, SY, SZ), jnp.float32),
+            pltpu.VMEM((2, SX, SY, 128), jnp.float32),
+            pltpu.VMEM((6 * SZ, 4 * SZ), jnp.bfloat16),
+            pltpu.VMEM((6 * SZ, 5 * SZ), jnp.bfloat16),
+            pltpu.VMEM((2 * SZ, 3 * SZ), jnp.bfloat16),
             pltpu.SemaphoreType.DMA((planes,)),
-            pltpu.SemaphoreType.DMA((5,)),
+            pltpu.SemaphoreType.DMA((9,)),
         ],
         compiler_params=pltpu.CompilerParams(vmem_limit_bytes=26 * 1024 * 1024),
         cost_estimate=pl.CostEstimate(
@@ -345,30 +383,36 @@
     )(*operands)
 
 
-def outer_part(odd, m, v, vx, ym, ye, zf, zh, face, mat, bands):
+def outer_part(odd, m, v, vx, vy, bands, zf, zh, face, mat):
     return pl.pallas_call(
         outer_kernel,
         out_shape=[jax.ShapeDtypeStruct((K // 2, K), jnp.float32)] * 4,
-        in_specs=[SMEM, HBM, HBM, HBM, HBM, HBM] + [VMEM] * 9,
+        in_specs=[SMEM] + [HBM] * 9 + [VMEM] * 4,
         out_specs=[VMEM] * 4,
         scratch_shapes=[
             pltpu.VMEM((14, SZ, K), jnp.bfloat16),
             pltpu.VMEM((14, SZ, K), jnp.bfloat16),
-            pltpu.VMEM((17, SZ, K), jnp.bfloat16),
+            pltpu.VMEM((17 * SZ, K), jnp.bfloat16),
             pltpu.VMEM((3, SY, SZ, K), jnp.bfloat16),
+            pltpu.VMEM((64, K), jnp.bfloat16),
             pltpu.VMEM((17, OUTER, K), jnp.float32),
             pltpu.VMEM((17, OUTER, K), jnp.float32),
             pltpu.VMEM((3, INNER, K), jnp.float32),
             pltpu.VMEM((3, INNER, K), jnp.float32),
             pltpu.VMEM((MAIN + FACE, 2 * K), jnp.bfloat16),
-            pltpu.SemaphoreType.DMA((14,)),
+            pltpu.SemaphoreType.DMA((20,)),
             pltpu.VMEM((K, 2 * K), jnp.float32),
             pltpu.VMEM((2, 2, K // 2, K), jnp.float32),
+            pltpu.VMEM((6 * SZ, 4 * SZ), jnp.bfloat16),
+            pltpu.VMEM((6 * SZ, 5 * SZ), jnp.bfloat16),
+            pltpu.VMEM((2 * SZ, 3 * SZ), jnp.bfloat16),
+            pltpu.VMEM((4 * SZ, 3 * SZ), jnp.bfloat16),
+            pltpu.VMEM((2 * FACE, FACE), jnp.bfloat16),
         ],
         compiler_params=pltpu.CompilerParams(vmem_limit_bytes=32 * 1024 * 1024),
         cost_estimate=pl.CostEstimate(flops=4_000_000_000, transcendentals=0, bytes_accessed=6_000_000),
         name="outer",
-    )(odd, m, v, vx, ym, ye, zf, zh, face, mat, *bands)
+    )(odd, m, v, vx, vy, *bands, zf, zh, face, mat)
 
 
 def pick(x, index, dim):
@@ -394,6 +438,10 @@
 def from_parts(rows):
     x = rows.astype(jnp.float32)
     return (x[:, 256:384] + x[:, 128:256]) + x[:, :128]
+
+
+def face_rows(rows):
+    return jnp.pad(rows.transpose(1, 0, 2), ((0, 0), (0, 7), (0, 0))).reshape(192, K)
 
 
 def per_device(eigvecs, material):
@@ -408,50 +456,45 @@
     def chain(x, dim):
         return jnp.where(odd, lax.rev(x, (dim,)), x)
 
-    ym = send(pick(eigvecs, side, 1), to_y)
     zf = pick(eigvecs, face, 2)
     kface = jnp.pad(pick(material[0], face, 2), ((0, 0), (0, 120)))
     zm = send(jnp.concatenate([zf.reshape(SX * SY, K), to_parts(kface)], axis=0), to_z)
-    own = jnp.pad(material, ((0, 0), (0, 0), (0, 0), (0, 128 - SZ)))
-    mat = chain(own, 2)
-    bands = [band_matrix(ins, outs) for ins, outs in NEAR]
-    m = inner_part(*PIECES[0], odd_flag, None, vectors, mat, bands)
+    bands = [in_hbm(band_matrix(ins, outs)) for ins, outs in NEAR]
+    raw = in_hbm(material)
+    m = inner_part(*PIECES[0], odd_flag, None, vectors, raw, bands)
     zm, m = lax.optimization_barrier((zm, m))
     zh = zm[: SX * SY].reshape(SX, SY, K)
     kz = from_parts(zm[SX * SY :])[:, :SY]
     lanes = jnp.arange(128)
+    own = jnp.pad(material, ((0, 0), (0, 0), (0, 0), (0, 128 - SZ)))
     matz = jnp.stack([jnp.where(lanes == 64, kz[..., None], own[0]), own[1]])
-    vx = send(
-        jnp.concatenate([eigvecs[0].reshape(SY * SZ, K), zh[0], to_parts(matz[:, 0].reshape(16, 128))], axis=0),
-        to_x,
-    )
-    m = inner_part(*PIECES[1], odd_flag, in_hbm(m), vectors, mat, bands)
+    plane = eigvecs[0].reshape(SY * SZ, K)
+    vx = send(jnp.concatenate([plane, zf[0], zh[0], to_parts(matz[:, 0].reshape(16, 128))], axis=0), to_x)
+    m = inner_part(*PIECES[1], odd_flag, in_hbm(m), vectors, raw, bands)
     vx, m = lax.optimization_barrier((vx, m))
-    xz = vx[SY * SZ : SY * SZ + SY]
-    matz = jnp.concatenate([matz, from_parts(vx[SY * SZ + SY :]).reshape(2, 1, SY, 128)], axis=1)
-    matz = chain(matz, 2)
+    at = SY * SZ
+    xf, xz = vx[at : at + SY], vx[at + SY : at + 2 * SY]
+    xmat = from_parts(vx[at + 2 * SY :]).reshape(2, 1, SY, 128)
+    matz = chain(jnp.concatenate([matz, xmat], axis=1), 2)
+    frows = chain(jnp.concatenate([zf, xf[None]], axis=0), 1)
     zrows = chain(jnp.concatenate([zh, xz[None]], axis=0), 1)
+    lines = pick(eigvecs, side, 1).reshape(SX * SZ, K)
     xline = lax.dynamic_slice_in_dim(vx, side * SZ, SZ, 0)
-    ye = send(jnp.concatenate([xline, zrows[:, 0], to_parts(matz[:, :, 0].reshape(34, 128))], axis=0), to_y)
-    m = inner_part(*PIECES[2], odd_flag, in_hbm(m), vectors, mat, bands)
-    ym, ye, m = lax.optimization_barrier((ym, ye, m))
-    my = from_parts(ye[SZ + 17 :]).reshape(2, 17, 1, 128)
+    gap = jnp.zeros((15, K), jnp.bfloat16)
+    parts = to_parts(matz[:, :, 0].reshape(34, 128))
+    vy = send(jnp.concatenate([lines, xline, frows[:, 0], gap, zrows[:, 0], gap, parts], axis=0), to_y)
+    zf = face_rows(frows)
+    zh = face_rows(zrows)
+    m = inner_part(*PIECES[2], odd_flag, in_hbm(m), vectors, raw, bands)
+    vy, m, zf, zh = lax.optimization_barrier((vy, m, zf, zh))
+    my = from_parts(vy[17 * SZ + 64 :]).reshape(2, 17, 1, 128)
     matz = jnp.concatenate([matz, my], axis=2)
     grids = jnp.stack([pick(matz[0], face, 2), pick(matz[1], face, 2), matz[0, :, :, 64]])
     grids = jnp.pad(grids, ((0, 0), (0, 7), (0, 119)))
     mat = jnp.pad(matz, ((0, 0), (0, 0), (0, 7), (0, 0)))
     mat = jnp.where(lanes < SZ, mat, 0.0)
-
-    def face_rows(main, line):
-        rows = jnp.concatenate([main, line[:, None]], axis=1).transpose(1, 0, 2)
-        return jnp.pad(jnp.pad(rows, ((0, 0), (0, 7), (0, 0))).reshape(216, K), ((0, FACE - 216), (0, 0)))
-
-    xf = pick(vx[: SY * SZ].reshape(SY, SZ, K), face, 1)
-    yf = jnp.concatenate([pick(ym, face, 1), lax.dynamic_slice_in_dim(ye, face, 1, 0)], axis=0)
-    zf = face_rows(chain(jnp.concatenate([zf, xf[None]], axis=0), 1), yf)
-    zh = face_rows(zrows, ye[SZ : SZ + 17])
-    bands = bands + [band_matrix(*EDGE), face_matrix()]
-    part = outer_part(odd_flag, in_hbm(m), vectors, vx, in_hbm(ym), ye, zf, zh, grids, mat, bands)
+    bands = bands + [in_hbm(band_matrix(*EDGE)), in_hbm(face_matrix())]
+    part = outer_part(odd_flag, in_hbm(m), vectors, vx, vy, bands, zf, zh, grids, mat)
     total = SX * SY * SZ * NGX * NGY * NGZ
     summed = reduce_to_owner(part) * (0.5 / total)
     return summed[:, :K], summed[:, K:]

time: 88.8 us -> 82.3 us (0.927)
  local copies, waits for them, and re-layouts: 10.6 us -> 6.44 us
  starting transfers between devices: 12.6 us -> 8.8 us
  Pallas kernels: 30.2 us -> 32.2 us
  waiting for transfers between devices: 2.12 us -> 3.74 us
  other arithmetic: 2.24 us -> 1.24 us
  blocking collectives: 29.3 us -> 28.4 us
    ppermute x6 -> x5, starting transfers between devices: 12.6 us -> 8.8 us  [send(): return lax.ppermute(value, ALL, links)]
    unnamed x22 -> x5, local copies, waits for them, and re-layouts: 2.73 us -> 0.09 us
    pallas_call x3, Pallas kernels: 22.2 us -> 24.1 us  [inner_part(): pl.pallas_call(body, out_shape=pltpu.HBM((K, 2 * K), jnp.float32), in_spe...]
    ppermute x6 -> x5, waiting for transfers between devices: 2.12 us -> 3.74 us  [send(): return lax.ppermute(value, ALL, links)]
    squeeze x2, local copies, waits for them, and re-layouts: 1.38 us -> 0.31 us  [pick(): return lax.dynamic_index_in_dim(x, index, dim, keepdims=False)]
    pad x5 -> x2, local copies, waits for them, and re-layouts: 0.99 us -> 0.04 us  [face_rows(): jnp.pad(rows.transpose(1, 0, 2), ((0, 0), (0, 7), (0, 0))).reshape(192, K)]
    all_to_all x1, blocking collectives: 29.3 us -> 28.4 us  [reduce_to_owner(): lax.all_to_all(blocks, ALL, 0, 0, tiled=True, axis_index_groups=groups)]
    select_n x3 -> x2, other arithmetic: 1.01 us -> 0.09 us  [chain(): return jnp.where(odd, lax.rev(x, (dim,)), x)]
  transfers between devices with their start and end apart: 6 -> 5, of which waited for: 2 -> 3; matrix products, arithmetic and copies ran while one was open for 4% -> 2% of each run, Pallas kernels for 25% -> 29%
where the time goes in v6:
time: 82.3 us; the launch traced here: 82 us
  Pallas kernels  32.2 us (39%)
  blocking collectives  28.4 us (35%)
  starting transfers between devices  8.8 us (11%)
  local copies, waits for them, and re-layouts  6.44 us (8%)
  waiting for transfers between devices  3.74 us (5%)
  other arithmetic  1.24 us (2%)
  between operations  1.15 us (1%)
    all_to_all x1, blocking collectives, reduce_to_owner(): lax.all_to_all(blocks, ALL, 0, 0, tiled=True, axis_index_groups=groups)  28.4 us
    pallas_call x3, Pallas kernels, inner_part(): pl.pallas_call(body, out_shape=pltpu.HBM((K, 2 * K), jnp.float32), in_spe...  24.1 us
    ppermute x5, starting transfers between devices, send(): return lax.ppermute(value, ALL, links)  8.8 us
    pallas_call x1, Pallas kernels, outer_part(): pl.pallas_call(outer_kernel, out_shape=[jax.ShapeDtypeStruct((K // 2, K),...  8.14 us
    ppermute x5, waiting for transfers between devices, send(): return lax.ppermute(value, ALL, links)  3.74 us
    dynamic_slice x5, local copies, waits for them, and re-layouts, pick(): return lax.dynamic_index_in_dim(x, index, dim, keepdims=False)  3.1 us
  transfers between devices with their start and end apart: 5, of which 3 were waited for; matrix products, arithmetic and copies ran while one was open for 2% of the time, Pallas kernels for 29%

profile of v6, /device:TPU:0, one launch (start us, length us, event | category | flops | bytes accessed | tf_op | source)
XLA Modules:
  0.0 82.0 jit_solution(4617545298927184988)
XLA Ops:
  0.6 0.8 %slice.98 = f32[1,16,8,48]{3,2,1,0:T(8,128)S(1)} slice(f32[2,16,8,48]{3,2,1,0:T(8,128)} %refs_2_.4), slice={[0:1], [0:16], [0:8], [0:48]} | slice | bytes 49152 | tf_op jit(solution)/shard_map/slice | solution.py:460
  1.5 0.1 constant_dynamic-slice_fusion.1
  1.6 0.2 copy.42
  1.7 1.5 %constant_dynamic-slice_fusion.2 = bf16[16,8,1,512]{3,2,1,0:T(2,128)(2,1)S(1)} fusion(bf16[16,8,48,512]{3,2,1,0:T(8,128)(2,1)} %v_hbm.1, s32[]{:T(128)S(6)} %select_n.57), kind=kLoop, calls=%fused_computation.67 | loop fusion | bytes 262148 | tf_op jit(solution)/shard_map/jit(dynamic_index_in_dim)/dynamic_slice | solution.py:419
  3.3 0.0 copy-start
  3.4 4.1 %collective-permute-start = (bf16[144,512]{1,0:T(8,128)(2,1)S(1)}, bf16[144,512]{1,0:T(8,128)(2,1)S(1)}, u32[]{:S(2)}, u32[]{:S(2)}) collective-permute-start(bf16[144,512]{1,0:T(8,128)(2,1)S(1)} %maximum_maximum_fusion.1), channel_id=1, source_target_pairs={{0,1},{1,0},{2,3},{3,2},{4,5},{5,4},{6,7},{7,6},{8,9},{9,8},{10,11... | collective-permute-start | bytes 442376 | tf_op jit(solution)/shard_map/ppermute | solution.py:34
  7.4 0.0 slice-start
  7.5 5.6 %inner0.1.refs_0_ = f32[512,1024]{1,0:T(8,128)} custom-call(s32[1]{0:T(128)} %bitcast.odd_ref, bf16[16,8,48,512]{3,2,1,0:T(8,128)(2,1)} %v_hbm.1, f32[2,16,8,48]{3,2,1,0:T(8,128)} %refs_2_.4, bf16[288,192]{1,0:T(8,128)(2,1)} %constant.80.clone.refs_2_.refs_3_.hbm0, bf16[288,240]{1,0:T(8,128)(2,1)} %constant.81.clone.refs_3_.refs_4_.hbm1, ...), custom_call_target="tpu_custom_call" | custom-call | flops 1800000000 | bytes 2000000 | tf_op jit(solution)/shard_map/inner0/pallas_call | solution.py:359
  13.1 0.1 copy.48
  13.2 1.2 %constant_dynamic-slice_fusion.3 = bf16[16,1,48,512]{3,2,1,0:T(8,128)(2,1)S(1)} fusion(bf16[16,8,48,512]{3,2,1,0:T(8,128)(2,1)} %v_hbm.1, s32[]{:T(128)S(6)} %select_n.56), kind=kLoop, calls=%fused_computation.68 | loop fusion | bytes 1572868 | tf_op jit(solution)/shard_map/jit(dynamic_index_in_dim)/dynamic_slice | solution.py:419
  14.4 0.0 collective-permute-done
  14.5 0.0 copy-done
  14.5 0.1 fusion.1
  14.6 0.0 slice-done
  14.7 1.3 %collective-permute-start.1 = (bf16[416,512]{1,0:T(8,128)(2,1)S(1)}, bf16[416,512]{1,0:T(8,128)(2,1)S(1)}, u32[]{:S(2)}, u32[]{:S(2)}) collective-permute-start(bf16[416,512]{1,0:T(8,128)(2,1)S(1)} %maximum_maximum_fusion), channel_id=1, source_target_pairs={{32,0},{33,1},{34,2},{35,3},{36,4},{37,5},{38,6},{39,7},{40,8},{41... | collective-permute-start | bytes 1277960 | tf_op jit(solution)/shard_map/ppermute | solution.py:34
  16.0 6.2 %inner1.1.refs_0_ = f32[512,1024]{1,0:T(8,128)} custom-call(s32[1]{0:T(128)} %bitcast.odd_ref, f32[512,1024]{1,0:T(8,128)} %inner0.1.refs_0_, bf16[16,8,48,512]{3,2,1,0:T(8,128)(2,1)} %v_hbm.1, f32[2,16,8,48]{3,2,1,0:T(8,128)} %refs_2_.4, bf16[288,192]{1,0:T(8,128)(2,1)} %constant.80.clone.refs_2_.refs_3_.hbm0, ...), custom_call_target="tpu_custom_call" | custom-call | flops 1800000000 | bytes 2000000 | tf_op jit(solution)/shard_map/inner1/pallas_call | solution.py:359
  22.3 0.0 collective-permute-done.1.vx_hbm
  22.4 0.1 reverse_select_fusion
  22.7 0.5 concatenate.44
  23.2 1.5 %collective-permute-start.2 = (bf16[914,512]{1,0:T(8,128)(2,1)S(1)}, bf16[914,512]{1,0:T(8,128)(2,1)S(1)}, u32[]{:S(2)}, u32[]{:S(2)}) collective-permute-start(bf16[914,512]{1,0:T(8,128)(2,1)S(1)} %concatenate.44), channel_id=1, source_target_pairs={{2,0},{3,1},{4,2},{5,3},{6,4},{7,5},{8,6},{9,7},{10,8},{11,9},{12,... | collective-permute-start | bytes 2807816 | tf_op jit(solution)/shard_map/ppermute | solution.py:34
  24.8 12.3 %inner2.1.m_hbm = f32[512,1024]{1,0:T(8,128)} custom-call(s32[1]{0:T(128)} %bitcast.odd_ref, f32[512,1024]{1,0:T(8,128)} %inner1.1.refs_0_, bf16[16,8,48,512]{3,2,1,0:T(8,128)(2,1)} %v_hbm.1, f32[2,16,8,48]{3,2,1,0:T(8,128)} %refs_2_.4, bf16[288,192]{1,0:T(8,128)(2,1)} %constant.80.clone.refs_2_.refs_3_.hbm0, ...), custom_call_target="tpu_custom_call" | custom-call | flops 5400000000 | bytes 6000000 | tf_op jit(solution)/shard_map/inner2/pallas_call | solution.py:359
  37.1 1.6 %collective-permute-done.2.vy_hbm = bf16[914,512]{1,0:T(8,128)(2,1)S(1)} collective-permute-done((bf16[914,512]{1,0:T(8,128)(2,1)S(1)}, bf16[914,512]{1,0:T(8,128)(2,1)S(1)}, u32[]{:S(2)}, u32[]{:S(2)}) %collective-permute-start.2) | collective-permute-done | bytes 935968 | tf_op jit(solution)/shard_map/ppermute | solution.py:34
  38.8 0.1 fusion
  39.0 0.1 copy.34
  39.1 0.1 copy.37
  39.2 0.1 dynamic-slice_maximum_fusion
  39.3 0.1 copy.33
  39.5 0.1 dynamic-slice_maximum_fusion.1
  39.6 0.1 copy.32
  39.8 0.1 copy.36
  39.9 0.1 copy.35
  40.0 8.1 %outer.1 = (f32[256,512]{1,0:T(8,128)S(1)}, f32[256,512]{1,0:T(8,128)S(1)}, f32[256,512]{1,0:T(8,128)S(1)}, f32[256,512]{1,0:T(8,128)S(1)}) custom-call(s32[1]{0:T(128)} %bitcast.odd_ref, f32[512,1024]{1,0:T(8,128)} %inner2.1.m_hbm, bf16[16,8,48,512]{3,2,1,0:T(8,128)(2,1)} %v_hbm.1, bf16[416,512]{1,0:T(8,128)(2,1)S(1)} %collective-permute-done.1.vx_hbm, ...), custom_call_target="tpu_custom_call" | custom-call | flops 4000000000 | bytes 6000000 | tf_op jit(solution)/shard_map/outer/pallas_call | solution.py:387
  48.2 1.9 %collective-permute-start.3 = (f32[256,512]{1,0:T(8,128)S(1)}, f32[256,512]{1,0:T(8,128)S(1)}, u32[]{:S(2)}, u32[]{:S(2)}) collective-permute-start(f32[256,512]{1,0:T(8,128)S(1)} %get-tuple-element.23), channel_id=1, source_target_pairs={{0,32},{1,33},{2,34},{3,35},{4,36},{5,37},{6,38},{7,39},{8,40},{9,... | collective-permute-start | bytes 1572872 | tf_op jit(solution)/shard_map/ppermute | solution.py:34
  50.0 0.1 collective-permute-start.4
  50.1 1.4 %collective-permute-done.3 = f32[256,512]{1,0:T(8,128)S(1)} collective-permute-done((f32[256,512]{1,0:T(8,128)S(1)}, f32[256,512]{1,0:T(8,128)S(1)}, u32[]{:S(2)}, u32[]{:S(2)}) %collective-permute-start.3) | collective-permute-done | bytes 524320 | tf_op jit(solution)/shard_map/ppermute | solution.py:34
  51.6 0.1 add.60
  51.7 0.7 collective-permute-done.4
  52.3 0.1 add.61
  52.4 0.1 pad_maximum_fusion
  52.5 0.3 reshape.57
  52.8 28.4 %all_to_all.5 = f32[64,4,1024]{2,1,0:T(4,128)S(1)} all-to-all(f32[64,4,1024]{2,1,0:T(4,128)S(1)} %reshape.57), channel_id=1, replica_groups={{0,1,2,3,4,5,6,7,8,9,10,11,12,13,14,15,16,17,18,19,20,21,22,23,24,25,26..., dimensions={0} | all-to-all | bytes 2097152 | tf_op jit(solution)/shard_map/all_to_all | solution.py:426
  81.2 0.2 reduce_sum.9
  81.4 0.6 fusion.9
  (47 shorter events, 0.6 us)
Async XLA Ops:
  3.3 11.2 %copy-start = (f32[2,16,8,48]{3,2,1,0:T(8,128)S(1)}, f32[2,16,8,48]{3,2,1,0:T(8,128)}, u32[]{:S(2)}) copy-start(f32[2,16,8,48]{3,2,1,0:T(8,128)} %refs_2_.4) | copy-start | bytes 147460
  3.4 11.1 %collective-permute-start = (bf16[144,512]{1,0:T(8,128)(2,1)S(1)}, bf16[144,512]{1,0:T(8,128)(2,1)S(1)}, u32[]{:S(2)}, u32[]{:S(2)}) collective-permute-start(bf16[144,512]{1,0:T(8,128)(2,1)S(1)} %maximum_maximum_fusion.1), channel_id=1, source_target_pairs={{0,1},{1,0},{2,3},{3,2},{4,5},{5,4},{6,7},{7,6},{8,9},{9,8},{10,11... | collective-permute-start | bytes 442376 | tf_op jit(solution)/shard_map/ppermute | solution.py:34
  7.4 7.2 %slice-start = ((bf16[16,8,48,512]{3,2,1,0:T(8,128)(2,1)}), bf16[1,8,48,512]{3,2,1,0:T(8,128)(2,1)S(1)}, s32[]{:S(2)}) async-start(bf16[16,8,48,512]{3,2,1,0:T(8,128)(2,1)} %v_hbm.1), calls=%async_computation.1 | async-start | bytes 786432 | tf_op jit(solution)/shard_map/slice | solution.py:471
  14.7 7.6 %collective-permute-start.1 = (bf16[416,512]{1,0:T(8,128)(2,1)S(1)}, bf16[416,512]{1,0:T(8,128)(2,1)S(1)}, u32[]{:S(2)}, u32[]{:S(2)}) collective-permute-start(bf16[416,512]{1,0:T(8,128)(2,1)S(1)} %maximum_maximum_fusion), channel_id=1, source_target_pairs={{32,0},{33,1},{34,2},{35,3},{36,4},{37,5},{38,6},{39,7},{40,8},{41... | collective-permute-start | bytes 1277960 | tf_op jit(solution)/shard_map/ppermute | solution.py:34
  23.2 15.6 %collective-permute-start.2 = (bf16[914,512]{1,0:T(8,128)(2,1)S(1)}, bf16[914,512]{1,0:T(8,128)(2,1)S(1)}, u32[]{:S(2)}, u32[]{:S(2)}) collective-permute-start(bf16[914,512]{1,0:T(8,128)(2,1)S(1)} %concatenate.44), channel_id=1, source_target_pairs={{2,0},{3,1},{4,2},{5,3},{6,4},{7,5},{8,6},{9,7},{10,8},{11,9},{12,... | collective-permute-start | bytes 2807816 | tf_op jit(solution)/shard_map/ppermute | solution.py:34
  48.2 3.4 %collective-permute-start.3 = (f32[256,512]{1,0:T(8,128)S(1)}, f32[256,512]{1,0:T(8,128)S(1)}, u32[]{:S(2)}, u32[]{:S(2)}) collective-permute-start(f32[256,512]{1,0:T(8,128)S(1)} %get-tuple-element.23), channel_id=1, source_target_pairs={{0,32},{1,33},{2,34},{3,35},{4,36},{5,37},{6,38},{7,39},{8,40},{9,... | collective-permute-start | bytes 1572872 | tf_op jit(solution)/shard_map/ppermute | solution.py:34
  50.0 2.3 %collective-permute-start.4 = (f32[256,512]{1,0:T(8,128)S(1)}, f32[256,512]{1,0:T(8,128)S(1)}, u32[]{:S(2)}, u32[]{:S(2)}) collective-permute-start(f32[256,512]{1,0:T(8,128)S(1)} %get-tuple-element.25), channel_id=1, source_target_pairs={{0,32},{1,33},{2,34},{3,35},{4,36},{5,37},{6,38},{7,39},{8,40},{9,... | collective-permute-start | bytes 1572872 | tf_op jit(solution)/shard_map/ppermute | solution.py:34

commit v7 on v6

--- a/solution.py
+++ b/solution.py
@@ -157,52 +157,71 @@
         return yz[p]
 
     def filter_plane(p):
-        loads[p].wait()
         for g, (ins, outs) in enumerate(NEAR):
             size = len(outs) * SZ
             a, b = apply_band(bands[g][...], [ve[p - low, place[l]] for l in ins], size)
             w2[p % 4, outs[0] * SZ : outs[0] * SZ + size] = a
             t2[p % 4, outs[0] * SZ : outs[0] * SZ + size] = b
 
-    def make_products(p, buf, base):
+    def plane_weights(p):
         f = 2.0 * kappa_of(p) + kappa_of(p + 1)
         if p:
             f = f + kappa_of(p - 1)
-        c = weights(mat_ref[0, p], mat_ref[1, p], f, True)
-        for l in range(7):
-            rows = slice(l * SZ, (l + 1) * SZ)
-            mid = w2[p % 4, rows]
-            w3 = (mid + mid) + w2[(p + 1) % 4, rows]
-            t3 = 4.0 * t2[p % 4, rows] + t2[(p + 1) % 4, rows]
-            if p:
-                w3 = w3 + w2[(p - 1) % 4, rows]
-                t3 = t3 + t2[(p - 1) % 4, rows]
-            store_products(u.at[buf], base + l * SZ, ve[p - low, place[l]], w3, t3, c, l, 8)
-
+        return weights(mat_ref[0, p], mat_ref[1, p], f, True)
+
+    def make_products(p, l, c, buf, base):
+        rows = slice(l * SZ, (l + 1) * SZ)
+        mid = w2[p % 4, rows]
+        w3 = (mid + mid) + w2[(p + 1) % 4, rows]
+        t3 = 4.0 * t2[p % 4, rows] + t2[(p + 1) % 4, rows]
+        if p:
+            w3 = w3 + w2[(p - 1) % 4, rows]
+            t3 = t3 + t2[(p - 1) % 4, rows]
+        store_products(u.at[buf], base + l * SZ, ve[p - low, place[l]], w3, t3, c, l, 8)
+
+    def gram_piece(k, piece):
+        cols = slice(piece * K, (piece + 1) * K)
+        left = jnp.concatenate([ve[BATCH * k + q - low, place[l]] for q in range(BATCH) for l in range(7)], axis=0)
+        part = gram(left, u[k % 2, :, cols])
+        if k == first and m_hbm is None:
+            acc[:, cols] = part
+        else:
+            acc[:, cols] += part
+        if k == last - 1:
+            pltpu.make_async_copy(acc.at[:, cols], out_hbm.at[:, cols], sem_m.at[piece]).start()
+
+    ready = min(low + 4, BATCH * last + 1)
+    for p in range(low, ready):
+        loads[p].wait()
     done = low
-    for n, k in enumerate(range(first, last)):
+    for k in range(first, last):
+        if k == first + 1:
+            for p in range(ready, BATCH * last + 1):
+                loads[p].wait()
+            if m_hbm is not None:
+                load_m.wait()
+        elif last == first + 1:
+            for p in range(ready, BATCH * last + 1):
+                loads[p].wait()
+        pieces = list(range(2)) if k > first else []
         for q in range(BATCH):
             p = BATCH * k + q
             while done <= p + 1:
                 filter_plane(done)
                 done += 1
-            make_products(p, k % 2, q * INNER)
-        left = jnp.concatenate(
-            [ve[BATCH * k + q - low, place[l]] for q in range(BATCH) for l in range(7)], axis=0
-        )
-        if n == 0 and m_hbm is not None:
-            load_m.wait()
-        for piece in range(4):
-            cols = slice(piece * 256, (piece + 1) * 256)
-            part = gram(left, u[k % 2, :, cols])
-            if n == 0 and m_hbm is None:
-                acc[:, cols] = part
-            else:
-                acc[:, cols] += part
-            if k == last - 1:
-                pltpu.make_async_copy(acc.at[:, cols], out_hbm.at[:, cols], sem_m.at[piece]).start()
-    for piece in range(4):
-        cols = slice(piece * 256, (piece + 1) * 256)
+            c = plane_weights(p)
+            for l in range(7):
+                make_products(p, l, c, k % 2, q * INNER)
+                if pieces and (q * 7 + l) % 10 == 0:
+                    gram_piece(k - 1, pieces.pop(0))
+        while pieces:
+            gram_piece(k - 1, pieces.pop(0))
+    if m_hbm is not None and last == first + 1:
+        load_m.wait()
+    for piece in range(2):
+        gram_piece(last - 1, piece)
+    for piece in range(2):
+        cols = slice(piece * K, (piece + 1) * K)
         pltpu.make_async_copy(acc.at[:, cols], out_hbm.at[:, cols], sem_m.at[piece]).wait()
 
 

time: 82.3 us -> 81.4 us (0.989)
  Pallas kernels: 32.2 us -> 29.5 us
  waiting for transfers between devices: 3.74 us -> 5.6 us
  starting transfers between devices: 8.8 us -> 7.46 us
  blocking collectives: 28.4 us -> 29.7 us
    pallas_call x3, Pallas kernels: 24.1 us -> 21.3 us  [inner_part(): pl.pallas_call(body, out_shape=pltpu.HBM((K, 2 * K), jnp.float32), in_spe...]
    ppermute x5, waiting for transfers between devices: 3.74 us -> 5.6 us  [send(): return lax.ppermute(value, ALL, links)]
    ppermute x5, starting transfers between devices: 8.8 us -> 7.46 us  [send(): return lax.ppermute(value, ALL, links)]
    all_to_all x1, blocking collectives: 28.4 us -> 29.7 us  [reduce_to_owner(): lax.all_to_all(blocks, ALL, 0, 0, tiled=True, axis_index_groups=groups)]
  transfers between devices with their start and end apart: 5 -> 5, of which waited for: 3 -> 3; matrix products, arithmetic and copies ran while one was open for 2% -> 2% of each run, Pallas kernels for 29% -> 26%
where the time goes in v7:
time: 81.4 us; the launch traced here: 81 us
  blocking collectives  29.7 us (36%)
  Pallas kernels  29.5 us (36%)
  starting transfers between devices  7.46 us (9%)
  local copies, waits for them, and re-layouts  6.44 us (8%)
  waiting for transfers between devices  5.6 us (7%)
  other arithmetic  1.24 us (2%)
  between operations  1.15 us (1%)
    all_to_all x1, blocking collectives, reduce_to_owner(): lax.all_to_all(blocks, ALL, 0, 0, tiled=True, axis_index_groups=groups)  29.7 us
    pallas_call x3, Pallas kernels, inner_part(): pl.pallas_call(body, out_shape=pltpu.HBM((K, 2 * K), jnp.float32), in_spe...  21.3 us
    pallas_call x1, Pallas kernels, outer_part(): pl.pallas_call(outer_kernel, out_shape=[jax.ShapeDtypeStruct((K // 2, K),...  8.15 us
    ppermute x5, starting transfers between devices, send(): return lax.ppermute(value, ALL, links)  7.46 us
    ppermute x5, waiting for transfers between devices, send(): return lax.ppermute(value, ALL, links)  5.6 us
    dynamic_slice x5, local copies, waits for them, and re-layouts, pick(): return lax.dynamic_index_in_dim(x, index, dim, keepdims=False)  3.1 us
  transfers between devices with their start and end apart: 5, of which 3 were waited for; matrix products, arithmetic and copies ran while one was open for 2% of the time, Pallas kernels for 26%

profile of v7, /device:TPU:0, one launch (start us, length us, event | category | flops | bytes accessed | tf_op | source)
XLA Modules:
  0.0 81.0 jit_solution(8922782187126313759)
XLA Ops:
  0.6 0.8 %slice.98 = f32[1,16,8,48]{3,2,1,0:T(8,128)S(1)} slice(f32[2,16,8,48]{3,2,1,0:T(8,128)} %refs_2_.4), slice={[0:1], [0:16], [0:8], [0:48]} | slice | bytes 49152 | tf_op jit(solution)/shard_map/slice | solution.py:479
  1.5 0.1 constant_dynamic-slice_fusion.1
  1.6 0.2 copy.42
  1.7 1.5 %constant_dynamic-slice_fusion.2 = bf16[16,8,1,512]{3,2,1,0:T(2,128)(2,1)S(1)} fusion(bf16[16,8,48,512]{3,2,1,0:T(8,128)(2,1)} %v_hbm.1, s32[]{:T(128)S(6)} %select_n.57), kind=kLoop, calls=%fused_computation.67 | loop fusion | bytes 262148 | tf_op jit(solution)/shard_map/jit(dynamic_index_in_dim)/dynamic_slice | solution.py:438
  3.3 0.0 copy-start
  3.4 4.1 %collective-permute-start = (bf16[144,512]{1,0:T(8,128)(2,1)S(1)}, bf16[144,512]{1,0:T(8,128)(2,1)S(1)}, u32[]{:S(2)}, u32[]{:S(2)}) collective-permute-start(bf16[144,512]{1,0:T(8,128)(2,1)S(1)} %maximum_maximum_fusion.1), channel_id=1, source_target_pairs={{0,1},{1,0},{2,3},{3,2},{4,5},{5,4},{6,7},{7,6},{8,9},{9,8},{10,11... | collective-permute-start | bytes 442376 | tf_op jit(solution)/shard_map/ppermute | solution.py:34
  7.4 0.0 slice-start
  7.5 5.1 %inner0.1.refs_0_ = f32[512,1024]{1,0:T(8,128)} custom-call(s32[1]{0:T(128)} %bitcast.odd_ref, bf16[16,8,48,512]{3,2,1,0:T(8,128)(2,1)} %v_hbm.1, f32[2,16,8,48]{3,2,1,0:T(8,128)} %refs_2_.4, bf16[288,192]{1,0:T(8,128)(2,1)} %constant.80.clone.refs_2_.refs_3_.hbm0, bf16[288,240]{1,0:T(8,128)(2,1)} %constant.81.clone.refs_3_.refs_4_.hbm1, ...), custom_call_target="tpu_custom_call" | custom-call | flops 1800000000 | bytes 2000000 | tf_op jit(solution)/shard_map/inner0/pallas_call | solution.py:378
  12.7 0.1 copy.48
  12.8 1.2 %constant_dynamic-slice_fusion.3 = bf16[16,1,48,512]{3,2,1,0:T(8,128)(2,1)S(1)} fusion(bf16[16,8,48,512]{3,2,1,0:T(8,128)(2,1)} %v_hbm.1, s32[]{:T(128)S(6)} %select_n.56), kind=kLoop, calls=%fused_computation.68 | loop fusion | bytes 1572868 | tf_op jit(solution)/shard_map/jit(dynamic_index_in_dim)/dynamic_slice | solution.py:438
  14.0 0.0 collective-permute-done
  14.1 0.0 copy-done
  14.1 0.1 fusion.1
  14.2 0.0 slice-done
  14.3 1.3 %collective-permute-start.1 = (bf16[416,512]{1,0:T(8,128)(2,1)S(1)}, bf16[416,512]{1,0:T(8,128)(2,1)S(1)}, u32[]{:S(2)}, u32[]{:S(2)}) collective-permute-start(bf16[416,512]{1,0:T(8,128)(2,1)S(1)} %maximum_maximum_fusion), channel_id=1, source_target_pairs={{32,0},{33,1},{34,2},{35,3},{36,4},{37,5},{38,6},{39,7},{40,8},{41... | collective-permute-start | bytes 1277960 | tf_op jit(solution)/shard_map/ppermute | solution.py:34
  15.6 5.7 %inner1.1.refs_0_ = f32[512,1024]{1,0:T(8,128)} custom-call(s32[1]{0:T(128)} %bitcast.odd_ref, f32[512,1024]{1,0:T(8,128)} %inner0.1.refs_0_, bf16[16,8,48,512]{3,2,1,0:T(8,128)(2,1)} %v_hbm.1, f32[2,16,8,48]{3,2,1,0:T(8,128)} %refs_2_.4, bf16[288,192]{1,0:T(8,128)(2,1)} %constant.80.clone.refs_2_.refs_3_.hbm0, ...), custom_call_target="tpu_custom_call" | custom-call | flops 1800000000 | bytes 2000000 | tf_op jit(solution)/shard_map/inner1/pallas_call | solution.py:378
  21.3 0.0 collective-permute-done.1.vx_hbm
  21.5 0.1 reverse_select_fusion
  21.8 0.5 concatenate.44
  22.2 1.5 %collective-permute-start.2 = (bf16[914,512]{1,0:T(8,128)(2,1)S(1)}, bf16[914,512]{1,0:T(8,128)(2,1)S(1)}, u32[]{:S(2)}, u32[]{:S(2)}) collective-permute-start(bf16[914,512]{1,0:T(8,128)(2,1)S(1)} %concatenate.44), channel_id=1, source_target_pairs={{2,0},{3,1},{4,2},{5,3},{6,4},{7,5},{8,6},{9,7},{10,8},{11,9},{12,... | collective-permute-start | bytes 2807816 | tf_op jit(solution)/shard_map/ppermute | solution.py:34
  23.8 10.5 %inner2.1.m_hbm = f32[512,1024]{1,0:T(8,128)} custom-call(s32[1]{0:T(128)} %bitcast.odd_ref, f32[512,1024]{1,0:T(8,128)} %inner1.1.refs_0_, bf16[16,8,48,512]{3,2,1,0:T(8,128)(2,1)} %v_hbm.1, f32[2,16,8,48]{3,2,1,0:T(8,128)} %refs_2_.4, bf16[288,192]{1,0:T(8,128)(2,1)} %constant.80.clone.refs_2_.refs_3_.hbm0, ...), custom_call_target="tpu_custom_call" | custom-call | flops 5400000000 | bytes 6000000 | tf_op jit(solution)/shard_map/inner2/pallas_call | solution.py:378
  34.3 3.5 %collective-permute-done.2.vy_hbm = bf16[914,512]{1,0:T(8,128)(2,1)S(1)} collective-permute-done((bf16[914,512]{1,0:T(8,128)(2,1)S(1)}, bf16[914,512]{1,0:T(8,128)(2,1)S(1)}, u32[]{:S(2)}, u32[]{:S(2)}) %collective-permute-start.2) | collective-permute-done | bytes 935968 | tf_op jit(solution)/shard_map/ppermute | solution.py:34
  37.8 0.1 fusion
  38.0 0.1 copy.34
  38.2 0.1 copy.37
  38.3 0.1 dynamic-slice_maximum_fusion
  38.4 0.1 copy.33
  38.5 0.1 dynamic-slice_maximum_fusion.1
  38.7 0.1 copy.32
  38.8 0.1 copy.36
  38.9 0.1 copy.35
  39.1 8.1 %outer.1 = (f32[256,512]{1,0:T(8,128)S(1)}, f32[256,512]{1,0:T(8,128)S(1)}, f32[256,512]{1,0:T(8,128)S(1)}, f32[256,512]{1,0:T(8,128)S(1)}) custom-call(s32[1]{0:T(128)} %bitcast.odd_ref, f32[512,1024]{1,0:T(8,128)} %inner2.1.m_hbm, bf16[16,8,48,512]{3,2,1,0:T(8,128)(2,1)} %v_hbm.1, bf16[416,512]{1,0:T(8,128)(2,1)S(1)} %collective-permute-done.1.vx_hbm, ...), custom_call_target="tpu_custom_call" | custom-call | flops 4000000000 | bytes 6000000 | tf_op jit(solution)/shard_map/outer/pallas_call | solution.py:406
  47.2 0.5 collective-permute-start.3
  47.8 0.1 collective-permute-start.4
  47.9 1.4 %collective-permute-done.3 = f32[256,512]{1,0:T(8,128)S(1)} collective-permute-done((f32[256,512]{1,0:T(8,128)S(1)}, f32[256,512]{1,0:T(8,128)S(1)}, u32[]{:S(2)}, u32[]{:S(2)}) %collective-permute-start.3) | collective-permute-done | bytes 524320 | tf_op jit(solution)/shard_map/ppermute | solution.py:34
  49.3 0.1 add.60
  49.4 0.7 collective-permute-done.4
  50.0 0.1 add.61
  50.1 0.1 pad_maximum_fusion
  50.2 0.3 reshape.57
  50.5 29.7 %all_to_all.5 = f32[64,4,1024]{2,1,0:T(4,128)S(1)} all-to-all(f32[64,4,1024]{2,1,0:T(4,128)S(1)} %reshape.57), channel_id=1, replica_groups={{0,1,2,3,4,5,6,7,8,9,10,11,12,13,14,15,16,17,18,19,20,21,22,23,24,25,26..., dimensions={0} | all-to-all | bytes 2097152 | tf_op jit(solution)/shard_map/all_to_all | solution.py:445
  80.2 0.2 reduce_sum.9
  80.4 0.6 fusion.9
  (47 shorter events, 0.6 us)
Async XLA Ops:
  3.3 10.8 %copy-start = (f32[2,16,8,48]{3,2,1,0:T(8,128)S(1)}, f32[2,16,8,48]{3,2,1,0:T(8,128)}, u32[]{:S(2)}) copy-start(f32[2,16,8,48]{3,2,1,0:T(8,128)} %refs_2_.4) | copy-start | bytes 147460
  3.4 10.7 %collective-permute-start = (bf16[144,512]{1,0:T(8,128)(2,1)S(1)}, bf16[144,512]{1,0:T(8,128)(2,1)S(1)}, u32[]{:S(2)}, u32[]{:S(2)}) collective-permute-start(bf16[144,512]{1,0:T(8,128)(2,1)S(1)} %maximum_maximum_fusion.1), channel_id=1, source_target_pairs={{0,1},{1,0},{2,3},{3,2},{4,5},{5,4},{6,7},{7,6},{8,9},{9,8},{10,11... | collective-permute-start | bytes 442376 | tf_op jit(solution)/shard_map/ppermute | solution.py:34
  7.4 6.8 %slice-start = ((bf16[16,8,48,512]{3,2,1,0:T(8,128)(2,1)}), bf16[1,8,48,512]{3,2,1,0:T(8,128)(2,1)S(1)}, s32[]{:S(2)}) async-start(bf16[16,8,48,512]{3,2,1,0:T(8,128)(2,1)} %v_hbm.1), calls=%async_computation.1 | async-start | bytes 786432 | tf_op jit(solution)/shard_map/slice | solution.py:490
  14.3 7.0 %collective-permute-start.1 = (bf16[416,512]{1,0:T(8,128)(2,1)S(1)}, bf16[416,512]{1,0:T(8,128)(2,1)S(1)}, u32[]{:S(2)}, u32[]{:S(2)}) collective-permute-start(bf16[416,512]{1,0:T(8,128)(2,1)S(1)} %maximum_maximum_fusion), channel_id=1, source_target_pairs={{32,0},{33,1},{34,2},{35,3},{36,4},{37,5},{38,6},{39,7},{40,8},{41... | collective-permute-start | bytes 1277960 | tf_op jit(solution)/shard_map/ppermute | solution.py:34
  22.2 15.6 %collective-permute-start.2 = (bf16[914,512]{1,0:T(8,128)(2,1)S(1)}, bf16[914,512]{1,0:T(8,128)(2,1)S(1)}, u32[]{:S(2)}, u32[]{:S(2)}) collective-permute-start(bf16[914,512]{1,0:T(8,128)(2,1)S(1)} %concatenate.44), channel_id=1, source_target_pairs={{2,0},{3,1},{4,2},{5,3},{6,4},{7,5},{8,6},{9,7},{10,8},{11,9},{12,... | collective-permute-start | bytes 2807816 | tf_op jit(solution)/shard_map/ppermute | solution.py:34
  47.2 2.1 %collective-permute-start.3 = (f32[256,512]{1,0:T(8,128)S(1)}, f32[256,512]{1,0:T(8,128)S(1)}, u32[]{:S(2)}, u32[]{:S(2)}) collective-permute-start(f32[256,512]{1,0:T(8,128)S(1)} %get-tuple-element.23), channel_id=1, source_target_pairs={{0,32},{1,33},{2,34},{3,35},{4,36},{5,37},{6,38},{7,39},{8,40},{9,... | collective-permute-start | bytes 1572872 | tf_op jit(solution)/shard_map/ppermute | solution.py:34
  47.8 2.3 %collective-permute-start.4 = (f32[256,512]{1,0:T(8,128)S(1)}, f32[256,512]{1,0:T(8,128)S(1)}, u32[]{:S(2)}, u32[]{:S(2)}) collective-permute-start(f32[256,512]{1,0:T(8,128)S(1)} %get-tuple-element.25), channel_id=1, source_target_pairs={{0,32},{1,33},{2,34},{3,35},{4,36},{5,37},{6,38},{7,39},{8,40},{9,... | collective-permute-start | bytes 1572872 | tf_op jit(solution)/shard_map/ppermute | solution.py:34

commit v8 on v7

--- a/solution.py
+++ b/solution.py
@@ -118,7 +118,7 @@
 
 
 def inner_kernel(
-    first, last, odd_ref, m_hbm, v_hbm, raw_hbm, hbm0, hbm1, hbm2, out_hbm,
+    first, last, buf, odd_ref, m_hbm, v_hbm, raw_hbm, hbm0, hbm1, hbm2, out_hbm,
     ve, w2, t2, u, acc, raw, mat_ref, band0, band1, band2, sem, sem_m,
 ):
     odd = odd_ref[0]
@@ -140,6 +140,14 @@
     if m_hbm is not None:
         load_m = pltpu.make_async_copy(m_hbm, acc, sem_m.at[4])
         load_m.start()
+    extra = []
+    if first == 0:
+        extra = [(v_hbm.at[0, y], buf.at[pl.ds(y * SZ, SZ)]) for y in range(SY)]
+    elif buf is not None:
+        extra = [(v_hbm.at[x, 7 * odd], buf.at[pl.ds(x * SZ, SZ)]) for x in range(SX)]
+    extra = [pltpu.make_async_copy(a, b, sem_m.at[9 + n]) for n, (a, b) in enumerate(extra)]
+    for copy in extra:
+        copy.start()
     side[3].wait()
     for i in range(2):
         for p in range(low, BATCH * last + 1):
@@ -220,6 +228,8 @@
         load_m.wait()
     for piece in range(2):
         gram_piece(last - 1, piece)
+    for copy in extra:
+        copy.wait()
     for piece in range(2):
         cols = slice(piece * K, (piece + 1) * K)
         pltpu.make_async_copy(acc.at[:, cols], out_hbm.at[:, cols], sem_m.at[piece]).wait()
@@ -367,19 +377,24 @@
 
 
 def inner_part(first, last, odd, m, v, mat, bands):
+    rows = {0: 416, 1: 914}.get(first)
+
     def body(odd_ref, *refs):
+        refs = list(refs)
         if m is None:
-            refs = (None,) + refs
-        inner_kernel(first, last, odd_ref, *refs)
+            refs = [None] + refs
+        buf = refs.pop(7) if rows else None
+        inner_kernel(first, last, buf, odd_ref, *refs)
 
     planes = BATCH * (last - first) + (2 if first else 1)
     operands = (odd,) + (() if m is None else (m,)) + (v, mat) + tuple(bands)
     specs = [SMEM] + [HBM] * (len(operands) - 1)
     return pl.pallas_call(
         body,
-        out_shape=pltpu.HBM((K, 2 * K), jnp.float32),
+        out_shape=[pltpu.HBM((K, 2 * K), jnp.float32)]
+        + ([jax.ShapeDtypeStruct((rows, K), jnp.bfloat16)] if rows else []),
         in_specs=specs,
-        out_specs=HBM,
+        out_specs=[HBM] + ([pl.BlockSpec(memory_space=pl.ANY)] if rows else []),
         scratch_shapes=[
             pltpu.VMEM((planes, SY, SZ, K), jnp.bfloat16),
             pltpu.VMEM((4, INNER, K), jnp.float32),
@@ -392,7 +407,7 @@
             pltpu.VMEM((6 * SZ, 5 * SZ), jnp.bfloat16),
             pltpu.VMEM((2 * SZ, 3 * SZ), jnp.bfloat16),
             pltpu.SemaphoreType.DMA((planes,)),
-            pltpu.SemaphoreType.DMA((9,)),
+            pltpu.SemaphoreType.DMA((25,)),
         ],
         compiler_params=pltpu.CompilerParams(vmem_limit_bytes=26 * 1024 * 1024),
         cost_estimate=pl.CostEstimate(
@@ -480,16 +495,16 @@
     zm = send(jnp.concatenate([zf.reshape(SX * SY, K), to_parts(kface)], axis=0), to_z)
     bands = [in_hbm(band_matrix(ins, outs)) for ins, outs in NEAR]
     raw = in_hbm(material)
-    m = inner_part(*PIECES[0], odd_flag, None, vectors, raw, bands)
+    m, xbuf = inner_part(*PIECES[0], odd_flag, None, vectors, raw, bands)
     zm, m = lax.optimization_barrier((zm, m))
     zh = zm[: SX * SY].reshape(SX, SY, K)
     kz = from_parts(zm[SX * SY :])[:, :SY]
     lanes = jnp.arange(128)
     own = jnp.pad(material, ((0, 0), (0, 0), (0, 0), (0, 128 - SZ)))
     matz = jnp.stack([jnp.where(lanes == 64, kz[..., None], own[0]), own[1]])
-    plane = eigvecs[0].reshape(SY * SZ, K)
-    vx = send(jnp.concatenate([plane, zf[0], zh[0], to_parts(matz[:, 0].reshape(16, 128))], axis=0), to_x)
-    m = inner_part(*PIECES[1], odd_flag, in_hbm(m), vectors, raw, bands)
+    rest = jnp.concatenate([zf[0], zh[0], to_parts(matz[:, 0].reshape(16, 128))], axis=0)
+    vx = send(lax.dynamic_update_slice(xbuf, rest, (SY * SZ, 0)), to_x)
+    m, ybuf = inner_part(*PIECES[1], odd_flag, in_hbm(m), vectors, raw, bands)
     vx, m = lax.optimization_barrier((vx, m))
     at = SY * SZ
     xf, xz = vx[at : at + SY], vx[at + SY : at + 2 * SY]
@@ -497,14 +512,14 @@
     matz = chain(jnp.concatenate([matz, xmat], axis=1), 2)
     frows = chain(jnp.concatenate([zf, xf[None]], axis=0), 1)
     zrows = chain(jnp.concatenate([zh, xz[None]], axis=0), 1)
-    lines = pick(eigvecs, side, 1).reshape(SX * SZ, K)
     xline = lax.dynamic_slice_in_dim(vx, side * SZ, SZ, 0)
     gap = jnp.zeros((15, K), jnp.bfloat16)
     parts = to_parts(matz[:, :, 0].reshape(34, 128))
-    vy = send(jnp.concatenate([lines, xline, frows[:, 0], gap, zrows[:, 0], gap, parts], axis=0), to_y)
+    rest = jnp.concatenate([xline, frows[:, 0], gap, zrows[:, 0], gap, parts], axis=0)
+    vy = send(lax.dynamic_update_slice(ybuf, rest, (SX * SZ, 0)), to_y)
     zf = face_rows(frows)
     zh = face_rows(zrows)
-    m = inner_part(*PIECES[2], odd_flag, in_hbm(m), vectors, raw, bands)
+    (m,) = inner_part(*PIECES[2], odd_flag, in_hbm(m), vectors, raw, bands)
     vy, m, zf, zh = lax.optimization_barrier((vy, m, zf, zh))
     my = from_parts(vy[17 * SZ + 64 :]).reshape(2, 17, 1, 128)
     matz = jnp.concatenate([matz, my], axis=2)

time: 81.4 us -> 81.6 us (level)
  Pallas kernels: 29.5 us -> 31 us
  local copies, waits for them, and re-layouts: 6.44 us -> 5.05 us
    pallas_call x3, Pallas kernels: 21.3 us -> 22.8 us  [inner_part(): pl.pallas_call(body, out_shape=[pltpu.HBM((K, 2 * K), jnp.float32)] + ([j...]
    dynamic_slice x5 -> x4, local copies, waits for them, and re-layouts: 3.1 us -> 1.91 us  [pick(): return lax.dynamic_index_in_dim(x, index, dim, keepdims=False)]
  transfers between devices with their start and end apart: 5 -> 5, of which waited for: 3 -> 3; matrix products, arithmetic and copies ran while one was open for 2% -> 0% of each run, Pallas kernels for 26% -> 28%
where the time goes in v8:
time: 81.6 us; the launch traced here: 81.3 us
  Pallas kernels  31 us (38%)
  blocking collectives  30.1 us (37%)
  starting transfers between devices  7.41 us (9%)
  waiting for transfers between devices  5.41 us (7%)
  local copies, waits for them, and re-layouts  5.05 us (6%)
  other arithmetic  1.21 us (1%)
  between operations  1.15 us (1%)
    all_to_all x1, blocking collectives, reduce_to_owner(): lax.all_to_all(blocks, ALL, 0, 0, tiled=True, axis_index_groups=groups)  30.1 us
    pallas_call x3, Pallas kernels, inner_part(): pl.pallas_call(body, out_shape=[pltpu.HBM((K, 2 * K), jnp.float32)] + ([j...  22.8 us
    pallas_call x1, Pallas kernels, outer_part(): pl.pallas_call(outer_kernel, out_shape=[jax.ShapeDtypeStruct((K // 2, K),...  8.15 us
    ppermute x5, starting transfers between devices, send(): return lax.ppermute(value, ALL, links)  7.41 us
    ppermute x5, waiting for transfers between devices, send(): return lax.ppermute(value, ALL, links)  5.41 us
    dynamic_slice x4, local copies, waits for them, and re-layouts, pick(): return lax.dynamic_index_in_dim(x, index, dim, keepdims=False)  1.91 us
  transfers between devices with their start and end apart: 5, of which 3 were waited for; matrix products, arithmetic and copies ran while one was open for 0% of the time, Pallas kernels for 28%

profile of v8, /device:TPU:0, one launch (start us, length us, event | category | flops | bytes accessed | tf_op | source)
XLA Modules:
  0.0 81.3 jit_solution(15615759429842399016)
XLA Ops:
  0.6 0.8 %slice.93 = f32[1,16,8,48]{3,2,1,0:T(8,128)S(1)} slice(f32[2,16,8,48]{3,2,1,0:T(8,128)} %refs_2_.4), slice={[0:1], [0:16], [0:8], [0:48]} | slice | bytes 49152 | tf_op jit(solution)/shard_map/slice | solution.py:494
  1.5 0.1 constant_dynamic-slice_fusion.1
  1.6 0.2 copy.42
  1.7 1.5 %constant_dynamic-slice_fusion.2 = bf16[16,8,1,512]{3,2,1,0:T(2,128)(2,1)S(1)} fusion(bf16[16,8,48,512]{3,2,1,0:T(8,128)(2,1)} %v_hbm.1, s32[]{:T(128)S(6)} %select_n.54), kind=kLoop, calls=%fused_computation.68 | loop fusion | bytes 262148 | tf_op jit(solution)/shard_map/jit(dynamic_index_in_dim)/dynamic_slice | solution.py:453
  3.4 4.1 %collective-permute-start = (bf16[144,512]{1,0:T(8,128)(2,1)S(1)}, bf16[144,512]{1,0:T(8,128)(2,1)S(1)}, u32[]{:S(2)}, u32[]{:S(2)}) collective-permute-start(bf16[144,512]{1,0:T(8,128)(2,1)S(1)} %maximum_maximum_fusion), channel_id=1, source_target_pairs={{0,1},{1,0},{2,3},{3,2},{4,5},{5,4},{6,7},{7,6},{8,9},{9,8},{10,11... | collective-permute-start | bytes 442376 | tf_op jit(solution)/shard_map/ppermute | solution.py:34
  7.4 0.1 copy.48
  7.7 0.0 copy-start
  7.7 5.5 %inner0.1 = (f32[512,1024]{1,0:T(8,128)}, bf16[416,512]{1,0:T(8,128)(2,1)S(1)}) custom-call(s32[1]{0:T(128)} %bitcast.odd_ref, bf16[16,8,48,512]{3,2,1,0:T(8,128)(2,1)} %v_hbm.1, f32[2,16,8,48]{3,2,1,0:T(8,128)} %refs_2_.4, bf16[288,192]{1,0:T(8,128)(2,1)} %constant.79.clone.refs_2_.refs_3_.hbm0, bf16[288,240]{1,0:T(8,128)(2,1)} %constant.80.clone.refs_3_.refs_4_.hbm1, ...), custom_call_target="tpu_custom_call" | custom-call | flops 1800000000 | bytes 2000000 | tf_op jit(solution)/shard_map/inner0/pallas_call | solution.py:392
  13.1 0.0 collective-permute-done
  13.2 0.0 copy-done
  13.2 0.1 fusion.1
  13.3 1.3 %collective-permute-start.1 = (bf16[416,512]{1,0:T(8,128)(2,1)S(1)}, bf16[416,512]{1,0:T(8,128)(2,1)S(1)}, u32[]{:S(2)}, u32[]{:S(2)}) collective-permute-start(bf16[416,512]{1,0:T(8,128)(2,1)S(1)} %maximum_dynamic-update-slice_fusion), channel_id=1, source_target_pairs={{32,0},{33,1},{34,2},{35,3},{36,4},{37,5},{38,6},{39,7},{40,8},{41... | collective-permute-start | bytes 1277960 | tf_op jit(solution)/shard_map/ppermute | solution.py:34
  14.7 6.7 %inner1.1 = (f32[512,1024]{1,0:T(8,128)}, bf16[914,512]{1,0:T(8,128)(2,1)S(1)}) custom-call(s32[1]{0:T(128)} %bitcast.odd_ref, f32[512,1024]{1,0:T(8,128)} %get-tuple-element.19.refs_0_, bf16[16,8,48,512]{3,2,1,0:T(8,128)(2,1)} %v_hbm.1, f32[2,16,8,48]{3,2,1,0:T(8,128)} %refs_2_.4, bf16[288,192]{1,0:T(8,128)(2,1)} %constant.79.clone.refs_2_.refs_3_.hbm0, ...), custom_call_target="tpu_custom_call" | custom-call | flops 1800000000 | bytes 2000000 | tf_op jit(solution)/shard_map/inner1/pallas_call | solution.py:392
  21.5 0.0 collective-permute-done.1.vx_hbm
  21.6 0.1 reverse_select_fusion
  21.9 0.3 concatenate.44
  22.2 1.5 %collective-permute-start.2 = (bf16[914,512]{1,0:T(8,128)(2,1)S(1)}, bf16[914,512]{1,0:T(8,128)(2,1)S(1)}, u32[]{:S(2)}, u32[]{:S(2)}) collective-permute-start(bf16[914,512]{1,0:T(8,128)(2,1)S(1)} %constant_dynamic-update-slice_fusion), channel_id=1, source_target_pairs={{2,0},{3,1},{4,2},{5,3},{6,4},{7,5},{8,6},{9,7},{10,8},{11,9},{12,... | collective-permute-start | bytes 2807816 | tf_op jit(solution)/shard_map/ppermute | solution.py:34
  23.8 10.6 %inner2.1.m_hbm = f32[512,1024]{1,0:T(8,128)} custom-call(s32[1]{0:T(128)} %bitcast.odd_ref, f32[512,1024]{1,0:T(8,128)} %get-tuple-element.25.refs_0_, bf16[16,8,48,512]{3,2,1,0:T(8,128)(2,1)} %v_hbm.1, f32[2,16,8,48]{3,2,1,0:T(8,128)} %refs_2_.4, bf16[288,192]{1,0:T(8,128)(2,1)} %constant.79.clone.refs_2_.refs_3_.hbm0, ...), custom_call_target="tpu_custom_call" | custom-call | flops 5400000000 | bytes 6000000 | tf_op jit(solution)/shard_map/inner2/pallas_call | solution.py:392
  34.4 3.3 %collective-permute-done.2.vy_hbm = bf16[914,512]{1,0:T(8,128)(2,1)S(1)} collective-permute-done((bf16[914,512]{1,0:T(8,128)(2,1)S(1)}, bf16[914,512]{1,0:T(8,128)(2,1)S(1)}, u32[]{:S(2)}, u32[]{:S(2)}) %collective-permute-start.2) | collective-permute-done | bytes 935968 | tf_op jit(solution)/shard_map/ppermute | solution.py:34
  37.8 0.1 fusion
  38.0 0.1 copy.34
  38.1 0.1 copy.37
  38.2 0.1 dynamic-slice_maximum_fusion
  38.3 0.1 copy.33
  38.5 0.1 dynamic-slice_maximum_fusion.1
  38.6 0.1 copy.32
  38.8 0.1 copy.36
  38.9 0.1 copy.35
  39.0 8.1 %outer.1 = (f32[256,512]{1,0:T(8,128)S(1)}, f32[256,512]{1,0:T(8,128)S(1)}, f32[256,512]{1,0:T(8,128)S(1)}, f32[256,512]{1,0:T(8,128)S(1)}) custom-call(s32[1]{0:T(128)} %bitcast.odd_ref, f32[512,1024]{1,0:T(8,128)} %inner2.1.m_hbm, bf16[16,8,48,512]{3,2,1,0:T(8,128)(2,1)} %v_hbm.1, bf16[416,512]{1,0:T(8,128)(2,1)S(1)} %collective-permute-done.1.vx_hbm, ...), custom_call_target="tpu_custom_call" | custom-call | flops 4000000000 | bytes 6000000 | tf_op jit(solution)/shard_map/outer/pallas_call | solution.py:421
  47.2 0.1 collective-permute-start.3
  47.3 0.5 collective-permute-start.4
  47.8 1.4 %collective-permute-done.3 = f32[256,512]{1,0:T(8,128)S(1)} collective-permute-done((f32[256,512]{1,0:T(8,128)S(1)}, f32[256,512]{1,0:T(8,128)S(1)}, u32[]{:S(2)}, u32[]{:S(2)}) %collective-permute-start.3) | collective-permute-done | bytes 524320 | tf_op jit(solution)/shard_map/ppermute | solution.py:34
  49.2 0.1 add.58
  49.2 0.7 collective-permute-done.4
  49.9 0.1 add.59
  50.0 0.1 pad_maximum_fusion
  50.1 0.3 reshape.52
  50.4 30.1 %all_to_all.5 = f32[64,4,1024]{2,1,0:T(4,128)S(1)} all-to-all(f32[64,4,1024]{2,1,0:T(4,128)S(1)} %reshape.52), channel_id=1, replica_groups={{0,1,2,3,4,5,6,7,8,9,10,11,12,13,14,15,16,17,18,19,20,21,22,23,24,25,26..., dimensions={0} | all-to-all | bytes 2097152 | tf_op jit(solution)/shard_map/all_to_all | solution.py:460
  80.5 0.2 reduce_sum.9
  80.7 0.6 fusion.9
  (48 shorter events, 0.6 us)
Async XLA Ops:
  3.4 9.8 %collective-permute-start = (bf16[144,512]{1,0:T(8,128)(2,1)S(1)}, bf16[144,512]{1,0:T(8,128)(2,1)S(1)}, u32[]{:S(2)}, u32[]{:S(2)}) collective-permute-start(bf16[144,512]{1,0:T(8,128)(2,1)S(1)} %maximum_maximum_fusion), channel_id=1, source_target_pairs={{0,1},{1,0},{2,3},{3,2},{4,5},{5,4},{6,7},{7,6},{8,9},{9,8},{10,11... | collective-permute-start | bytes 442376 | tf_op jit(solution)/shard_map/ppermute | solution.py:34
  7.7 5.5 %copy-start = (f32[2,16,8,48]{3,2,1,0:T(8,128)S(1)}, f32[2,16,8,48]{3,2,1,0:T(8,128)}, u32[]{:S(2)}) copy-start(f32[2,16,8,48]{3,2,1,0:T(8,128)} %refs_2_.4) | copy-start | bytes 147460
  13.3 8.1 %collective-permute-start.1 = (bf16[416,512]{1,0:T(8,128)(2,1)S(1)}, bf16[416,512]{1,0:T(8,128)(2,1)S(1)}, u32[]{:S(2)}, u32[]{:S(2)}) collective-permute-start(bf16[416,512]{1,0:T(8,128)(2,1)S(1)} %maximum_dynamic-update-slice_fusion), channel_id=1, source_target_pairs={{32,0},{33,1},{34,2},{35,3},{36,4},{37,5},{38,6},{39,7},{40,8},{41... | collective-permute-start | bytes 1277960 | tf_op jit(solution)/shard_map/ppermute | solution.py:34
  22.2 15.6 %collective-permute-start.2 = (bf16[914,512]{1,0:T(8,128)(2,1)S(1)}, bf16[914,512]{1,0:T(8,128)(2,1)S(1)}, u32[]{:S(2)}, u32[]{:S(2)}) collective-permute-start(bf16[914,512]{1,0:T(8,128)(2,1)S(1)} %constant_dynamic-update-slice_fusion), channel_id=1, source_target_pairs={{2,0},{3,1},{4,2},{5,3},{6,4},{7,5},{8,6},{9,7},{10,8},{11,9},{12,... | collective-permute-start | bytes 2807816 | tf_op jit(solution)/shard_map/ppermute | solution.py:34
  47.2 2.0 %collective-permute-start.3 = (f32[256,512]{1,0:T(8,128)S(1)}, f32[256,512]{1,0:T(8,128)S(1)}, u32[]{:S(2)}, u32[]{:S(2)}) collective-permute-start(f32[256,512]{1,0:T(8,128)S(1)} %get-tuple-element.31), channel_id=1, source_target_pairs={{0,32},{1,33},{2,34},{3,35},{4,36},{5,37},{6,38},{7,39},{8,40},{9,... | collective-permute-start | bytes 1572872 | tf_op jit(solution)/shard_map/ppermute | solution.py:34
  47.3 2.6 %collective-permute-start.4 = (f32[256,512]{1,0:T(8,128)S(1)}, f32[256,512]{1,0:T(8,128)S(1)}, u32[]{:S(2)}, u32[]{:S(2)}) collective-permute-start(f32[256,512]{1,0:T(8,128)S(1)} %get-tuple-element.33), channel_id=1, source_target_pairs={{0,32},{1,33},{2,34},{3,35},{4,36},{5,37},{6,38},{7,39},{8,40},{9,... | collective-permute-start | bytes 1572872 | tf_op jit(solution)/shard_map/ppermute | solution.py:34

commit v9 on v7

--- a/solution.py
+++ b/solution.py
@@ -232,23 +232,24 @@
 ):
     odd = odd_ref[0]
     bands = (band0, band1, band2)
-    loads = [
-        pltpu.make_async_copy(v_hbm.at[pl.ds(0, 14), line_index(odd, 6)], v6, sem.at[0]),
-        pltpu.make_async_copy(v_hbm.at[pl.ds(0, 14), line_index(odd, 7)], v7, sem.at[1]),
-        pltpu.make_async_copy(vy_hbm.at[pl.ds(0, 17 * SZ)], v8, sem.at[2]),
-        pltpu.make_async_copy(v_hbm.at[pl.ds(14, 2)], vp.at[pl.ds(0, 2)], sem.at[3]),
-    ]
-    for y in range(SY):
-        loads.append(pltpu.make_async_copy(vx_hbm.at[pl.ds(y * SZ, SZ)], vp.at[2, y], sem.at[5 + y]))
-    place = [line_index(odd, c) for c in range(8)]
-    load_m = pltpu.make_async_copy(m_hbm, acc, sem.at[13])
     early = [
         pltpu.make_async_copy(hbmz, bandz, sem.at[14]),
         pltpu.make_async_copy(vy_hbm.at[pl.ds(17 * SZ, 64)], zl, sem.at[15]),
     ]
-    for n, (a, b) in enumerate(((hbm0, band0), (hbm1, band1), (hbm2, band2), (hbm3, band3))):
-        loads.append(pltpu.make_async_copy(a, b, sem.at[16 + n]))
-    for load in early + loads + [load_m]:
+    loads = [
+        pltpu.make_async_copy(hbm3, band3, sem.at[19]),
+        pltpu.make_async_copy(v_hbm.at[pl.ds(0, 14), line_index(odd, 6)], v6, sem.at[0]),
+        pltpu.make_async_copy(v_hbm.at[pl.ds(0, 14), line_index(odd, 7)], v7, sem.at[1]),
+        pltpu.make_async_copy(vy_hbm.at[pl.ds(0, 17 * SZ)], v8, sem.at[2]),
+    ]
+    late = [pltpu.make_async_copy(v_hbm.at[pl.ds(14, 2)], vp.at[pl.ds(0, 2)], sem.at[3])]
+    for y in range(SY):
+        late.append(pltpu.make_async_copy(vx_hbm.at[pl.ds(y * SZ, SZ)], vp.at[2, y], sem.at[5 + y]))
+    for n, (a, b) in enumerate(((hbm0, band0), (hbm1, band1), (hbm2, band2))):
+        late.append(pltpu.make_async_copy(a, b, sem.at[16 + n]))
+    load_m = pltpu.make_async_copy(m_hbm, acc, sem.at[13])
+    place = [line_index(odd, c) for c in range(8)]
+    for load in early + loads + [load_m] + late:
         load.start()
     for load in early:
         load.wait()
@@ -333,6 +334,8 @@
         make_products(p)
         if p == 7:
             load_m.wait()
+            for load in late:
+                load.wait()
             left = jnp.concatenate([line(q, l) for q in range(8) for l in (7, 8)], axis=0)
             acc[...] += gram(left, u[: 8 * OUTER])
     rows = [line(p, l) for p in range(8, 17) for l in range(0 if p >= 15 else 7, 9)]
@@ -476,7 +479,8 @@
         return jnp.where(odd, lax.rev(x, (dim,)), x)
 
     zf = pick(eigvecs, face, 2)
-    kface = jnp.pad(pick(material[0], face, 2), ((0, 0), (0, 120)))
+    kface = lax.dynamic_slice(material, (0, 0, 0, face), (1, SX, SY, 1)).reshape(SX, SY)
+    kface = jnp.pad(kface, ((0, 0), (0, 120)))
     zm = send(jnp.concatenate([zf.reshape(SX * SY, K), to_parts(kface)], axis=0), to_z)
     bands = [in_hbm(band_matrix(ins, outs)) for ins, outs in NEAR]
     raw = in_hbm(material)

time: 81.4 us -> 81 us (level)
    dynamic_slice x0 -> x1, local copies, waits for them, and re-layouts: none -> 0.92 us  [per_device(): lax.dynamic_slice(material, (0, 0, 0, face), (1, SX, SY, 1)).reshape(SX, SY)]
    slice x1 -> x0, local copies, waits for them, and re-layouts: 0.85 us -> none  [per_device(): kface = jnp.pad(pick(material[0], face, 2), ((0, 0), (0, 120)))]
    dynamic_slice x5 -> x4, local copies, waits for them, and re-layouts: 3.1 us -> 3.02 us  [pick(): return lax.dynamic_index_in_dim(x, index, dim, keepdims=False)]
where the time goes in v9:
time: 81 us; the launch traced here: 80.7 us
  blocking collectives  29.7 us (37%)
  Pallas kernels  29.1 us (36%)
  starting transfers between devices  7.45 us (9%)
  local copies, waits for them, and re-layouts  6.44 us (8%)
  waiting for transfers between devices  5.6 us (7%)
  other arithmetic  1.24 us (2%)
  between operations  1.16 us (1%)
    all_to_all x1, blocking collectives, reduce_to_owner(): lax.all_to_all(blocks, ALL, 0, 0, tiled=True, axis_index_groups=groups)  29.7 us
    pallas_call x3, Pallas kernels, inner_part(): pl.pallas_call(body, out_shape=pltpu.HBM((K, 2 * K), jnp.float32), in_spe...  21.3 us
    pallas_call x1, Pallas kernels, outer_part(): pl.pallas_call(outer_kernel, out_shape=[jax.ShapeDtypeStruct((K // 2, K),...  7.76 us
    ppermute x5, starting transfers between devices, send(): return lax.ppermute(value, ALL, links)  7.45 us
    ppermute x5, waiting for transfers between devices, send(): return lax.ppermute(value, ALL, links)  5.6 us
    dynamic_slice x4, local copies, waits for them, and re-layouts, pick(): return lax.dynamic_index_in_dim(x, index, dim, keepdims=False)  3.02 us
  transfers between devices with their start and end apart: 5, of which 3 were waited for; matrix products, arithmetic and copies ran while one was open for 2% of the time, Pallas kernels for 26%

profile of v9, /device:TPU:0, one launch (start us, length us, event | category | flops | bytes accessed | tf_op | source)
XLA Modules:
  0.0 80.7 jit_solution(115553425140755811)
XLA Ops:
  0.6 0.9 %constant_dynamic-slice_fusion.1 = f32[1,16,8,1]{3,2,1,0:T(8,128)S(1)} fusion(f32[2,16,8,48]{3,2,1,0:T(8,128)} %refs_2_.4, s32[]{:T(128)S(6)} %select_n.56), kind=kLoop, calls=%fused_computation.66 | loop fusion | bytes 1028 | tf_op jit(solution)/shard_map/dynamic_slice | solution.py:482
  1.6 0.2 copy.41
  1.7 1.5 %constant_dynamic-slice_fusion.2 = bf16[16,8,1,512]{3,2,1,0:T(2,128)(2,1)S(1)} fusion(bf16[16,8,48,512]{3,2,1,0:T(8,128)(2,1)} %v_hbm.1, s32[]{:T(128)S(6)} %select_n.56), kind=kLoop, calls=%fused_computation.67 | loop fusion | bytes 262148 | tf_op jit(solution)/shard_map/jit(dynamic_index_in_dim)/dynamic_slice | solution.py:441
  3.3 0.0 copy-start
  3.4 4.1 %collective-permute-start = (bf16[144,512]{1,0:T(8,128)(2,1)S(1)}, bf16[144,512]{1,0:T(8,128)(2,1)S(1)}, u32[]{:S(2)}, u32[]{:S(2)}) collective-permute-start(bf16[144,512]{1,0:T(8,128)(2,1)S(1)} %maximum_maximum_fusion.1), channel_id=1, source_target_pairs={{0,1},{1,0},{2,3},{3,2},{4,5},{5,4},{6,7},{7,6},{8,9},{9,8},{10,11... | collective-permute-start | bytes 442376 | tf_op jit(solution)/shard_map/ppermute | solution.py:34
  7.4 0.0 slice-start
  7.5 5.2 %inner0.1.refs_0_ = f32[512,1024]{1,0:T(8,128)} custom-call(s32[1]{0:T(128)} %bitcast.odd_ref, bf16[16,8,48,512]{3,2,1,0:T(8,128)(2,1)} %v_hbm.1, f32[2,16,8,48]{3,2,1,0:T(8,128)} %refs_2_.4, bf16[288,192]{1,0:T(8,128)(2,1)} %constant.75.clone.refs_2_.refs_3_.hbm0, bf16[288,240]{1,0:T(8,128)(2,1)} %constant.76.clone.refs_3_.refs_4_.hbm1, ...), custom_call_target="tpu_custom_call" | custom-call | flops 1800000000 | bytes 2000000 | tf_op jit(solution)/shard_map/inner0/pallas_call | solution.py:381
  12.7 0.1 copy.47
  12.8 1.2 %constant_dynamic-slice_fusion.3 = bf16[16,1,48,512]{3,2,1,0:T(8,128)(2,1)S(1)} fusion(bf16[16,8,48,512]{3,2,1,0:T(8,128)(2,1)} %v_hbm.1, s32[]{:T(128)S(6)} %select_n.55), kind=kLoop, calls=%fused_computation.68 | loop fusion | bytes 1572868 | tf_op jit(solution)/shard_map/jit(dynamic_index_in_dim)/dynamic_slice | solution.py:441
  14.0 0.0 collective-permute-done
  14.1 0.0 copy-done
  14.1 0.1 fusion.1
  14.2 0.0 slice-done
  14.3 1.3 %collective-permute-start.1 = (bf16[416,512]{1,0:T(8,128)(2,1)S(1)}, bf16[416,512]{1,0:T(8,128)(2,1)S(1)}, u32[]{:S(2)}, u32[]{:S(2)}) collective-permute-start(bf16[416,512]{1,0:T(8,128)(2,1)S(1)} %maximum_maximum_fusion), channel_id=1, source_target_pairs={{32,0},{33,1},{34,2},{35,3},{36,4},{37,5},{38,6},{39,7},{40,8},{41... | collective-permute-start | bytes 1277960 | tf_op jit(solution)/shard_map/ppermute | solution.py:34
  15.6 5.7 %inner1.1.refs_0_ = f32[512,1024]{1,0:T(8,128)} custom-call(s32[1]{0:T(128)} %bitcast.odd_ref, f32[512,1024]{1,0:T(8,128)} %inner0.1.refs_0_, bf16[16,8,48,512]{3,2,1,0:T(8,128)(2,1)} %v_hbm.1, f32[2,16,8,48]{3,2,1,0:T(8,128)} %refs_2_.4, bf16[288,192]{1,0:T(8,128)(2,1)} %constant.75.clone.refs_2_.refs_3_.hbm0, ...), custom_call_target="tpu_custom_call" | custom-call | flops 1800000000 | bytes 2000000 | tf_op jit(solution)/shard_map/inner1/pallas_call | solution.py:381
  21.3 0.0 collective-permute-done.1.vx_hbm
  21.5 0.1 reverse_select_fusion
  21.8 0.5 concatenate.44
  22.2 1.5 %collective-permute-start.2 = (bf16[914,512]{1,0:T(8,128)(2,1)S(1)}, bf16[914,512]{1,0:T(8,128)(2,1)S(1)}, u32[]{:S(2)}, u32[]{:S(2)}) collective-permute-start(bf16[914,512]{1,0:T(8,128)(2,1)S(1)} %concatenate.44), channel_id=1, source_target_pairs={{2,0},{3,1},{4,2},{5,3},{6,4},{7,5},{8,6},{9,7},{10,8},{11,9},{12,... | collective-permute-start | bytes 2807816 | tf_op jit(solution)/shard_map/ppermute | solution.py:34
  23.8 10.5 %inner2.1.m_hbm = f32[512,1024]{1,0:T(8,128)} custom-call(s32[1]{0:T(128)} %bitcast.odd_ref, f32[512,1024]{1,0:T(8,128)} %inner1.1.refs_0_, bf16[16,8,48,512]{3,2,1,0:T(8,128)(2,1)} %v_hbm.1, f32[2,16,8,48]{3,2,1,0:T(8,128)} %refs_2_.4, bf16[288,192]{1,0:T(8,128)(2,1)} %constant.75.clone.refs_2_.refs_3_.hbm0, ...), custom_call_target="tpu_custom_call" | custom-call | flops 5400000000 | bytes 6000000 | tf_op jit(solution)/shard_map/inner2/pallas_call | solution.py:381
  34.3 3.5 %collective-permute-done.2.vy_hbm = bf16[914,512]{1,0:T(8,128)(2,1)S(1)} collective-permute-done((bf16[914,512]{1,0:T(8,128)(2,1)S(1)}, bf16[914,512]{1,0:T(8,128)(2,1)S(1)}, u32[]{:S(2)}, u32[]{:S(2)}) %collective-permute-start.2) | collective-permute-done | bytes 935968 | tf_op jit(solution)/shard_map/ppermute | solution.py:34
  37.8 0.1 fusion
  38.0 0.1 copy.34
  38.2 0.1 copy.37
  38.3 0.1 dynamic-slice_maximum_fusion
  38.4 0.1 copy.33
  38.5 0.1 dynamic-slice_maximum_fusion.1
  38.7 0.1 copy.32
  38.8 0.1 copy.36
  38.9 0.1 copy.35
  39.1 7.8 %outer.1 = (f32[256,512]{1,0:T(8,128)S(1)}, f32[256,512]{1,0:T(8,128)S(1)}, f32[256,512]{1,0:T(8,128)S(1)}, f32[256,512]{1,0:T(8,128)S(1)}) custom-call(s32[1]{0:T(128)} %bitcast.odd_ref, f32[512,1024]{1,0:T(8,128)} %inner2.1.m_hbm, bf16[16,8,48,512]{3,2,1,0:T(8,128)(2,1)} %v_hbm.1, bf16[416,512]{1,0:T(8,128)(2,1)S(1)} %collective-permute-done.1.vx_hbm, ...), custom_call_target="tpu_custom_call" | custom-call | flops 4000000000 | bytes 6000000 | tf_op jit(solution)/shard_map/outer/pallas_call | solution.py:409
  46.8 0.5 collective-permute-start.3
  47.4 0.1 collective-permute-start.4
  47.5 1.4 %collective-permute-done.3 = f32[256,512]{1,0:T(8,128)S(1)} collective-permute-done((f32[256,512]{1,0:T(8,128)S(1)}, f32[256,512]{1,0:T(8,128)S(1)}, u32[]{:S(2)}, u32[]{:S(2)}) %collective-permute-start.3) | collective-permute-done | bytes 524320 | tf_op jit(solution)/shard_map/ppermute | solution.py:34
  48.9 0.1 add.59
  49.0 0.7 collective-permute-done.4
  49.7 0.1 add.60
  49.7 0.1 pad_maximum_fusion
  49.8 0.3 reshape.59
  50.1 29.7 %all_to_all.5 = f32[64,4,1024]{2,1,0:T(4,128)S(1)} all-to-all(f32[64,4,1024]{2,1,0:T(4,128)S(1)} %reshape.59), channel_id=1, replica_groups={{0,1,2,3,4,5,6,7,8,9,10,11,12,13,14,15,16,17,18,19,20,21,22,23,24,25,26..., dimensions={0} | all-to-all | bytes 2097152 | tf_op jit(solution)/shard_map/all_to_all | solution.py:448
  79.9 0.2 reduce_sum.9
  80.1 0.6 fusion.9
  (47 shorter events, 0.6 us)
Async XLA Ops:
  3.3 10.8 %copy-start = (f32[2,16,8,48]{3,2,1,0:T(8,128)S(1)}, f32[2,16,8,48]{3,2,1,0:T(8,128)}, u32[]{:S(2)}) copy-start(f32[2,16,8,48]{3,2,1,0:T(8,128)} %refs_2_.4) | copy-start | bytes 147460
  3.4 10.7 %collective-permute-start = (bf16[144,512]{1,0:T(8,128)(2,1)S(1)}, bf16[144,512]{1,0:T(8,128)(2,1)S(1)}, u32[]{:S(2)}, u32[]{:S(2)}) collective-permute-start(bf16[144,512]{1,0:T(8,128)(2,1)S(1)} %maximum_maximum_fusion.1), channel_id=1, source_target_pairs={{0,1},{1,0},{2,3},{3,2},{4,5},{5,4},{6,7},{7,6},{8,9},{9,8},{10,11... | collective-permute-start | bytes 442376 | tf_op jit(solution)/shard_map/ppermute | solution.py:34
  7.4 6.8 %slice-start = ((bf16[16,8,48,512]{3,2,1,0:T(8,128)(2,1)}), bf16[1,8,48,512]{3,2,1,0:T(8,128)(2,1)S(1)}, s32[]{:S(2)}) async-start(bf16[16,8,48,512]{3,2,1,0:T(8,128)(2,1)} %v_hbm.1), calls=%async_computation.1 | async-start | bytes 786432 | tf_op jit(solution)/shard_map/slice | solution.py:494
  14.3 7.0 %collective-permute-start.1 = (bf16[416,512]{1,0:T(8,128)(2,1)S(1)}, bf16[416,512]{1,0:T(8,128)(2,1)S(1)}, u32[]{:S(2)}, u32[]{:S(2)}) collective-permute-start(bf16[416,512]{1,0:T(8,128)(2,1)S(1)} %maximum_maximum_fusion), channel_id=1, source_target_pairs={{32,0},{33,1},{34,2},{35,3},{36,4},{37,5},{38,6},{39,7},{40,8},{41... | collective-permute-start | bytes 1277960 | tf_op jit(solution)/shard_map/ppermute | solution.py:34
  22.2 15.6 %collective-permute-start.2 = (bf16[914,512]{1,0:T(8,128)(2,1)S(1)}, bf16[914,512]{1,0:T(8,128)(2,1)S(1)}, u32[]{:S(2)}, u32[]{:S(2)}) collective-permute-start(bf16[914,512]{1,0:T(8,128)(2,1)S(1)} %concatenate.44), channel_id=1, source_target_pairs={{2,0},{3,1},{4,2},{5,3},{6,4},{7,5},{8,6},{9,7},{10,8},{11,9},{12,... | collective-permute-start | bytes 2807816 | tf_op jit(solution)/shard_map/ppermute | solution.py:34
  46.8 2.1 %collective-permute-start.3 = (f32[256,512]{1,0:T(8,128)S(1)}, f32[256,512]{1,0:T(8,128)S(1)}, u32[]{:S(2)}, u32[]{:S(2)}) collective-permute-start(f32[256,512]{1,0:T(8,128)S(1)} %get-tuple-element.23), channel_id=1, source_target_pairs={{0,32},{1,33},{2,34},{3,35},{4,36},{5,37},{6,38},{7,39},{8,40},{9,... | collective-permute-start | bytes 1572872 | tf_op jit(solution)/shard_map/ppermute | solution.py:34
  47.4 2.3 %collective-permute-start.4 = (f32[256,512]{1,0:T(8,128)S(1)}, f32[256,512]{1,0:T(8,128)S(1)}, u32[]{:S(2)}, u32[]{:S(2)}) collective-permute-start(f32[256,512]{1,0:T(8,128)S(1)} %get-tuple-element.25), channel_id=1, source_target_pairs={{0,32},{1,33},{2,34},{3,35},{4,36},{5,37},{6,38},{7,39},{8,40},{9,... | collective-permute-start | bytes 1572872 | tf_op jit(solution)/shard_map/ppermute | solution.py:34

commit v10 on v9

--- a/solution.py
+++ b/solution.py
@@ -16,7 +16,7 @@
 BATCH = 3
 FACE = 224
 MAIN = 15 * OUTER + 18 * SZ
-PIECES = ((0, 1), (1, 2), (2, 5))
+PIECES = ((0, 1), (1, 5))
 
 
 def linear(x, y, z):
@@ -482,10 +482,9 @@
     kface = lax.dynamic_slice(material, (0, 0, 0, face), (1, SX, SY, 1)).reshape(SX, SY)
     kface = jnp.pad(kface, ((0, 0), (0, 120)))
     zm = send(jnp.concatenate([zf.reshape(SX * SY, K), to_parts(kface)], axis=0), to_z)
+    zm, odd_flag = lax.optimization_barrier((zm, odd_flag))
     bands = [in_hbm(band_matrix(ins, outs)) for ins, outs in NEAR]
     raw = in_hbm(material)
-    m = inner_part(*PIECES[0], odd_flag, None, vectors, raw, bands)
-    zm, m = lax.optimization_barrier((zm, m))
     zh = zm[: SX * SY].reshape(SX, SY, K)
     kz = from_parts(zm[SX * SY :])[:, :SY]
     lanes = jnp.arange(128)
@@ -493,7 +492,7 @@
     matz = jnp.stack([jnp.where(lanes == 64, kz[..., None], own[0]), own[1]])
     plane = eigvecs[0].reshape(SY * SZ, K)
     vx = send(jnp.concatenate([plane, zf[0], zh[0], to_parts(matz[:, 0].reshape(16, 128))], axis=0), to_x)
-    m = inner_part(*PIECES[1], odd_flag, in_hbm(m), vectors, raw, bands)
+    m = inner_part(*PIECES[0], odd_flag, None, vectors, raw, bands)
     vx, m = lax.optimization_barrier((vx, m))
     at = SY * SZ
     xf, xz = vx[at : at + SY], vx[at + SY : at + 2 * SY]
@@ -508,7 +507,7 @@
     vy = send(jnp.concatenate([lines, xline, frows[:, 0], gap, zrows[:, 0], gap, parts], axis=0), to_y)
     zf = face_rows(frows)
     zh = face_rows(zrows)
-    m = inner_part(*PIECES[2], odd_flag, in_hbm(m), vectors, raw, bands)
+    m = inner_part(*PIECES[1], odd_flag, in_hbm(m), vectors, raw, bands)
     vy, m, zf, zh = lax.optimization_barrier((vy, m, zf, zh))
     my = from_parts(vy[17 * SZ + 64 :]).reshape(2, 17, 1, 128)
     matz = jnp.concatenate([matz, my], axis=2)

time: 81 us -> 81.5 us (level)
  Pallas kernels: 29.1 us -> 25.8 us
  starting transfers between devices: 7.45 us -> 10.6 us
  waiting for transfers between devices: 5.6 us -> 4.52 us
  local copies, waits for them, and re-layouts: 6.44 us -> 7.46 us
  other arithmetic: 1.24 us -> 2.13 us
    pallas_call x3 -> x2, Pallas kernels: 21.3 us -> 18 us  [inner_part(): pl.pallas_call(body, out_shape=pltpu.HBM((K, 2 * K), jnp.float32), in_spe...]
    ppermute x5, starting transfers between devices: 7.45 us -> 10.6 us  [send(): return lax.ppermute(value, ALL, links)]
    ppermute x5, waiting for transfers between devices: 5.6 us -> 4.52 us  [send(): return lax.ppermute(value, ALL, links)]
    slice x2 -> x1, local copies, waits for them, and re-layouts: 0.01 us -> 1.02 us  [per_device(): plane = eigvecs[0].reshape(SY * SZ, K)]
    select_n x1, other arithmetic: 0.09 us -> 0.96 us  [per_device(): matz = jnp.stack([jnp.where(lanes == 64, kz[..., None], own[0]), own[1]])]
  transfers between devices with their start and end apart: 5 -> 5, of which waited for: 3 -> 4; matrix products, arithmetic and copies ran while one was open for 2% -> 3% of each run, Pallas kernels for 26% -> 22%
where the time goes in v10:
time: 81.5 us; the launch traced here: 81.1 us
  blocking collectives  29.5 us (36%)
  Pallas kernels  25.8 us (32%)
  starting transfers between devices  10.6 us (13%)
  local copies, waits for them, and re-layouts  7.46 us (9%)
  waiting for transfers between devices  4.52 us (6%)
  other arithmetic  2.13 us (3%)
  between operations  1.11 us (1%)
    all_to_all x1, blocking collectives, reduce_to_owner(): lax.all_to_all(blocks, ALL, 0, 0, tiled=True, axis_index_groups=groups)  29.5 us
    pallas_call x2, Pallas kernels, inner_part(): pl.pallas_call(body, out_shape=pltpu.HBM((K, 2 * K), jnp.float32), in_spe...  18 us
    ppermute x5, starting transfers between devices, send(): return lax.ppermute(value, ALL, links)  10.6 us
    pallas_call x1, Pallas kernels, outer_part(): pl.pallas_call(outer_kernel, out_shape=[jax.ShapeDtypeStruct((K // 2, K),...  7.76 us
    ppermute x5, waiting for transfers between devices, send(): return lax.ppermute(value, ALL, links)  4.52 us
    dynamic_slice x4, local copies, waits for them, and re-layouts, pick(): return lax.dynamic_index_in_dim(x, index, dim, keepdims=False)  3.02 us
  transfers between devices with their start and end apart: 5, of which 4 were waited for; matrix products, arithmetic and copies ran while one was open for 3% of the time, Pallas kernels for 22%

profile of v10, /device:TPU:0, one launch (start us, length us, event | category | flops | bytes accessed | tf_op | source)
XLA Modules:
  0.0 81.1 jit_solution(4608342278344665770)
XLA Ops:
  0.6 0.9 %constant_dynamic-slice_fusion.2 = f32[1,16,8,1]{3,2,1,0:T(8,128)S(1)} fusion(f32[2,16,8,48]{3,2,1,0:T(8,128)} %refs_2_.2, s32[]{:T(128)S(6)} %select_n.54), kind=kLoop, calls=%fused_computation.67 | loop fusion | bytes 1028 | tf_op jit(solution)/shard_map/dynamic_slice | solution.py:482
  1.6 0.2 copy.41
  1.7 1.5 %constant_dynamic-slice_fusion.3 = bf16[16,8,1,512]{3,2,1,0:T(2,128)(2,1)S(1)} fusion(bf16[16,8,48,512]{3,2,1,0:T(8,128)(2,1)} %v_hbm.1, s32[]{:T(128)S(6)} %select_n.54), kind=kLoop, calls=%fused_computation.68 | loop fusion | bytes 262148 | tf_op jit(solution)/shard_map/jit(dynamic_index_in_dim)/dynamic_slice | solution.py:441
  3.3 4.1 %collective-permute-start = (bf16[144,512]{1,0:T(8,128)(2,1)S(1)}, bf16[144,512]{1,0:T(8,128)(2,1)S(1)}, u32[]{:S(2)}, u32[]{:S(2)}) collective-permute-start(bf16[144,512]{1,0:T(8,128)(2,1)S(1)} %maximum_maximum_fusion.1), channel_id=1, source_target_pairs={{0,1},{1,0},{2,3},{3,2},{4,5},{5,4},{6,7},{7,6},{8,9},{9,8},{10,11... | collective-permute-start | bytes 442376 | tf_op jit(solution)/shard_map/ppermute | solution.py:34
  7.5 0.1 copy.47
  7.6 1.0 %slice.93 = bf16[1,8,48,512]{3,2,1,0:T(8,128)(2,1)S(1)} slice(bf16[16,8,48,512]{3,2,1,0:T(8,128)(2,1)} %v_hbm.1), slice={[0:1], [0:8], [0:48], [0:512]} | slice | bytes 786432 | tf_op jit(solution)/shard_map/slice | solution.py:493
  8.7 1.2 %constant_dynamic-slice_fusion.1 = bf16[16,1,48,512]{3,2,1,0:T(8,128)(2,1)S(1)} fusion(bf16[16,8,48,512]{3,2,1,0:T(8,128)(2,1)} %v_hbm.1, s32[]{:T(128)S(6)} %select_n.56), kind=kLoop, calls=%fused_computation.66 | loop fusion | bytes 1572868 | tf_op jit(solution)/shard_map/jit(dynamic_index_in_dim)/dynamic_slice | solution.py:441
  9.9 1.4 %collective-permute-done = bf16[144,512]{1,0:T(8,128)(2,1)S(1)} collective-permute-done((bf16[144,512]{1,0:T(8,128)(2,1)S(1)}, bf16[144,512]{1,0:T(8,128)(2,1)S(1)}, u32[]{:S(2)}, u32[]{:S(2)}) %collective-permute-start) | collective-permute-done | bytes 147488 | tf_op jit(solution)/shard_map/ppermute | solution.py:34
  11.3 1.0 %fusion.1 = (f32[1,16,8,128]{3,2,1,0:T(8,128)S(1)}, f32[1,16,8,128]{3,2,1,0:T(8,128)S(1)}) fusion(f32[2,16,8,48]{3,2,1,0:T(8,128)} %refs_2_.2, f32[16,8]{1,0:T(8,128)S(1)} %slice_add_fusion.4, pred[128]{0:T(512)(128)(4,1)S(1)} %iota_compare_fusion.3), kind=kLoop, calls=%fused_computation.24 | loop fusion | flops 16384 | bytes 180864 | tf_op jit(solution)/shard_map/jit(_where)/select_n | solution.py:492
  12.3 1.3 %collective-permute-start.1 = (bf16[416,512]{1,0:T(8,128)(2,1)S(1)}, bf16[416,512]{1,0:T(8,128)(2,1)S(1)}, u32[]{:S(2)}, u32[]{:S(2)}) collective-permute-start(bf16[416,512]{1,0:T(8,128)(2,1)S(1)} %maximum_maximum_fusion), channel_id=1, source_target_pairs={{32,0},{33,1},{34,2},{35,3},{36,4},{37,5},{38,6},{39,7},{40,8},{41... | collective-permute-start | bytes 1277960 | tf_op jit(solution)/shard_map/ppermute | solution.py:34
  13.6 5.1 %inner0.1.refs_0_ = f32[512,1024]{1,0:T(8,128)} custom-call(s32[1]{0:T(128)} %bitcast.2.odd_ref, bf16[16,8,48,512]{3,2,1,0:T(8,128)(2,1)} %v_hbm.1, f32[2,16,8,48]{3,2,1,0:T(8,128)} %refs_2_.2, bf16[288,192]{1,0:T(8,128)(2,1)} %constant.75.clone.refs_2_.refs_3_.hbm0, bf16[288,240]{1,0:T(8,128)(2,1)} %constant.76.clone.refs_3_.refs_4_.hbm1, ...), custom_call_target="tpu_custom_call" | custom-call | flops 1800000000 | bytes 2000000 | tf_op jit(solution)/shard_map/inner0/pallas_call | solution.py:381
  18.8 0.0 collective-permute-done.1.vx_hbm
  19.3 0.5 concatenate.44
  19.8 1.5 %collective-permute-start.2 = (bf16[914,512]{1,0:T(8,128)(2,1)S(1)}, bf16[914,512]{1,0:T(8,128)(2,1)S(1)}, u32[]{:S(2)}, u32[]{:S(2)}) collective-permute-start(bf16[914,512]{1,0:T(8,128)(2,1)S(1)} %concatenate.44), channel_id=1, source_target_pairs={{2,0},{3,1},{4,2},{5,3},{6,4},{7,5},{8,6},{9,7},{10,8},{11,9},{12,... | collective-permute-start | bytes 2807816 | tf_op jit(solution)/shard_map/ppermute | solution.py:34
  21.4 12.9 %inner1.1.m_hbm = f32[512,1024]{1,0:T(8,128)} custom-call(s32[1]{0:T(128)} %bitcast.2.odd_ref, f32[512,1024]{1,0:T(8,128)} %inner0.1.refs_0_, bf16[16,8,48,512]{3,2,1,0:T(8,128)(2,1)} %v_hbm.1, f32[2,16,8,48]{3,2,1,0:T(8,128)} %refs_2_.2, bf16[288,192]{1,0:T(8,128)(2,1)} %constant.75.clone.refs_2_.refs_3_.hbm0, ...), custom_call_target="tpu_custom_call" | custom-call | flops 7200000000 | bytes 8000000 | tf_op jit(solution)/shard_map/inner1/pallas_call | solution.py:381
  34.3 1.0 %collective-permute-done.2.vy_hbm = bf16[914,512]{1,0:T(8,128)(2,1)S(1)} collective-permute-done((bf16[914,512]{1,0:T(8,128)(2,1)S(1)}, bf16[914,512]{1,0:T(8,128)(2,1)S(1)}, u32[]{:S(2)}, u32[]{:S(2)}) %collective-permute-start.2) | collective-permute-done | bytes 935968 | tf_op jit(solution)/shard_map/ppermute | solution.py:34
  35.4 0.1 fusion
  35.6 0.1 copy.34
  35.7 0.1 copy.37
  35.8 0.2 dynamic-slice_maximum_fusion
  36.0 0.1 copy.33
  36.2 0.1 copy.32
  36.3 0.1 copy.35
  36.4 0.1 copy.36
  36.6 7.8 %outer.1 = (f32[256,512]{1,0:T(8,128)S(1)}, f32[256,512]{1,0:T(8,128)S(1)}, f32[256,512]{1,0:T(8,128)S(1)}, f32[256,512]{1,0:T(8,128)S(1)}) custom-call(s32[1]{0:T(128)} %bitcast.2.odd_ref, f32[512,1024]{1,0:T(8,128)} %inner1.1.m_hbm, bf16[16,8,48,512]{3,2,1,0:T(8,128)(2,1)} %v_hbm.1, bf16[416,512]{1,0:T(8,128)(2,1)S(1)} %collective-permute-done.1.vx_hbm, ...), custom_call_target="tpu_custom_call" | custom-call | flops 4000000000 | bytes 6000000 | tf_op jit(solution)/shard_map/outer/pallas_call | solution.py:409
  44.3 3.6 %collective-permute-start.3 = (f32[256,512]{1,0:T(8,128)S(1)}, f32[256,512]{1,0:T(8,128)S(1)}, u32[]{:S(2)}, u32[]{:S(2)}) collective-permute-start(f32[256,512]{1,0:T(8,128)S(1)} %get-tuple-element.23), channel_id=1, source_target_pairs={{0,32},{1,33},{2,34},{3,35},{4,36},{5,37},{6,38},{7,39},{8,40},{9,... | collective-permute-start | bytes 1572872 | tf_op jit(solution)/shard_map/ppermute | solution.py:34
  48.0 0.1 collective-permute-start.4
  48.1 1.4 %collective-permute-done.3 = f32[256,512]{1,0:T(8,128)S(1)} collective-permute-done((f32[256,512]{1,0:T(8,128)S(1)}, f32[256,512]{1,0:T(8,128)S(1)}, u32[]{:S(2)}, u32[]{:S(2)}) %collective-permute-start.3) | collective-permute-done | bytes 524320 | tf_op jit(solution)/shard_map/ppermute | solution.py:34
  49.5 0.1 add.59
  49.6 0.7 collective-permute-done.4
  50.3 0.1 add.60
  50.4 0.1 pad_maximum_fusion
  50.4 0.3 reshape.60
  50.8 29.5 %all_to_all.5 = f32[64,4,1024]{2,1,0:T(4,128)S(1)} all-to-all(f32[64,4,1024]{2,1,0:T(4,128)S(1)} %reshape.60), channel_id=1, replica_groups={{0,1,2,3,4,5,6,7,8,9,10,11,12,13,14,15,16,17,18,19,20,21,22,23,24,25,26..., dimensions={0} | all-to-all | bytes 2097152 | tf_op jit(solution)/shard_map/all_to_all | solution.py:448
  80.3 0.2 reduce_sum.9
  80.5 0.6 fusion.9
  (51 shorter events, 0.8 us)
Async XLA Ops:
  3.3 7.9 %collective-permute-start = (bf16[144,512]{1,0:T(8,128)(2,1)S(1)}, bf16[144,512]{1,0:T(8,128)(2,1)S(1)}, u32[]{:S(2)}, u32[]{:S(2)}) collective-permute-start(bf16[144,512]{1,0:T(8,128)(2,1)S(1)} %maximum_maximum_fusion.1), channel_id=1, source_target_pairs={{0,1},{1,0},{2,3},{3,2},{4,5},{5,4},{6,7},{7,6},{8,9},{9,8},{10,11... | collective-permute-start | bytes 442376 | tf_op jit(solution)/shard_map/ppermute | solution.py:34
  12.3 6.5 %collective-permute-start.1 = (bf16[416,512]{1,0:T(8,128)(2,1)S(1)}, bf16[416,512]{1,0:T(8,128)(2,1)S(1)}, u32[]{:S(2)}, u32[]{:S(2)}) collective-permute-start(bf16[416,512]{1,0:T(8,128)(2,1)S(1)} %maximum_maximum_fusion), channel_id=1, source_target_pairs={{32,0},{33,1},{34,2},{35,3},{36,4},{37,5},{38,6},{39,7},{40,8},{41... | collective-permute-start | bytes 1277960 | tf_op jit(solution)/shard_map/ppermute | solution.py:34
  19.8 15.6 %collective-permute-start.2 = (bf16[914,512]{1,0:T(8,128)(2,1)S(1)}, bf16[914,512]{1,0:T(8,128)(2,1)S(1)}, u32[]{:S(2)}, u32[]{:S(2)}) collective-permute-start(bf16[914,512]{1,0:T(8,128)(2,1)S(1)} %concatenate.44), channel_id=1, source_target_pairs={{2,0},{3,1},{4,2},{5,3},{6,4},{7,5},{8,6},{9,7},{10,8},{11,9},{12,... | collective-permute-start | bytes 2807816 | tf_op jit(solution)/shard_map/ppermute | solution.py:34
  44.3 5.2 %collective-permute-start.3 = (f32[256,512]{1,0:T(8,128)S(1)}, f32[256,512]{1,0:T(8,128)S(1)}, u32[]{:S(2)}, u32[]{:S(2)}) collective-permute-start(f32[256,512]{1,0:T(8,128)S(1)} %get-tuple-element.23), channel_id=1, source_target_pairs={{0,32},{1,33},{2,34},{3,35},{4,36},{5,37},{6,38},{7,39},{8,40},{9,... | collective-permute-start | bytes 1572872 | tf_op jit(solution)/shard_map/ppermute | solution.py:34
  48.0 2.3 %collective-permute-start.4 = (f32[256,512]{1,0:T(8,128)S(1)}, f32[256,512]{1,0:T(8,128)S(1)}, u32[]{:S(2)}, u32[]{:S(2)}) collective-permute-start(f32[256,512]{1,0:T(8,128)S(1)} %get-tuple-element.25), channel_id=1, source_target_pairs={{0,32},{1,33},{2,34},{3,35},{4,36},{5,37},{6,38},{7,39},{8,40},{9,... | collective-permute-start | bytes 1572872 | tf_op jit(solution)/shard_map/ppermute | solution.py:34

commit v11 on v10

--- a/solution.py
+++ b/solution.py
@@ -488,14 +488,16 @@
     zh = zm[: SX * SY].reshape(SX, SY, K)
     kz = from_parts(zm[SX * SY :])[:, :SY]
     lanes = jnp.arange(128)
-    own = jnp.pad(material, ((0, 0), (0, 0), (0, 0), (0, 128 - SZ)))
-    matz = jnp.stack([jnp.where(lanes == 64, kz[..., None], own[0]), own[1]])
+    first = jnp.pad(material[:, 0], ((0, 0), (0, 0), (0, 128 - SZ)))
+    first = jnp.stack([jnp.where(lanes == 64, kz[0][:, None], first[0]), first[1]])
     plane = eigvecs[0].reshape(SY * SZ, K)
-    vx = send(jnp.concatenate([plane, zf[0], zh[0], to_parts(matz[:, 0].reshape(16, 128))], axis=0), to_x)
+    vx = send(jnp.concatenate([plane, zf[0], zh[0], to_parts(first.reshape(16, 128))], axis=0), to_x)
     m = inner_part(*PIECES[0], odd_flag, None, vectors, raw, bands)
     vx, m = lax.optimization_barrier((vx, m))
     at = SY * SZ
     xf, xz = vx[at : at + SY], vx[at + SY : at + 2 * SY]
+    own = jnp.pad(material, ((0, 0), (0, 0), (0, 0), (0, 128 - SZ)))
+    matz = jnp.stack([jnp.where(lanes == 64, kz[..., None], own[0]), own[1]])
     xmat = from_parts(vx[at + 2 * SY :]).reshape(2, 1, SY, 128)
     matz = chain(jnp.concatenate([matz, xmat], axis=1), 2)
     frows = chain(jnp.concatenate([zf, xf[None]], axis=0), 1)

time: 81.5 us -> 80.9 us (level)
  starting transfers between devices: 10.6 us -> 9.58 us
    ppermute x5, starting transfers between devices: 10.6 us -> 9.58 us  [send(): return lax.ppermute(value, ALL, links)]
  transfers between devices with their start and end apart: 5 -> 5, of which waited for: 4 -> 4; matrix products, arithmetic and copies ran while one was open for 3% -> 5% of each run, Pallas kernels for 22% -> 22%
where the time goes in v11:
time: 80.9 us; the launch traced here: 80.5 us
  blocking collectives  29.8 us (37%)
  Pallas kernels  25.7 us (32%)
  starting transfers between devices  9.58 us (12%)
  local copies, waits for them, and re-layouts  8.15 us (10%)
  waiting for transfers between devices  3.87 us (5%)
  other arithmetic  2.2 us (3%)
  between operations  1.1 us (1%)
    all_to_all x1, blocking collectives, reduce_to_owner(): lax.all_to_all(blocks, ALL, 0, 0, tiled=True, axis_index_groups=groups)  29.8 us
    pallas_call x2, Pallas kernels, inner_part(): pl.pallas_call(body, out_shape=pltpu.HBM((K, 2 * K), jnp.float32), in_spe...  18 us
    ppermute x5, starting transfers between devices, send(): return lax.ppermute(value, ALL, links)  9.58 us
    pallas_call x1, Pallas kernels, outer_part(): pl.pallas_call(outer_kernel, out_shape=[jax.ShapeDtypeStruct((K // 2, K),...  7.77 us
    ppermute x5, waiting for transfers between devices, send(): return lax.ppermute(value, ALL, links)  3.87 us
    dynamic_slice x4, local copies, waits for them, and re-layouts, pick(): return lax.dynamic_index_in_dim(x, index, dim, keepdims=False)  3.02 us
  transfers between devices with their start and end apart: 5, of which 4 were waited for; matrix products, arithmetic and copies ran while one was open for 5% of the time, Pallas kernels for 22%

profile of v11, /device:TPU:0, one launch (start us, length us, event | category | flops | bytes accessed | tf_op | source)
XLA Modules:
  0.0 80.5 jit_solution(10920086516718809326)
XLA Ops:
  0.6 0.9 %constant_dynamic-slice_fusion.2 = f32[1,16,8,1]{3,2,1,0:T(8,128)S(1)} fusion(f32[2,16,8,48]{3,2,1,0:T(8,128)} %refs_2_.2, s32[]{:T(128)S(6)} %select_n.59), kind=kLoop, calls=%fused_computation.70 | loop fusion | bytes 1028 | tf_op jit(solution)/shard_map/dynamic_slice | solution.py:482
  1.6 0.2 copy.41
  1.7 1.5 %constant_dynamic-slice_fusion.3 = bf16[16,8,1,512]{3,2,1,0:T(2,128)(2,1)S(1)} fusion(bf16[16,8,48,512]{3,2,1,0:T(8,128)(2,1)} %v_hbm.1, s32[]{:T(128)S(6)} %select_n.59), kind=kLoop, calls=%fused_computation.71 | loop fusion | bytes 262148 | tf_op jit(solution)/shard_map/jit(dynamic_index_in_dim)/dynamic_slice | solution.py:441
  3.3 4.1 %collective-permute-start = (bf16[144,512]{1,0:T(8,128)(2,1)S(1)}, bf16[144,512]{1,0:T(8,128)(2,1)S(1)}, u32[]{:S(2)}, u32[]{:S(2)}) collective-permute-start(bf16[144,512]{1,0:T(8,128)(2,1)S(1)} %maximum_maximum_fusion.1), channel_id=1, source_target_pairs={{0,1},{1,0},{2,3},{3,2},{4,5},{5,4},{6,7},{7,6},{8,9},{9,8},{10,11... | collective-permute-start | bytes 442376 | tf_op jit(solution)/shard_map/ppermute | solution.py:34
  7.4 0.7 slice_bitcast_fusion.6
  8.2 0.1 copy.47
  8.3 1.0 %slice.105 = bf16[1,8,48,512]{3,2,1,0:T(8,128)(2,1)S(1)} slice(bf16[16,8,48,512]{3,2,1,0:T(8,128)(2,1)} %v_hbm.1), slice={[0:1], [0:8], [0:48], [0:512]} | slice | bytes 786432 | tf_op jit(solution)/shard_map/slice | solution.py:493
  9.4 1.2 %constant_dynamic-slice_fusion.1 = bf16[16,1,48,512]{3,2,1,0:T(8,128)(2,1)S(1)} fusion(bf16[16,8,48,512]{3,2,1,0:T(8,128)(2,1)} %v_hbm.1, s32[]{:T(128)S(6)} %select_n.61), kind=kLoop, calls=%fused_computation.69 | loop fusion | bytes 1572868 | tf_op jit(solution)/shard_map/jit(dynamic_index_in_dim)/dynamic_slice | solution.py:441
  10.6 0.7 collective-permute-done
  11.3 0.1 fusion.6
  11.4 1.3 %collective-permute-start.1 = (bf16[416,512]{1,0:T(8,128)(2,1)S(1)}, bf16[416,512]{1,0:T(8,128)(2,1)S(1)}, u32[]{:S(2)}, u32[]{:S(2)}) collective-permute-start(bf16[416,512]{1,0:T(8,128)(2,1)S(1)} %maximum_maximum_fusion), channel_id=1, source_target_pairs={{32,0},{33,1},{34,2},{35,3},{36,4},{37,5},{38,6},{39,7},{40,8},{41... | collective-permute-start | bytes 1277960 | tf_op jit(solution)/shard_map/ppermute | solution.py:34
  12.7 1.0 %fusion.1 = (f32[1,16,8,128]{3,2,1,0:T(8,128)S(1)}, f32[1,16,8,128]{3,2,1,0:T(8,128)S(1)}) fusion(f32[2,16,8,48]{3,2,1,0:T(8,128)} %refs_2_.2, f32[16,8]{1,0:T(8,128)S(1)} %bitcast.55, pred[128]{0:T(512)(128)(4,1)S(1)} %iota_compare_fusion.3), kind=kLoop, calls=%fused_computation.24 | loop fusion | flops 16384 | bytes 180864 | tf_op jit(solution)/shard_map/jit(_where)/select_n | solution.py:500
  13.7 5.1 %inner0.1.refs_0_ = f32[512,1024]{1,0:T(8,128)} custom-call(s32[1]{0:T(128)} %bitcast.2.odd_ref, bf16[16,8,48,512]{3,2,1,0:T(8,128)(2,1)} %v_hbm.1, f32[2,16,8,48]{3,2,1,0:T(8,128)} %refs_2_.2, bf16[288,192]{1,0:T(8,128)(2,1)} %constant.75.clone.refs_2_.refs_3_.hbm0, bf16[288,240]{1,0:T(8,128)(2,1)} %constant.76.clone.refs_3_.refs_4_.hbm1, ...), custom_call_target="tpu_custom_call" | custom-call | flops 1800000000 | bytes 2000000 | tf_op jit(solution)/shard_map/inner0/pallas_call | solution.py:381
  18.9 0.0 collective-permute-done.1.vx_hbm
  19.4 0.5 concatenate.44
  19.9 1.5 %collective-permute-start.2 = (bf16[914,512]{1,0:T(8,128)(2,1)S(1)}, bf16[914,512]{1,0:T(8,128)(2,1)S(1)}, u32[]{:S(2)}, u32[]{:S(2)}) collective-permute-start(bf16[914,512]{1,0:T(8,128)(2,1)S(1)} %concatenate.44), channel_id=1, source_target_pairs={{2,0},{3,1},{4,2},{5,3},{6,4},{7,5},{8,6},{9,7},{10,8},{11,9},{12,... | collective-permute-start | bytes 2807816 | tf_op jit(solution)/shard_map/ppermute | solution.py:34
  21.5 12.9 %inner1.1.m_hbm = f32[512,1024]{1,0:T(8,128)} custom-call(s32[1]{0:T(128)} %bitcast.2.odd_ref, f32[512,1024]{1,0:T(8,128)} %inner0.1.refs_0_, bf16[16,8,48,512]{3,2,1,0:T(8,128)(2,1)} %v_hbm.1, f32[2,16,8,48]{3,2,1,0:T(8,128)} %refs_2_.2, bf16[288,192]{1,0:T(8,128)(2,1)} %constant.75.clone.refs_2_.refs_3_.hbm0, ...), custom_call_target="tpu_custom_call" | custom-call | flops 7200000000 | bytes 8000000 | tf_op jit(solution)/shard_map/inner1/pallas_call | solution.py:381
  34.3 1.1 %collective-permute-done.2.vy_hbm = bf16[914,512]{1,0:T(8,128)(2,1)S(1)} collective-permute-done((bf16[914,512]{1,0:T(8,128)(2,1)S(1)}, bf16[914,512]{1,0:T(8,128)(2,1)S(1)}, u32[]{:S(2)}, u32[]{:S(2)}) %collective-permute-start.2) | collective-permute-done | bytes 935968 | tf_op jit(solution)/shard_map/ppermute | solution.py:34
  35.5 0.1 fusion
  35.6 0.1 copy.34
  35.8 0.1 copy.37
  35.9 0.2 dynamic-slice_maximum_fusion
  36.1 0.1 copy.33
  36.2 0.1 copy.32
  36.4 0.1 copy.35
  36.5 0.1 copy.36
  36.6 7.8 %outer.1 = (f32[256,512]{1,0:T(8,128)S(1)}, f32[256,512]{1,0:T(8,128)S(1)}, f32[256,512]{1,0:T(8,128)S(1)}, f32[256,512]{1,0:T(8,128)S(1)}) custom-call(s32[1]{0:T(128)} %bitcast.2.odd_ref, f32[512,1024]{1,0:T(8,128)} %inner1.1.m_hbm, bf16[16,8,48,512]{3,2,1,0:T(8,128)(2,1)} %v_hbm.1, bf16[416,512]{1,0:T(8,128)(2,1)S(1)} %collective-permute-done.1.vx_hbm, ...), custom_call_target="tpu_custom_call" | custom-call | flops 4000000000 | bytes 6000000 | tf_op jit(solution)/shard_map/outer/pallas_call | solution.py:409
  44.4 2.7 %collective-permute-start.3 = (f32[256,512]{1,0:T(8,128)S(1)}, f32[256,512]{1,0:T(8,128)S(1)}, u32[]{:S(2)}, u32[]{:S(2)}) collective-permute-start(f32[256,512]{1,0:T(8,128)S(1)} %get-tuple-element.23), channel_id=1, source_target_pairs={{0,32},{1,33},{2,34},{3,35},{4,36},{5,37},{6,38},{7,39},{8,40},{9,... | collective-permute-start | bytes 1572872 | tf_op jit(solution)/shard_map/ppermute | solution.py:34
  47.0 0.1 collective-permute-start.4
  47.1 1.4 %collective-permute-done.3 = f32[256,512]{1,0:T(8,128)S(1)} collective-permute-done((f32[256,512]{1,0:T(8,128)S(1)}, f32[256,512]{1,0:T(8,128)S(1)}, u32[]{:S(2)}, u32[]{:S(2)}) %collective-permute-start.3) | collective-permute-done | bytes 524320 | tf_op jit(solution)/shard_map/ppermute | solution.py:34
  48.6 0.1 add.61
  48.7 0.7 collective-permute-done.4
  49.3 0.1 add.62
  49.4 0.1 pad_maximum_fusion
  49.5 0.3 reshape.76
  49.8 29.8 %all_to_all.5 = f32[64,4,1024]{2,1,0:T(4,128)S(1)} all-to-all(f32[64,4,1024]{2,1,0:T(4,128)S(1)} %reshape.76), channel_id=1, replica_groups={{0,1,2,3,4,5,6,7,8,9,10,11,12,13,14,15,16,17,18,19,20,21,22,23,24,25,26..., dimensions={0} | all-to-all | bytes 2097152 | tf_op jit(solution)/shard_map/all_to_all | solution.py:448
  79.6 0.2 reduce_sum.9
  79.9 0.6 fusion.7
  (50 shorter events, 0.8 us)
Async XLA Ops:
  3.3 7.9 %collective-permute-start = (bf16[144,512]{1,0:T(8,128)(2,1)S(1)}, bf16[144,512]{1,0:T(8,128)(2,1)S(1)}, u32[]{:S(2)}, u32[]{:S(2)}) collective-permute-start(bf16[144,512]{1,0:T(8,128)(2,1)S(1)} %maximum_maximum_fusion.1), channel_id=1, source_target_pairs={{0,1},{1,0},{2,3},{3,2},{4,5},{5,4},{6,7},{7,6},{8,9},{9,8},{10,11... | collective-permute-start | bytes 442376 | tf_op jit(solution)/shard_map/ppermute | solution.py:34
  11.4 7.4 %collective-permute-start.1 = (bf16[416,512]{1,0:T(8,128)(2,1)S(1)}, bf16[416,512]{1,0:T(8,128)(2,1)S(1)}, u32[]{:S(2)}, u32[]{:S(2)}) collective-permute-start(bf16[416,512]{1,0:T(8,128)(2,1)S(1)} %maximum_maximum_fusion), channel_id=1, source_target_pairs={{32,0},{33,1},{34,2},{35,3},{36,4},{37,5},{38,6},{39,7},{40,8},{41... | collective-permute-start | bytes 1277960 | tf_op jit(solution)/shard_map/ppermute | solution.py:34
  19.9 15.6 %collective-permute-start.2 = (bf16[914,512]{1,0:T(8,128)(2,1)S(1)}, bf16[914,512]{1,0:T(8,128)(2,1)S(1)}, u32[]{:S(2)}, u32[]{:S(2)}) collective-permute-start(bf16[914,512]{1,0:T(8,128)(2,1)S(1)} %concatenate.44), channel_id=1, source_target_pairs={{2,0},{3,1},{4,2},{5,3},{6,4},{7,5},{8,6},{9,7},{10,8},{11,9},{12,... | collective-permute-start | bytes 2807816 | tf_op jit(solution)/shard_map/ppermute | solution.py:34
  44.4 4.2 %collective-permute-start.3 = (f32[256,512]{1,0:T(8,128)S(1)}, f32[256,512]{1,0:T(8,128)S(1)}, u32[]{:S(2)}, u32[]{:S(2)}) collective-permute-start(f32[256,512]{1,0:T(8,128)S(1)} %get-tuple-element.23), channel_id=1, source_target_pairs={{0,32},{1,33},{2,34},{3,35},{4,36},{5,37},{6,38},{7,39},{8,40},{9,... | collective-permute-start | bytes 1572872 | tf_op jit(solution)/shard_map/ppermute | solution.py:34
  47.0 2.3 %collective-permute-start.4 = (f32[256,512]{1,0:T(8,128)S(1)}, f32[256,512]{1,0:T(8,128)S(1)}, u32[]{:S(2)}, u32[]{:S(2)}) collective-permute-start(f32[256,512]{1,0:T(8,128)S(1)} %get-tuple-element.25), channel_id=1, source_target_pairs={{0,32},{1,33},{2,34},{3,35},{4,36},{5,37},{6,38},{7,39},{8,40},{9,... | collective-permute-start | bytes 1572872 | tf_op jit(solution)/shard_map/ppermute | solution.py:34
